TPU v7x, 32 devices: a whole 2x2x4 slice. The times are simulated.
32 devices in a mesh: tm: 32 (over z, y, x, core), panel: 1.
Axes of the slice: x: 2, y: 2, z: 4, core: 2. Of those that a mesh axis runs over, the one named last changes fastest.
Arguments:
- observations: float32 [1024, 64], P('tm'), may hold values from -600 to 600
- obs_weights: float32 [1024, 64], P('tm'), may hold values from 0 to 1
- damping: float32 [1024, 256], P('tm'), may hold values from 0.1 to 1
- transition: float32 [256, 256], replicated, may hold values from -1 to 1
- obs_matrix: float32 [64, 256], replicated, may hold values from -0.25 to 0.25
- smoother_gain: float32 [256, 256], replicated, may hold values from -1 to 1
- prior_mean: float32 [256], replicated, may hold values from -6 to 6
Outputs:
- filtered: float32 [1024, 256], P('tm')
- smoothed: float32 [1024, 256], P('tm')
All inputs are finite; a program needn't handle non-finite values.
Results may differ from a plain program's by a relative error of at most 0.0003.
Values sent between devices are 32-bit elements; how exact they have to be, the bound alone decides.
No kernel may reach another device: no remote copies, remote signals or barrier semaphores. Data moves between devices by JAX's collectives and lax.ppermute only.
A program may use at most 64 MiB of HBM per device.

v0:
```python
import jax
import jax.numpy as jnp
from jax import lax
from jax.sharding import PartitionSpec as P

highest = lax.Precision.HIGHEST


def prefix(value, axis, join, neutral, backward):
    count, mine = (lax.axis_size(axis), lax.axis_index(axis))
    pieces = jax.tree.map(lambda part: lax.all_gather(part, axis), value)
    if backward:
        pieces = jax.tree.map(lambda part: part[::-1], pieces)
        mine = count - 1 - mine
    subtotal = jax.tree.map(
        lambda part, zero: jnp.full_like(part, 0) + jnp.asarray(zero, part.dtype), value, neutral
    )

    def lap(position, subtotal):
        longer = join(subtotal, jax.tree.map(lambda part: part[position], pieces))
        return jax.tree.map(lambda new, old: jnp.where(position < mine, new, old), longer, subtotal)

    return lax.fori_loop(0, count - 1, lap, subtotal)


def product(left, right):
    return jnp.dot(left, right, precision=highest, preferred_element_type=jnp.float32)


def filter_update(estimate, obs_row, weight_row, damp_row, inject_row, transition, obs_matrix):
    predicted = product(transition, damp_row * estimate) + inject_row
    innovation = obs_row - product(obs_matrix, predicted)
    return predicted + product(weight_row * innovation, obs_matrix)


def per_device(
    observations, obs_weights, damping, transition, obs_matrix, smoother_gain, prior_mean
):
    step_count, state_width = damping.shape
    panel_count = lax.axis_size("panel")
    row_count = state_width // panel_count
    panel_index = lax.axis_index("panel")
    time_index = lax.axis_index("tm")
    block_count = lax.axis_size("tm")
    is_first = (time_index == 0).astype(jnp.float32)
    is_final = (time_index == block_count - 1).astype(jnp.float32)
    trans_t = transition.T
    obs_t = obs_matrix.T
    row_ids = lax.broadcasted_iota(jnp.int32, (row_count, state_width), 0) + panel_index * row_count
    col_ids = lax.broadcasted_iota(jnp.int32, (row_count, state_width), 1)
    start_rows = (row_ids == col_ids).astype(jnp.float32) * (1.0 - is_first)
    step_ids = lax.broadcasted_iota(jnp.int32, (step_count, 1), 0)
    inject = (step_ids == 0).astype(jnp.float32) * is_first * prior_mean[None, :]

    def forward_step(carried, inputs):
        panel_rows, estimate = carried
        obs_row, weight_row, damp_row, inject_row = inputs
        estimate = filter_update(
            estimate, obs_row, weight_row, damp_row, inject_row, transition, obs_matrix
        )
        advanced = product(panel_rows * damp_row[None, :], trans_t)
        panel_rows = advanced - product(product(advanced, obs_t) * weight_row[None, :], obs_matrix)
        return ((panel_rows, estimate), (estimate, panel_rows))

    zero_state = jnp.zeros((state_width,), jnp.float32)
    step_inputs = (observations, obs_weights, damping, inject)
    (panel_rows, block_end), trajectory = lax.scan(
        forward_step, (start_rows, zero_state), step_inputs
    )
    base_means = trajectory[0]
    summary = lax.all_gather(panel_rows, "panel", axis=0, tiled=True)
    identity = jnp.eye(state_width, dtype=jnp.float32)

    def chain_forward(inner_part, outer_part):
        return (
            product(inner_part[0], outer_part[0]),
            product(inner_part[1], outer_part[0]) + outer_part[1],
        )

    entering = prefix((summary, block_end), "tm", chain_forward, (identity, zero_state), False)[1]
    own_part = lax.dynamic_slice_in_dim(entering, panel_index * row_count, row_count)
    partial_terms = jnp.einsum("c,tcn->tn", own_part, trajectory[1], precision=highest)
    filtered = base_means + lax.psum(partial_terms, "panel")
    end_flags = (step_ids == step_count - 1).astype(jnp.float32) * is_final
    gain_powers = [smoother_gain]
    for bit_index in range(1, step_count.bit_length()):
        gain_powers.append(product(gain_powers[-1], gain_powers[-1]))
    gain_trans = product(smoother_gain, transition)
    base_smooth = filtered - (1.0 - end_flags) * product(filtered, gain_trans.T)
    for level_index in range((step_count - 1).bit_length()):
        distance = 1 << level_index
        later_rows = jnp.concatenate(
            [base_smooth[distance:], jnp.zeros((distance, state_width), jnp.float32)], axis=0
        )
        base_smooth = base_smooth + product(later_rows, gain_powers[level_index].T)
    offset = base_smooth[0]
    block_power = identity
    for bit_index in range(step_count.bit_length()):
        if step_count >> bit_index & 1:
            block_power = product(block_power, gain_powers[bit_index])

    def chain_backward(inner_part, outer_part):
        return (
            product(outer_part[0], inner_part[0]),
            product(outer_part[0], inner_part[1]) + outer_part[1],
        )

    element = (block_power * (1.0 - is_final), offset)
    incoming = prefix(element, "tm", chain_backward, (identity, zero_state), True)[1]
    lifted = product(smoother_gain, incoming)[None, :]
    for level_index in range((step_count - 1).bit_length()):
        lifted = jnp.concatenate([lifted, product(lifted, gain_powers[level_index].T)], axis=0)
    smoothed = base_smooth + jnp.flip(lifted, 0)
    return (filtered, smoothed)


def solution(mesh):
    return jax.shard_map(
        per_device,
        mesh=mesh,
        in_specs=(P("tm", None), P("tm", None), P("tm", None), P(), P(), P(), P()),
        out_specs=(P("tm", None), P("tm", None)),
        check_vma=False,
    )
```

profile of v0, /device:TPU:0, one launch (start us, length us, event | category | flops | bytes accessed | tf_op | source)
XLA Modules:
  0.0 505.2 jit_solution(17998382190177535720)
XLA Ops:
  10.1 238.2 %while.45 = (s32[]{:T(128)}, f32[256,256]{1,0:T(8,128)S(1)}, f32[256]{0:T(256)S(1)}, f32[32,256]{1,0:T(8,128)S(1)}, f32[32,256,256]{2,1,0:T(8,128)}, /*index=5*/...) while((s32[]{:T(128)}, f32[256,256]{1,0:T(8,128)S(1)}, ...), condition=%wide.region_1.2_spmd.clone, body=%wide.region_0.1_spmd.clone.sunk | while | flops 303318144 | bytes 2512819 | solution.py:67
  27.1 1.9 bitcast_dynamic-update-slice_fusion.2
  34.6 1.9 bitcast_dynamic-update-slice_fusion.2
  42.0 1.9 bitcast_dynamic-update-slice_fusion.2
  49.5 1.9 bitcast_dynamic-update-slice_fusion.2
  56.9 1.9 bitcast_dynamic-update-slice_fusion.2
  64.4 1.9 bitcast_dynamic-update-slice_fusion.2
  79.3 1.9 bitcast_dynamic-update-slice_fusion.2
  86.7 1.9 bitcast_dynamic-update-slice_fusion.2
  94.2 1.9 bitcast_dynamic-update-slice_fusion.2
  109.0 1.9 bitcast_dynamic-update-slice_fusion.2
  116.5 1.9 bitcast_dynamic-update-slice_fusion.2
  146.2 1.9 bitcast_dynamic-update-slice_fusion.2
  153.7 1.9 bitcast_dynamic-update-slice_fusion.2
  161.1 1.9 bitcast_dynamic-update-slice_fusion.2
  168.6 1.9 bitcast_dynamic-update-slice_fusion.2
  176.1 1.9 bitcast_dynamic-update-slice_fusion.2
  183.5 1.9 bitcast_dynamic-update-slice_fusion.2
  198.4 1.9 bitcast_dynamic-update-slice_fusion.2
  205.8 1.9 bitcast_dynamic-update-slice_fusion.2
  213.3 1.9 bitcast_dynamic-update-slice_fusion.2
  228.2 1.9 bitcast_dynamic-update-slice_fusion.2
  235.6 1.9 bitcast_dynamic-update-slice_fusion.2
  243.1 1.9 bitcast_dynamic-update-slice_fusion.2
  253.5 43.7 %all-gather.3 = f32[32,1,256]{2,1,0:T(1,128)S(1)} all-gather(f32[1,1,256]{2,1,0:T(1,128)S(1)} %bitcast.183), channel_id=3, replica_groups=mesh['tm'=32,'panel'=1] {'tm'}, dimensions={0}, use_global_device_ids=true | all-gather | bytes 33792 | tf_op jit(solution)/shard_map/all_gather | solution.py:11
  297.1 31.8 %all-gather.8.cloned.1.call-done = f32[8192,256]{1,0:T(8,128)} async-done(((f32[256,256]{1,0:T(8,128)}), f32[8192,256]{1,0:T(8,128)}) %all-gather.8.cloned.1.call-update) | async-done | bytes 8388624 | tf_op jit(solution)/shard_map/all_gather | solution.py:11
  329.0 39.1 %while.46 = (s32[]{:T(128)}, f32[256]{0:T(256)S(1)}, s32[]{:T(128)}, f32[32,256,256]{2,1,0:T(8,128)}, f32[32,256]{1,0:T(8,128)S(1)}, /*index=5*/s32[]{:T(128)}, s32[]{:T(128)}) while((s32[]{:T(128)}, f32[256]{0:T(256)S(1)}, s32[]{:T(128)}, f32[32,256,256]{2,1,0:T(8,128)}, f32[32,256]{1,0:T(8,128)S(1)}, /*index=5*/s32[]{:T(128)}, ...), condition=%wide.region_3.4_spmd.clone, body=%wide.region_2.3_spmd.clone.sunk | while | flops 787460 | bytes 272498 | solution.py:23
  368.1 7.4 %fusion.54 = f32[1,32,256]{2,0,1:T(1,128)S(1)} fusion(f32[256,1,1]{0,1,2:T(1,128)S(1)} %bitcast.181, f32[32,256,256]{2,1,0:T(8,128)} %get-tuple-element.264), kind=kOutput, calls=%fused_computation.84 | convolution fusion | flops 25165824 | bytes 8422400 | tf_op jit(solution)/shard_map/c,tcn->tn/dot_general | solution.py:82
  377.7 29.7 %all-gather.10.cloned.1.call-done = f32[8192,256]{1,0:T(8,128)} async-done(((f32[256,256]{1,0:T(8,128)}), f32[8192,256]{1,0:T(8,128)}) %all-gather.10.cloned.1.call-update) | async-done | bytes 8388624 | tf_op jit(solution)/shard_map/all_gather | solution.py:11
  407.4 7.5 %rev.10 = f32[32,256,256]{2,1,0:T(8,128)} reverse(f32[32,256,256]{2,1,0:T(8,128)} %bitcast.173), dimensions={0} | reverse | bytes 16777216 | tf_op jit(solution)/shard_map/rev | solution.py:13
  414.9 39.1 %all-gather.4 = f32[32,1,256]{2,1,0:T(1,128)S(1)} all-gather(f32[1,1,256]{2,1,0:T(1,128)S(1)} %slice_bitcast_fusion), channel_id=1, replica_groups=mesh['tm'=32,'panel'=1] {'tm'}, dimensions={0}, use_global_device_ids=true | all-gather | bytes 33792 | tf_op jit(solution)/shard_map/all_gather | solution.py:11
  454.1 41.6 %while.47 = (s32[]{:T(128)}, f32[256]{0:T(256)S(1)}, s32[]{:T(128)}, f32[32,256,256]{2,1,0:T(8,128)}, f32[32,256]{1,0:T(8,128)S(1)}, /*index=5*/s32[]{:T(128)}, s32[]{:T(128)}) while((s32[]{:T(128)}, f32[256]{0:T(256)S(1)}, s32[]{:T(128)}, f32[32,256,256]{2,1,0:T(8,128)}, f32[32,256]{1,0:T(8,128)S(1)}, /*index=5*/s32[]{:T(128)}, ...), condition=%wide.region_5.6_spmd.clone, body=%wide.region_4.5_spmd.clone.sunk | while | flops 787460 | bytes 272498 | solution.py:23
  (663 shorter events, 282.2 us)
Async XLA Ops:
  7.2 242.0 %copy-start = (f32[256,256]{1,0:T(8,128)S(1)}, f32[256,256]{1,0:T(8,128)}, u32[]{:S(2)}) copy-start(f32[256,256]{1,0:T(8,128)} %param.18) | copy-start | bytes 786436
  7.2 321.8 %all-gather.8.cloned.1.call-start = ((), (), s32[]{:S(2)}) async-start(), calls=%async_computation | async-start | bytes 8650752 | tf_op jit(solution)/shard_map/all_gather | solution.py:11
  248.3 0.7 copy-start.1
  249.1 158.3 %all-gather.10.cloned.1.call-start = ((), (), s32[]{:S(2)}) async-start(), calls=%async_computation.1 | async-start | bytes 8650752 | tf_op jit(solution)/shard_map/all_gather | solution.py:11
  375.5 39.4 %copy-start.2 = (f32[32,256]{1,0:T(8,128)}, f32[32,256]{1,0:T(8,128)S(1)}, u32[]{:S(2)}) copy-start(f32[32,256]{1,0:T(8,128)S(1)} %bitcast_add_fusion) | copy-start | bytes 98308
Sparse Core Ops, SparseCore 0:
  249.2 79.7 all-gather.7
  331.8 75.5 all-gather.9
where the time goes:
time: 515 us; the launch traced here: 505 us
  matrix products  278 us (54%)
  blocking collectives  82.8 us (16%)
  waiting for transfers between devices  61.6 us (12%)
  local copies, waits for them, and re-layouts  59.6 us (12%)
  between operations  14.4 us (3%)
  loops' own time  5.4 us (1%)
    dot_general x273, matrix products, product(): jnp.dot(left, right, precision=highest, preferred_element_type=jnp.float32)  271 us
    all_gather x2, blocking collectives, prefix(): pieces = jax.tree.map(lambda part: lax.all_gather(part, axis), value)  82.8 us
    all_gather x2, waiting for transfers between devices, prefix(): pieces = jax.tree.map(lambda part: lax.all_gather(part, axis), value)  61.5 us
    dynamic_slice x32, local copies, waits for them, and re-layouts, per_device(): lax.scan(forward_step, (start_rows, zero_state), step_inputs)  22.6 us
    mul x32, local copies, waits for them, and re-layouts, forward_step(): product(advanced, obs_t) * weight_row[None, :]  22.3 us
  transfers between devices with their start and end apart: 2, of which 2 were waited for; matrix products, arithmetic and copies ran while one was open for 10% of the time, Pallas kernels for 0%

commit v1 on v0

v1 whole, which is shorter than its diff:
```python
import functools

import jax
import jax.numpy as jnp
from jax import lax
from jax.experimental import pallas as pl
from jax.experimental.pallas import tpu as pltpu
from jax.sharding import PartitionSpec as P

f32, bf16 = jnp.float32, jnp.bfloat16
highest = lax.Precision.HIGHEST
PAD = 8
CHUNKS = 4
PLANE = 8


def exact(left, right):
    return jnp.dot(left, right, precision=highest, preferred_element_type=f32)


def split(value):
    high = value.astype(bf16)
    return high, (value - high.astype(f32)).astype(bf16)


def stack_right(high, low):
    return jnp.concatenate([high, low, high], axis=0)


def dot_split(left, right_stack):
    high, low = split(left)
    return jnp.dot(
        jnp.concatenate([high, high, low], axis=1), right_stack, preferred_element_type=f32
    )


def compose(first, second):
    width = first.shape[1]
    joined = dot_split(first, stack_right(*split(second[:width])))
    return jnp.concatenate([joined[:width], joined[width:] + second[width:]], axis=0)


def eye_map(width):
    rows = lax.broadcasted_iota(jnp.int32, (width + PAD, width), 0)
    cols = lax.broadcasted_iota(jnp.int32, (width + PAD, width), 1)
    return (rows == cols).astype(f32)


def local_kernel(
    obs_ref, weight_ref, damp_ref, trans_ref, obsmat_ref, prior_ref,
    path_ref, chunk_ref, total_ref,
    high_ref, low_ref, state_ref, offset_ref, wide_ref, base_ref,
):
    steps, width = damp_ref.shape
    span = steps // CHUNKS
    is_first = (lax.axis_index("tm") == 0).astype(f32)
    obs_mat = obsmat_ref[...]
    weights = weight_ref[...]
    trans_t = trans_ref[...].T
    base_ref[0] = trans_t
    observed = lax.dot_general(
        trans_t, obs_mat, (((1,), (1,)), ((), ())), precision=highest, preferred_element_type=f32
    )
    base_ref[1] = jnp.concatenate([observed] * 4, axis=1)
    wide_ref[...] = jnp.concatenate([weights] * 4, axis=1)
    obs_high, obs_low = split(obs_mat)
    obs_stack = jnp.concatenate([obs_high, obs_low, obs_high, obs_low], axis=0)
    offsets = exact(weights * obs_ref[...], obs_mat)
    prior = jnp.broadcast_to(prior_ref[...], (PAD, width))
    seen = lax.dot_general(
        prior, obs_mat, (((1,), (1,)), ((), ())), precision=highest, preferred_element_type=f32
    )
    begun = prior - exact(seen * weights[0:1], obs_mat)
    step_ids = lax.broadcasted_iota(jnp.int32, (steps, 1), 0)
    offsets = offsets + jnp.where(step_ids == 0, is_first, 0.0) * begun[0:1]
    offset_ref[...] = offsets

    def make(step, carry):
        scaled = base_ref[1] * wide_ref[pl.ds(step, 1), :]
        high, low = split(scaled)
        half = width // 2
        pieces = jnp.concatenate([high[:, :half], low[:, half:]], axis=1)
        moved = base_ref[0] - jnp.dot(pieces, obs_stack, preferred_element_type=f32)
        high, low = split(moved)
        high_ref[step] = high
        low_ref[step] = low
        return carry

    lax.fori_loop(0, steps, make, 0, unroll=2)

    identity = eye_map(width)
    for chunk in range(CHUNKS):
        state_ref[chunk] = identity * (1.0 - is_first) if chunk == 0 else identity

    def advance(step, carry):
        for chunk in range(CHUNKS):
            time = chunk * span + step
            damped = state_ref[chunk] * damp_ref[pl.ds(time, 1), :]
            moved = dot_split(damped, stack_right(high_ref[time], low_ref[time]))
            moved = jnp.concatenate(
                [moved[:width], moved[width:] + offset_ref[pl.ds(time, 1), :]], axis=0
            )
            state_ref[chunk] = moved
            path_ref[time] = moved
        return carry

    lax.fori_loop(0, span, advance, 0)

    entering = state_ref[0]
    for chunk in range(1, CHUNKS):
        chunk_ref[chunk - 1] = entering
        entering = compose(entering, state_ref[chunk])
    total_ref[...] = entering


def pair_kernel(mine_ref, other_ref, chip_ref, half_ref):
    core = lax.axis_index("tm") % 2
    mine, other = mine_ref[...], other_ref[...]
    upper = core == 1
    whole = compose(jnp.where(upper, other, mine), jnp.where(upper, mine, other))
    chip_ref[...] = whole
    half = whole.shape[1] // 2
    half_ref[...] = jnp.where(upper, whole[:, half:], whole[:, :half])


def plane_kernel(chip_ref, mine_ref, other_ref, plane_ref, before_ref, all_ref, prefix_ref):
    me = lax.axis_index("tm")
    upper = me % 2 == 1
    place = (me // 2) % 4
    half = chip_ref.shape[1] // 2
    all_ref[place] = chip_ref[...]
    for distance in range(1, 4):
        mine, other = mine_ref[distance - 1], other_ref[distance - 1]
        all_ref[place ^ distance, :, :half] = jnp.where(upper, other, mine)
        all_ref[place ^ distance, :, half:] = jnp.where(upper, mine, other)
    running = all_ref[0]
    prefix_ref[0] = eye_map(chip_ref.shape[1])
    for position in range(1, 4):
        prefix_ref[position] = running
        running = compose(running, all_ref[position])
    plane_ref[...] = running
    before_ref[...] = prefix_ref[place]


def entry_kernel(before_ref, other_ref, chunk_ref, entry_ref):
    upper = lax.axis_index("tm") % 2 == 1
    before = before_ref[...]
    joined = compose(before, other_ref[...])
    start = jnp.where(upper, joined, before)
    entry_ref[0] = start
    for chunk in range(1, CHUNKS):
        entry_ref[chunk] = compose(start, chunk_ref[chunk - 1])


def power_kernel(trans_ref, gain_ref, mix_ref, high_ref, low_ref):
    gain_t = gain_ref[...].T
    mix_high, mix_low = split(exact(trans_ref[...].T, gain_t))
    mix_ref[...] = stack_right(mix_high, mix_low)
    power = gain_t
    for level in range(high_ref.shape[0]):
        high_ref[level], low_ref[level] = split(power)
        if level + 1 < high_ref.shape[0]:
            power = exact(power, power)


def suffix_scan(rows, high_ref, low_ref, first_level, levels):
    count, width = rows.shape
    for level in range(levels):
        distance = 1 << level
        later = jnp.concatenate(
            [rows[distance:], jnp.zeros((distance, width), f32)], axis=0
        )
        right = stack_right(high_ref[first_level + level], low_ref[first_level + level])
        rows = rows + dot_split(later, right)
    return rows


def filter_kernel(
    enter_ref, entry_ref, path_ref, mix_ref, high_ref, low_ref,
    filtered_ref, local_ref, *, levels
):
    steps, _, width = path_ref.shape
    span = steps // CHUNKS
    is_final = lax.axis_index("tm") == lax.axis_size("tm") - 1
    column = jnp.broadcast_to(enter_ref[0:1], (PAD, width)).T[:, 0:1]
    for chunk in range(CHUNKS):
        entry = entry_ref[chunk]
        start = jnp.sum(entry[:width] * column, axis=0, keepdims=True) + entry[width : width + 1]
        begin = jnp.broadcast_to(start, (PAD, width)).T[:, 0:1]
        for step in range(chunk * span, (chunk + 1) * span):
            path = path_ref[step, :width]
            filtered_ref[step : step + 1] = (
                jnp.sum(path * begin, axis=0, keepdims=True) + path_ref[step, width : width + 1]
            )
    filtered = filtered_ref[...]
    step_ids = lax.broadcasted_iota(jnp.int32, (steps, 1), 0)
    keep = jnp.where(jnp.logical_and(step_ids == steps - 1, is_final), 0.0, 1.0)
    change = filtered - keep * dot_split(filtered, mix_ref[...])
    local_ref[...] = suffix_scan(change, high_ref, low_ref, 0, levels)


def smooth_kernel(all_ref, local_ref, high_ref, low_ref, out_ref, sum_ref, *, levels):
    count, width = all_ref.shape
    steps = local_ref.shape[0]
    me = lax.axis_index("tm")
    sum_ref[pl.ds(count, PAD), :] = jnp.zeros((PAD, width), f32)
    sum_ref[pl.ds(0, count), :] = suffix_scan(
        all_ref[...], high_ref, low_ref, levels, (count - 1).bit_length()
    )
    incoming = jnp.broadcast_to(sum_ref[pl.ds(me + 1, 1), :], (PAD, width))
    lifted = dot_split(incoming, stack_right(high_ref[0], low_ref[0]))[0:1]
    step_ids = lax.broadcasted_iota(jnp.int32, (steps, 1), 0)
    rows = jnp.where(step_ids == steps - 1, lifted, 0.0)
    out_ref[...] = local_ref[...] + suffix_scan(rows, high_ref, low_ref, 0, levels)


def call(kernel, outs, scratch=(), flops=0, limit=16):
    return pl.pallas_call(
        kernel,
        out_shape=outs,
        scratch_shapes=scratch,
        compiler_params=pltpu.CompilerParams(vmem_limit_bytes=limit << 20),
        cost_estimate=pl.CostEstimate(flops=flops, bytes_accessed=1 << 20, transcendentals=0),
    )


def swap(count, distance):
    return [(index, index ^ distance) for index in range(count)]


def per_device(
    observations, obs_weights, damping, transition, obs_matrix, smoother_gain, prior_mean
):
    steps, width = damping.shape
    count = lax.axis_size("tm")
    rows = width + PAD
    levels = (steps - 1).bit_length()
    cube = 2 * width**3

    def struct(*shape, dtype=f32):
        return jax.ShapeDtypeStruct(shape, dtype)

    path, chunk_maps, total = call(
        local_kernel,
        (struct(steps, rows, width), struct(CHUNKS - 1, rows, width), struct(rows, width)),
        (
            pltpu.VMEM((steps, width, width), bf16),
            pltpu.VMEM((steps, width, width), bf16),
            pltpu.VMEM((CHUNKS, rows, width), f32),
            pltpu.VMEM((steps, width), f32),
            pltpu.VMEM((steps, width), f32),
            pltpu.VMEM((2, width, width), f32),
        ),
        flops=130 * cube,
        limit=36,
    )(observations, obs_weights, damping, transition, obs_matrix, prior_mean[None, :])

    power_count = levels + max((count - 1).bit_length(), 1)
    mix, power_high, power_low = call(
        power_kernel,
        (
            struct(3 * width, width, dtype=bf16),
            struct(power_count, width, width, dtype=bf16),
            struct(power_count, width, width, dtype=bf16),
        ),
        flops=60 * cube,
    )(transition, smoother_gain)

    partner = lax.ppermute(total, "tm", swap(count, 1))
    chip, half = call(
        pair_kernel, (struct(rows, width), struct(rows, width // 2)), flops=3 * cube
    )(total, partner)

    halves = jnp.stack(
        [lax.ppermute(half, "tm", swap(count, 2 * distance)) for distance in range(1, 4)]
    )
    other_halves = lax.ppermute(halves, "tm", swap(count, 1))
    plane, before = call(
        plane_kernel,
        (struct(rows, width), struct(rows, width)),
        (pltpu.VMEM((4, rows, width), f32), pltpu.VMEM((4, rows, width), f32)),
        flops=9 * cube,
    )(chip, halves, other_halves)
    entry = call(entry_kernel, struct(CHUNKS, rows, width), flops=12 * cube)(
        before, partner, chunk_maps
    )

    group = lax.axis_index("tm") // PLANE
    enter = jnp.zeros((1, width), f32)
    for hop in range(count // PLANE - 1):
        leave = jnp.sum(plane[:width] * enter.T, axis=0, keepdims=True) + plane[width : width + 1]
        low, high = hop * PLANE, (hop + 1) * PLANE
        pairs = [(low + i, high + i) for i in range(PLANE)]
        pairs = pairs + [(b, a) for a, b in pairs]
        enter = jnp.where(group == hop + 1, lax.ppermute(leave, "tm", pairs), enter)

    filtered, local = call(
        functools.partial(filter_kernel, levels=levels),
        (struct(steps, width), struct(steps, width)),
        flops=20 * cube,
        limit=32,
    )(enter, entry, path, mix, power_high, power_low)

    sent = jnp.broadcast_to(local[0:1], (count, width))
    offsets = lax.all_to_all(sent, "tm", 0, 0, tiled=True)
    smoothed = call(
        functools.partial(smooth_kernel, levels=levels),
        struct(steps, width),
        (pltpu.VMEM((count + PAD, width), f32),),
        flops=20 * cube,
    )(offsets, local, power_high, power_low)
    return filtered, smoothed


def solution(mesh):
    return jax.shard_map(
        per_device,
        mesh=mesh,
        in_specs=(P("tm", None), P("tm", None), P("tm", None), P(), P(), P(), P()),
        out_specs=(P("tm", None), P("tm", None)),
        check_vma=False,
    )
```

time: 515 us -> 80.1 us (0.16); the launches traced: 505 us -> 79.5 us
  matrix products: 278 us -> 0 us
  blocking collectives: 82.8 us -> 15.5 us
  waiting for transfers between devices: 61.6 us -> 11.6 us
  local copies, waits for them, and re-layouts: 59.6 us -> 17.1 us
  Pallas kernels: 0 us -> 23.3 us
  between operations: 14.4 us -> 0.83 us
  starting transfers between devices: 0.08 us -> 10.3 us
  loops' own time: 5.4 us -> 0 us
    dot_general x274 -> x0, matrix products: 278 us -> none  [the longest x273 271 us: product(): jnp.dot(left, right, precision=highest, preferred_element_type=jnp.float32)]
    all_gather x2 -> x0, blocking collectives: 82.8 us -> none  [prefix(): pieces = jax.tree.map(lambda part: lax.all_gather(part, axis), value)]
    all_gather x2 -> x0, waiting for transfers between devices: 61.5 us -> none  [prefix(): pieces = jax.tree.map(lambda part: lax.all_gather(part, axis), value)]
    dynamic_slice x94 -> x0, local copies, waits for them, and re-layouts: 25.5 us -> none  [the longest x32 22.6 us: per_device(): lax.scan(forward_step, (start_rows, zero_state), step_inputs)]
    pallas_call x0 -> x7, Pallas kernels: none -> 23.3 us  [the longest x1 10.8 us: per_device(): call(local_kernel, (struct(steps, rows, width), struct(CHUNKS - 1, rows,...]
    mul x32 -> x0, local copies, waits for them, and re-layouts: 22.3 us -> none  [forward_step(): product(advanced, obs_t) * weight_row[None, :]]
    all_to_all x0 -> x1, blocking collectives: none -> 15.5 us  [per_device(): offsets = lax.all_to_all(sent, 'tm', 0, 0, tiled=True)]
    unnamed x11 -> x31, local copies, waits for them, and re-layouts: 2.75 us -> 17.1 us
  transfers between devices with their start and end apart: 2 -> 8, of which waited for: 2 -> 5; matrix products, arithmetic and copies ran while one was open for 10% -> 0% of each run, Pallas kernels for 0% -> 7%
where the time goes in v1:
time: 80.1 us; the launch traced here: 79.5 us
  Pallas kernels  23.3 us (29%)
  local copies, waits for them, and re-layouts  17.1 us (21%)
  blocking collectives  15.5 us (19%)
  waiting for transfers between devices  11.6 us (14%)
  starting transfers between devices  10.3 us (13%)
  other arithmetic  0.94 us (1%)
  between operations  0.83 us (1%)
    unnamed x31, local copies, waits for them, and re-layouts  17.1 us
    all_to_all x1, blocking collectives, per_device(): offsets = lax.all_to_all(sent, 'tm', 0, 0, tiled=True)  15.5 us
    pallas_call x1, Pallas kernels, per_device(): call(local_kernel, (struct(steps, rows, width), struct(CHUNKS - 1, rows,...  10.8 us
    ppermute x3, waiting for transfers between devices, per_device(): lax.ppermute(half, 'tm', swap(count, 2 * distance))  6.7 us
    ppermute x3, starting transfers between devices, per_device(): enter = jnp.where(group == hop + 1, lax.ppermute(leave, 'tm', pairs), enter)  5.32 us
    pallas_call x1, Pallas kernels, per_device(): call(power_kernel, (struct(3 * width, width, dtype=bf16), struct(power_co...  4.9 us
    ppermute x3, starting transfers between devices, per_device(): lax.ppermute(half, 'tm', swap(count, 2 * distance))  4.46 us
    pallas_call x1, Pallas kernels, per_device(): call(functools.partial(filter_kernel, levels=levels), (struct(steps, widt...  2.81 us
  transfers between devices with their start and end apart: 8, of which 5 were waited for; matrix products, arithmetic and copies ran while one was open for 0% of the time, Pallas kernels for 7%

profile of v1, /device:TPU:0, one launch (start us, length us, event | category | flops | bytes accessed | tf_op | source)
XLA Modules:
  0.0 79.5 jit_solution(5461540970880010527)
XLA Ops:
  0.6 0.9 %copy-done.6 = f32[256,256]{1,0:T(8,128)S(1)} copy-done((f32[256,256]{1,0:T(8,128)S(1)}, f32[256,256]{1,0:T(8,128)}, u32[]{:S(2)}) %copy-start.6) | copy-done | bytes 262168
  1.6 0.8 %copy-done.9 = f32[64,256]{1,0:T(8,128)S(1)} copy-done((f32[64,256]{1,0:T(8,128)S(1)}, f32[64,256]{1,0:T(8,128)}, u32[]{:S(2)}) %copy-start.9) | copy-done | bytes 65560
  2.4 0.8 copy-done.10
  3.2 0.7 copy-done.11
  3.9 0.7 copy-done.12
  4.6 0.7 copy-done.13
  5.3 10.8 %shard_map.86 = (f32[32,264,256]{2,1,0:T(8,128)S(1)}, f32[3,264,256]{2,1,0:T(8,128)S(1)}, f32[264,256]{1,0:T(8,128)S(1)}) custom-call(f32[32,64]{1,0:T(8,128)S(1)} %copy-done.11, f32[32,64]{1,0:T(8,128)S(1)} %copy-done.12, f32[32,256]{1,0:T(8,128)S(1)} %copy-done.10, f32[256,256]{1,0:T(8,128)S(1)} %copy-done.6, f32[64,256]{1,0:T(8,128)S(1)} %copy-done.9, ...), custom_call_target="tpu_custom_call" | custom-call | flops 4362076160 | bytes 1048576 | tf_op jit(solution)/shard_map/pallas_call | solution.py:243
  16.1 3.3 %copy-done = f32[32,264,256]{2,1,0:T(8,128)} copy-done((f32[32,264,256]{2,1,0:T(8,128)}, f32[32,264,256]{2,1,0:T(8,128)S(1)}, u32[]{:S(2)}) %copy-start) | copy-done | bytes 8650776
  19.4 1.0 %copy-done.2 = f32[3,264,256]{2,1,0:T(8,128)} copy-done((f32[3,264,256]{2,1,0:T(8,128)}, f32[3,264,256]{2,1,0:T(8,128)S(1)}, u32[]{:S(2)}) %copy-start.2) | copy-done | bytes 811032
  20.9 1.2 %collective-permute-done.other_ref = f32[264,256]{1,0:T(8,128)S(1)} collective-permute-done((f32[264,256]{1,0:T(8,128)S(1)}, f32[264,256]{1,0:T(8,128)S(1)}, u32[]{:S(2)}, u32[]{:S(2)}) %collective-permute-start) | collective-permute-done | bytes 270368 | tf_op jit(solution)/shard_map/ppermute | solution.py:269
  22.4 2.9 %collective-permute-start.1 = (f32[264,128]{1,0:T(8,128)S(1)}, f32[264,128]{1,0:T(8,128)S(1)}, u32[]{:S(2)}, u32[]{:S(2)}) collective-permute-start(f32[264,128]{1,0:T(8,128)S(1)} %get-tuple-element.16), channel_id=1, source_target_pairs={{0,2},{1,3},{2,0},{3,1},{4,6},{5,7},{6,4},{7,5},{8,10},{9,11},{10,... | collective-permute-start | bytes 405512 | tf_op jit(solution)/shard_map/ppermute | solution.py:275
  25.3 1.5 %collective-permute-start.2 = (f32[264,128]{1,0:T(8,128)S(1)}, f32[264,128]{1,0:T(8,128)S(1)}, u32[]{:S(2)}, u32[]{:S(2)}) collective-permute-start(f32[264,128]{1,0:T(8,128)S(1)} %get-tuple-element.16), channel_id=1, source_target_pairs={{0,4},{1,5},{2,6},{3,7},{4,0},{5,1},{6,2},{7,3},{8,12},{9,13},{10,... | collective-permute-start | bytes 405512 | tf_op jit(solution)/shard_map/ppermute | solution.py:275
  26.8 2.6 %collective-permute-done.1 = f32[264,128]{1,0:T(8,128)S(1)} collective-permute-done((f32[264,128]{1,0:T(8,128)S(1)}, f32[264,128]{1,0:T(8,128)S(1)}, u32[]{:S(2)}, u32[]{:S(2)}) %collective-permute-start.1) | collective-permute-done | bytes 135200 | tf_op jit(solution)/shard_map/ppermute | solution.py:275
  29.4 4.1 %collective-permute-done.2 = f32[264,128]{1,0:T(8,128)S(1)} collective-permute-done((f32[264,128]{1,0:T(8,128)S(1)}, f32[264,128]{1,0:T(8,128)S(1)}, u32[]{:S(2)}, u32[]{:S(2)}) %collective-permute-start.2) | collective-permute-done | bytes 135200 | tf_op jit(solution)/shard_map/ppermute | solution.py:275
  33.6 1.7 %collective-permute-done.4.other_ref = f32[3,264,128]{2,1,0:T(8,128)S(1)} collective-permute-done((f32[3,264,128]{2,1,0:T(8,128)S(1)}, f32[3,264,128]{2,1,0:T(8,128)S(1)}, u32[]{:S(2)}, u32[]{:S(2)}) %collective-permute-start.4) | collective-permute-done | bytes 405536 | tf_op jit(solution)/shard_map/ppermute | solution.py:277
  35.4 0.9 %shard_map.88 = (f32[264,256]{1,0:T(8,128)S(1)}, f32[264,256]{1,0:T(8,128)S(1)}) custom-call(f32[264,256]{1,0:T(8,128)S(1)} %get-tuple-element.15.chip_ref, f32[3,264,128]{2,1,0:T(8,128)S(1)} %pad_maximum_fusion.mine_ref, f32[3,264,128]{2,1,0:T(8,128)S(1)} %collective-permute-done.4.other_ref), custom_call_target="tpu_custom_call" | custom-call | flops 301989888 | bytes 1048576 | tf_op jit(solution)/shard_map/pallas_call | solution.py:278
  36.3 0.7 copy-done.4
  37.1 3.5 %collective-permute-start.5 = (f32[1,256]{1,0:T(1,128)S(1)}, f32[1,256]{1,0:T(1,128)S(1)}, u32[]{:S(2)}, u32[]{:S(2)}) collective-permute-start(f32[1,256]{1,0:T(1,128)S(1)} %slice_add_fusion.2), channel_id=1, source_target_pairs={{0,8},{1,9},{2,10},{3,11},{4,12},{5,13},{6,14},{7,15},{8,0},{9,1},... | collective-permute-start | bytes 3080 | tf_op jit(solution)/shard_map/ppermute | solution.py:295
  40.6 2.0 %collective-permute-done.5 = f32[1,256]{1,0:T(1,128)S(1)} collective-permute-done((f32[1,256]{1,0:T(1,128)S(1)}, f32[1,256]{1,0:T(1,128)S(1)}, u32[]{:S(2)}, u32[]{:S(2)}) %collective-permute-start.5) | collective-permute-done | bytes 1056 | tf_op jit(solution)/shard_map/ppermute | solution.py:295
  42.6 0.6 slice_add_fusion.1
  43.2 1.2 %collective-permute-start.6 = (f32[1,256]{1,0:T(1,128)}, f32[1,256]{1,0:T(1,128)}, u32[]{:S(2)}, u32[]{:S(2)}) collective-permute-start(f32[1,256]{1,0:T(1,128)} %slice_add_fusion.1), channel_id=1, source_target_pairs={{8,16},{9,17},{10,18},{11,19},{12,20},{13,21},{14,22},{15,23},{16,... | collective-permute-start | bytes 3080 | tf_op jit(solution)/shard_map/ppermute | solution.py:295
  44.4 0.9 %copy-done.7 = f32[256,256]{1,0:T(8,128)S(1)} copy-done((f32[256,256]{1,0:T(8,128)S(1)}, f32[256,256]{1,0:T(8,128)}, u32[]{:S(2)}) %copy-start.7) | copy-done | bytes 262168
  45.4 0.9 %copy-done.8 = f32[256,256]{1,0:T(8,128)S(1)} copy-done((f32[256,256]{1,0:T(8,128)S(1)}, f32[256,256]{1,0:T(8,128)}, u32[]{:S(2)}) %copy-start.8) | copy-done | bytes 262168
  46.3 4.9 %shard_map.90 = (bf16[768,256]{1,0:T(8,128)(2,1)S(1)}, bf16[10,256,256]{2,1,0:T(8,128)(2,1)S(1)}, bf16[10,256,256]{2,1,0:T(8,128)(2,1)S(1)}) custom-call(f32[256,256]{1,0:T(8,128)S(1)} %copy-done.7, f32[256,256]{1,0:T(8,128)S(1)} %copy-done.8), custom_call_target="tpu_custom_call" | custom-call | flops 2013265920 | bytes 1048576 | tf_op jit(solution)/shard_map/pallas_call | solution.py:259
  51.4 0.7 collective-permute-start.7
  52.1 1.1 %copy-done.3 = f32[3,264,256]{2,1,0:T(8,128)S(1)} copy-done((f32[3,264,256]{2,1,0:T(8,128)S(1)}, f32[3,264,256]{2,1,0:T(8,128)}, u32[]{:S(2)}) %copy-start.3) | copy-done | bytes 811032
  53.2 1.0 %copy-done.5 = f32[264,256]{1,0:T(8,128)S(1)} copy-done((f32[264,256]{1,0:T(8,128)S(1)}, f32[264,256]{1,0:T(8,128)}, u32[]{:S(2)}) %copy-start.5) | copy-done | bytes 270360
  54.2 0.9 %shard_map.89.entry_ref = f32[4,264,256]{2,1,0:T(8,128)S(1)} custom-call(f32[264,256]{1,0:T(8,128)S(1)} %copy-done.5, f32[264,256]{1,0:T(8,128)S(1)} %collective-permute-done.other_ref, f32[3,264,256]{2,1,0:T(8,128)S(1)} %copy-done.3), custom_call_target="tpu_custom_call" | custom-call | flops 402653184 | bytes 1048576 | tf_op jit(solution)/shard_map/pallas_call | solution.py:284
  55.1 3.4 %copy-done.1 = f32[32,264,256]{2,1,0:T(8,128)S(1)} copy-done((f32[32,264,256]{2,1,0:T(8,128)S(1)}, f32[32,264,256]{2,1,0:T(8,128)}, u32[]{:S(2)}) %copy-start.1) | copy-done | bytes 8650776
  58.5 2.8 %shard_map.91 = (f32[32,256]{1,0:T(8,128)}, f32[32,256]{1,0:T(8,128)S(1)}) custom-call(f32[1,256]{1,0:T(1,128)S(1)} %broadcast_select_fusion.2.enter_ref, f32[4,264,256]{2,1,0:T(8,128)S(1)} %shard_map.89.entry_ref, f32[32,264,256]{2,1,0:T(8,128)S(1)} %copy-done.1, bf16[768,256]{1,0:T(8,128)(2,1)S(1)} %get-tuple-element.21.mix_ref, ...), custom_call_target="tpu_custom_call" | custom-call | flops 671088640 | bytes 1048576 | tf_op jit(solution)/shard_map/pallas_call | solution.py:297
  61.4 15.5 %all_to_all.8 = f32[32,1,256]{2,1,0:T(1,128)S(1)} all-to-all(f32[32,1,256]{2,1,0:T(1,128)S(1)} %broadcast_in_dim.25), channel_id=1, replica_groups=mesh['tm'=32,'panel'=1] {'tm'}, dimensions={0} | all-to-all | bytes 65536 | tf_op jit(solution)/shard_map/all_to_all | solution.py:305
  76.8 2.7 %shard_map.92 = f32[32,256]{1,0:T(8,128)} custom-call(f32[32,256]{1,0:T(8,128)S(1)} %bitcast.13, f32[32,256]{1,0:T(8,128)S(1)} %get-tuple-element.25.local_ref, bf16[10,256,256]{2,1,0:T(8,128)(2,1)S(1)} %get-tuple-element.22.high_ref, bf16[10,256,256]{2,1,0:T(8,128)(2,1)S(1)} %get-tuple-element.23.low_ref), custom_call_target="tpu_custom_call" | custom-call | flops 671088640 | bytes 1048576 | tf_op jit(solution)/shard_map/pallas_call | solution.py:306
  (35 shorter events, 1.3 us)
Async XLA Ops:
  0.6 1.0 %copy-start.6 = (f32[256,256]{1,0:T(8,128)S(1)}, f32[256,256]{1,0:T(8,128)}, u32[]{:S(2)}) copy-start(f32[256,256]{1,0:T(8,128)} %trans_ref.3) | copy-start | bytes 786436
  1.6 0.8 %copy-start.9 = (f32[64,256]{1,0:T(8,128)S(1)}, f32[64,256]{1,0:T(8,128)}, u32[]{:S(2)}) copy-start(f32[64,256]{1,0:T(8,128)} %obsmat_ref.1) | copy-start | bytes 196612
  2.4 0.8 copy-start.10
  3.2 0.7 copy-start.11
  3.9 0.7 copy-start.12
  4.6 0.7 copy-start.13
  16.1 3.3 %copy-start = (f32[32,264,256]{2,1,0:T(8,128)}, f32[32,264,256]{2,1,0:T(8,128)S(1)}, u32[]{:S(2)}) copy-start(f32[32,264,256]{2,1,0:T(8,128)S(1)} %get-tuple-element.20.path_ref) | copy-start | bytes 25952260
  19.4 1.0 %copy-start.2 = (f32[3,264,256]{2,1,0:T(8,128)}, f32[3,264,256]{2,1,0:T(8,128)S(1)}, u32[]{:S(2)}) copy-start(f32[3,264,256]{2,1,0:T(8,128)S(1)} %get-tuple-element.19.chunk_ref) | copy-start | bytes 2433028
  20.4 1.7 %collective-permute-start = (f32[264,256]{1,0:T(8,128)S(1)}, f32[264,256]{1,0:T(8,128)S(1)}, u32[]{:S(2)}, u32[]{:S(2)}) collective-permute-start(f32[264,256]{1,0:T(8,128)S(1)} %get-tuple-element.14.mine_ref), channel_id=1, source_target_pairs={{0,1},{1,0},{2,3},{3,2},{4,5},{5,4},{6,7},{7,6},{8,9},{9,8},{10,11... | collective-permute-start | bytes 811016 | tf_op jit(solution)/shard_map/ppermute | solution.py:269
  22.4 7.1 %collective-permute-start.1 = (f32[264,128]{1,0:T(8,128)S(1)}, f32[264,128]{1,0:T(8,128)S(1)}, u32[]{:S(2)}, u32[]{:S(2)}) collective-permute-start(f32[264,128]{1,0:T(8,128)S(1)} %get-tuple-element.16), channel_id=1, source_target_pairs={{0,2},{1,3},{2,0},{3,1},{4,6},{5,7},{6,4},{7,5},{8,10},{9,11},{10,... | collective-permute-start | bytes 405512 | tf_op jit(solution)/shard_map/ppermute | solution.py:275
  25.3 8.2 %collective-permute-start.2 = (f32[264,128]{1,0:T(8,128)S(1)}, f32[264,128]{1,0:T(8,128)S(1)}, u32[]{:S(2)}, u32[]{:S(2)}) collective-permute-start(f32[264,128]{1,0:T(8,128)S(1)} %get-tuple-element.16), channel_id=1, source_target_pairs={{0,4},{1,5},{2,6},{3,7},{4,0},{5,1},{6,2},{7,3},{8,12},{9,13},{10,... | collective-permute-start | bytes 405512 | tf_op jit(solution)/shard_map/ppermute | solution.py:275
  26.8 6.7 %collective-permute-start.3 = (f32[264,128]{1,0:T(8,128)S(1)}, f32[264,128]{1,0:T(8,128)S(1)}, u32[]{:S(2)}, u32[]{:S(2)}) collective-permute-start(f32[264,128]{1,0:T(8,128)S(1)} %get-tuple-element.16), channel_id=1, source_target_pairs={{0,6},{1,7},{2,4},{3,5},{4,2},{5,3},{6,0},{7,1},{8,14},{9,15},{10,... | collective-permute-start | bytes 405512 | tf_op jit(solution)/shard_map/ppermute | solution.py:275
  33.6 1.8 %collective-permute-start.4 = (f32[3,264,128]{2,1,0:T(8,128)S(1)}, f32[3,264,128]{2,1,0:T(8,128)S(1)}, u32[]{:S(2)}, u32[]{:S(2)}) collective-permute-start(f32[3,264,128]{2,1,0:T(8,128)S(1)} %pad_maximum_fusion.mine_ref), channel_id=1, source_target_pairs={{0,1},{1,0},{2,3},{3,2},{4,5},{5,4},{6,7},{7,6},{8,9},{9,8},{10,11... | collective-permute-start | bytes 1216520 | tf_op jit(solution)/shard_map/ppermute | solution.py:277
  36.3 0.7 copy-start.4
  37.1 5.5 %collective-permute-start.5 = (f32[1,256]{1,0:T(1,128)S(1)}, f32[1,256]{1,0:T(1,128)S(1)}, u32[]{:S(2)}, u32[]{:S(2)}) collective-permute-start(f32[1,256]{1,0:T(1,128)S(1)} %slice_add_fusion.2), channel_id=1, source_target_pairs={{0,8},{1,9},{2,10},{3,11},{4,12},{5,13},{6,14},{7,15},{8,0},{9,1},... | collective-permute-start | bytes 3080 | tf_op jit(solution)/shard_map/ppermute | solution.py:295
  42.5 0.7 copy-start.14
  43.2 8.0 %collective-permute-start.6 = (f32[1,256]{1,0:T(1,128)}, f32[1,256]{1,0:T(1,128)}, u32[]{:S(2)}, u32[]{:S(2)}) collective-permute-start(f32[1,256]{1,0:T(1,128)} %slice_add_fusion.1), channel_id=1, source_target_pairs={{8,16},{9,17},{10,18},{11,19},{12,20},{13,21},{14,22},{15,23},{16,... | collective-permute-start | bytes 3080 | tf_op jit(solution)/shard_map/ppermute | solution.py:295
  44.4 0.9 %copy-start.7 = (f32[256,256]{1,0:T(8,128)S(1)}, f32[256,256]{1,0:T(8,128)}, u32[]{:S(2)}) copy-start(f32[256,256]{1,0:T(8,128)} %trans_ref.3) | copy-start | bytes 786436
  45.4 0.9 %copy-start.8 = (f32[256,256]{1,0:T(8,128)S(1)}, f32[256,256]{1,0:T(8,128)}, u32[]{:S(2)}) copy-start(f32[256,256]{1,0:T(8,128)} %gain_ref.1) | copy-start | bytes 786436
  51.4 3.7 %collective-permute-start.7 = (f32[1,256]{1,0:T(1,128)S(1)}, f32[1,256]{1,0:T(1,128)S(1)}, u32[]{:S(2)}, u32[]{:S(2)}) collective-permute-start(f32[1,256]{1,0:T(1,128)S(1)} %slice_add_fusion), channel_id=1, source_target_pairs={{16,24},{17,25},{18,26},{19,27},{20,28},{21,29},{22,30},{23,31},{2... | collective-permute-start | bytes 3080 | tf_op jit(solution)/shard_map/ppermute | solution.py:295
  52.1 1.1 %copy-start.3 = (f32[3,264,256]{2,1,0:T(8,128)S(1)}, f32[3,264,256]{2,1,0:T(8,128)}, u32[]{:S(2)}) copy-start(f32[3,264,256]{2,1,0:T(8,128)} %copy-done.2) | copy-start | bytes 2433028
  53.2 1.0 %copy-start.5 = (f32[264,256]{1,0:T(8,128)S(1)}, f32[264,256]{1,0:T(8,128)}, u32[]{:S(2)}) copy-start(f32[264,256]{1,0:T(8,128)} %copy-done.4) | copy-start | bytes 811012
  55.1 3.5 %copy-start.1 = (f32[32,264,256]{2,1,0:T(8,128)S(1)}, f32[32,264,256]{2,1,0:T(8,128)}, u32[]{:S(2)}) copy-start(f32[32,264,256]{2,1,0:T(8,128)} %copy-done) | copy-start | bytes 25952260

commit v2 on v1

--- a/solution.py
+++ b/solution.py
@@ -46,11 +46,28 @@
     return (rows == cols).astype(f32)
 
 
+def fetch(sources, targets, sems):
+    copies = [
+        pltpu.make_async_copy(source, target, sems.at[index])
+        for index, (source, target) in enumerate(zip(sources, targets))
+    ]
+    for copy in copies:
+        copy.start()
+    for copy in copies:
+        copy.wait()
+
+
 def local_kernel(
-    obs_ref, weight_ref, damp_ref, trans_ref, obsmat_ref, prior_ref,
+    obs_hbm, weight_hbm, damp_hbm, trans_hbm, obsmat_hbm, prior_hbm,
     path_ref, chunk_ref, total_ref,
     high_ref, low_ref, state_ref, offset_ref, wide_ref, base_ref,
+    obs_ref, weight_ref, damp_ref, trans_ref, obsmat_ref, prior_ref, sems,
 ):
+    fetch(
+        (trans_hbm, obsmat_hbm, damp_hbm, weight_hbm, obs_hbm, prior_hbm),
+        (trans_ref, obsmat_ref, damp_ref, weight_ref, obs_ref, prior_ref),
+        sems,
+    )
     steps, width = damp_ref.shape
     span = steps // CHUNKS
     is_first = (lax.axis_index("tm") == 0).astype(f32)
@@ -123,7 +140,9 @@
     half_ref[...] = jnp.where(upper, whole[:, half:], whole[:, :half])
 
 
-def plane_kernel(chip_ref, mine_ref, other_ref, plane_ref, before_ref, all_ref, prefix_ref):
+def plane_kernel(
+    chip_ref, mine_ref, other_ref, _, plane_ref, before_ref, leave_ref, all_ref, prefix_ref
+):
     me = lax.axis_index("tm")
     upper = me % 2 == 1
     place = (me // 2) % 4
@@ -139,7 +158,21 @@
         prefix_ref[position] = running
         running = compose(running, all_ref[position])
     plane_ref[...] = running
+    leave_ref[...] = running[chip_ref.shape[1] :]
     before_ref[...] = prefix_ref[place]
+
+
+def as_column(rows):
+    return rows.T[:, 0:1]
+
+
+def hop_kernel(plane_ref, came_ref, enter_ref, leave_ref, next_ref, *, hop):
+    width = plane_ref.shape[1]
+    here = lax.axis_index("tm") // PLANE == hop
+    enter = jnp.where(here, came_ref[...], enter_ref[...])
+    next_ref[...] = enter
+    moved = jnp.sum(plane_ref[:width] * as_column(enter), axis=0, keepdims=True)
+    leave_ref[...] = moved + plane_ref[width:]
 
 
 def entry_kernel(before_ref, other_ref, chunk_ref, entry_ref):
@@ -152,7 +185,8 @@
         entry_ref[chunk] = compose(start, chunk_ref[chunk - 1])
 
 
-def power_kernel(trans_ref, gain_ref, mix_ref, high_ref, low_ref):
+def power_kernel(trans_hbm, gain_hbm, _, mix_ref, high_ref, low_ref, trans_ref, gain_ref, sems):
+    fetch((trans_hbm, gain_hbm), (trans_ref, gain_ref), sems)
     gain_t = gain_ref[...].T
     mix_high, mix_low = split(exact(trans_ref[...].T, gain_t))
     mix_ref[...] = stack_right(mix_high, mix_low)
@@ -176,17 +210,18 @@
 
 
 def filter_kernel(
-    enter_ref, entry_ref, path_ref, mix_ref, high_ref, low_ref,
-    filtered_ref, local_ref, *, levels
+    came_ref, enter_ref, entry_ref, path_ref, mix_ref, high_ref, low_ref,
+    filtered_ref, local_ref, *, levels, hop
 ):
     steps, _, width = path_ref.shape
     span = steps // CHUNKS
     is_final = lax.axis_index("tm") == lax.axis_size("tm") - 1
-    column = jnp.broadcast_to(enter_ref[0:1], (PAD, width)).T[:, 0:1]
+    here = lax.axis_index("tm") // PLANE == hop
+    column = as_column(jnp.where(here, came_ref[...], enter_ref[...]))
     for chunk in range(CHUNKS):
         entry = entry_ref[chunk]
         start = jnp.sum(entry[:width] * column, axis=0, keepdims=True) + entry[width : width + 1]
-        begin = jnp.broadcast_to(start, (PAD, width)).T[:, 0:1]
+        begin = as_column(jnp.broadcast_to(start, (PAD, width)))
         for step in range(chunk * span, (chunk + 1) * span):
             path = path_ref[step, :width]
             filtered_ref[step : step + 1] = (
@@ -214,10 +249,12 @@
     out_ref[...] = local_ref[...] + suffix_scan(rows, high_ref, low_ref, 0, levels)
 
 
-def call(kernel, outs, scratch=(), flops=0, limit=16):
+def call(kernel, outs, scratch=(), flops=0, limit=8, spaces=None):
+    extra = {} if spaces is None else {"in_specs": [pl.BlockSpec(memory_space=s) for s in spaces]}
     return pl.pallas_call(
         kernel,
         out_shape=outs,
+        **extra,
         scratch_shapes=scratch,
         compiler_params=pltpu.CompilerParams(vmem_limit_bytes=limit << 20),
         cost_estimate=pl.CostEstimate(flops=flops, bytes_accessed=1 << 20, transcendentals=0),
@@ -250,11 +287,28 @@
             pltpu.VMEM((steps, width), f32),
             pltpu.VMEM((steps, width), f32),
             pltpu.VMEM((2, width, width), f32),
+            pltpu.VMEM(observations.shape, f32),
+            pltpu.VMEM(obs_weights.shape, f32),
+            pltpu.VMEM(damping.shape, f32),
+            pltpu.VMEM(transition.shape, f32),
+            pltpu.VMEM(obs_matrix.shape, f32),
+            pltpu.VMEM((1, width), f32),
+            pltpu.SemaphoreType.DMA((6,)),
         ),
         flops=130 * cube,
-        limit=36,
+        limit=32,
+        spaces=[pltpu.HBM] * 6,
     )(observations, obs_weights, damping, transition, obs_matrix, prior_mean[None, :])
 
+    partner = lax.ppermute(total, "tm", swap(count, 1))
+    chip, half = call(
+        pair_kernel, (struct(rows, width), struct(rows, width // 2)), flops=3 * cube
+    )(total, partner)
+
+    halves = jnp.stack(
+        [lax.ppermute(half, "tm", swap(count, 2 * distance)) for distance in range(1, 4)]
+    )
+    other_halves = lax.ppermute(halves, "tm", swap(count, 1))
     power_count = levels + max((count - 1).bit_length(), 1)
     mix, power_high, power_low = call(
         power_kernel,
@@ -263,43 +317,46 @@
             struct(power_count, width, width, dtype=bf16),
             struct(power_count, width, width, dtype=bf16),
         ),
+        (
+            pltpu.VMEM(transition.shape, f32),
+            pltpu.VMEM(transition.shape, f32),
+            pltpu.SemaphoreType.DMA((2,)),
+        ),
         flops=60 * cube,
-    )(transition, smoother_gain)
-
-    partner = lax.ppermute(total, "tm", swap(count, 1))
-    chip, half = call(
-        pair_kernel, (struct(rows, width), struct(rows, width // 2)), flops=3 * cube
-    )(total, partner)
-
-    halves = jnp.stack(
-        [lax.ppermute(half, "tm", swap(count, 2 * distance)) for distance in range(1, 4)]
-    )
-    other_halves = lax.ppermute(halves, "tm", swap(count, 1))
-    plane, before = call(
+        spaces=[pltpu.HBM, pltpu.HBM, pl.ANY],
+    )(transition, smoother_gain, half)
+    plane, before, leave = call(
         plane_kernel,
-        (struct(rows, width), struct(rows, width)),
+        (struct(rows, width), struct(rows, width), struct(PAD, width)),
         (pltpu.VMEM((4, rows, width), f32), pltpu.VMEM((4, rows, width), f32)),
         flops=9 * cube,
-    )(chip, halves, other_halves)
+        spaces=[pltpu.VMEM] * 3 + [pl.ANY],
+    )(chip, halves, other_halves, mix)
     entry = call(entry_kernel, struct(CHUNKS, rows, width), flops=12 * cube)(
         before, partner, chunk_maps
     )
 
-    group = lax.axis_index("tm") // PLANE
-    enter = jnp.zeros((1, width), f32)
-    for hop in range(count // PLANE - 1):
-        leave = jnp.sum(plane[:width] * enter.T, axis=0, keepdims=True) + plane[width : width + 1]
+    enter = jnp.zeros((PAD, width), f32)
+    came = leave
+    hops = count // PLANE - 1
+    for hop in range(hops):
+        if hop > 0:
+            leave, enter = call(
+                functools.partial(hop_kernel, hop=hop),
+                (struct(PAD, width), struct(PAD, width)),
+                flops=cube // 64,
+                limit=2,
+            )(plane, came, enter)
         low, high = hop * PLANE, (hop + 1) * PLANE
         pairs = [(low + i, high + i) for i in range(PLANE)]
         pairs = pairs + [(b, a) for a, b in pairs]
-        enter = jnp.where(group == hop + 1, lax.ppermute(leave, "tm", pairs), enter)
+        came = lax.ppermute(leave, "tm", pairs)
 
     filtered, local = call(
-        functools.partial(filter_kernel, levels=levels),
+        functools.partial(filter_kernel, levels=levels, hop=hops),
         (struct(steps, width), struct(steps, width)),
         flops=20 * cube,
-        limit=32,
-    )(enter, entry, path, mix, power_high, power_low)
+    )(came, enter, entry, path, mix, power_high, power_low)
 
     sent = jnp.broadcast_to(local[0:1], (count, width))
     offsets = lax.all_to_all(sent, "tm", 0, 0, tiled=True)

time: 80.1 us -> 67.9 us (0.85)
  local copies, waits for them, and re-layouts: 17.1 us -> 4.69 us
  blocking collectives: 15.5 us -> 18.2 us
  waiting for transfers between devices: 11.6 us -> 9.94 us
  other arithmetic: 0.94 us -> 0.04 us
    unnamed x31 -> x15, local copies, waits for them, and re-layouts: 17.1 us -> 4.66 us
    all_to_all x1, blocking collectives: 15.5 us -> 18.2 us  [per_device(): offsets = lax.all_to_all(sent, 'tm', 0, 0, tiled=True)]
    ppermute x1, waiting for transfers between devices: 1.72 us -> 0.01 us  [per_device(): other_halves = lax.ppermute(halves, 'tm', swap(count, 1))]
    pallas_call x2 -> x4, Pallas kernels: 3.73 us -> 4.26 us  [the longest x1 2.8 us: per_device(): call(functools.partial(filter_kernel, levels=levels, hop=hops), (struct(s...]
  transfers between devices with their start and end apart: 8 -> 8, of which waited for: 5 -> 4; matrix products, arithmetic and copies ran while one was open for 0% -> 0% of each run, Pallas kernels for 7% -> 9%
where the time goes in v2:
time: 67.9 us; the launch traced here: 67.5 us
  Pallas kernels  23.9 us (35%)
  blocking collectives  18.2 us (27%)
  waiting for transfers between devices  9.94 us (15%)
  starting transfers between devices  9.89 us (15%)
  local copies, waits for them, and re-layouts  4.69 us (7%)
  between operations  0.77 us (1%)
    all_to_all x1, blocking collectives, per_device(): offsets = lax.all_to_all(sent, 'tm', 0, 0, tiled=True)  18.2 us
    pallas_call x1, Pallas kernels, per_device(): call(local_kernel, (struct(steps, rows, width), struct(CHUNKS - 1, rows,...  10.9 us
    ppermute x3, waiting for transfers between devices, per_device(): lax.ppermute(half, 'tm', swap(count, 2 * distance))  6.7 us
    pallas_call x1, Pallas kernels, per_device(): call(power_kernel, (struct(3 * width, width, dtype=bf16), struct(power_co...  4.96 us
    ppermute x3, starting transfers between devices, per_device(): came = lax.ppermute(leave, 'tm', pairs)  4.81 us
    unnamed x15, local copies, waits for them, and re-layouts  4.66 us
    ppermute x3, starting transfers between devices, per_device(): lax.ppermute(half, 'tm', swap(count, 2 * distance))  4.46 us
    pallas_call x1, Pallas kernels, per_device(): call(functools.partial(filter_kernel, levels=levels, hop=hops), (struct(s...  2.8 us
  transfers between devices with their start and end apart: 8, of which 4 were waited for; matrix products, arithmetic and copies ran while one was open for 0% of the time, Pallas kernels for 9%

profile of v2, /device:TPU:0, one launch (start us, length us, event | category | flops | bytes accessed | tf_op | source)
XLA Modules:
  0.0 67.5 jit_solution(9727033861301734359)
XLA Ops:
  0.6 0.9 %copy-done = f32[256,256]{1,0:T(8,128)S(1)} copy-done((f32[256,256]{1,0:T(8,128)S(1)}, f32[256,256]{1,0:T(8,128)}, u32[]{:S(2)}) %copy-start) | copy-done | bytes 262168
  1.6 0.8 %copy-done.2 = f32[64,256]{1,0:T(8,128)S(1)} copy-done((f32[64,256]{1,0:T(8,128)S(1)}, f32[64,256]{1,0:T(8,128)}, u32[]{:S(2)}) %copy-start.2) | copy-done | bytes 65560
  2.4 0.8 %copy-done.3 = f32[32,256]{1,0:T(8,128)S(1)} copy-done((f32[32,256]{1,0:T(8,128)S(1)}, f32[32,256]{1,0:T(8,128)}, u32[]{:S(2)}) %copy-start.3) | copy-done | bytes 32792
  3.2 0.7 %copy-done.4 = f32[32,64]{1,0:T(8,128)S(1)} copy-done((f32[32,64]{1,0:T(8,128)S(1)}, f32[32,64]{1,0:T(8,128)}, u32[]{:S(2)}) %copy-start.4) | copy-done | bytes 8216
  3.9 0.7 %copy-done.5 = f32[32,64]{1,0:T(8,128)S(1)} copy-done((f32[32,64]{1,0:T(8,128)S(1)}, f32[32,64]{1,0:T(8,128)}, u32[]{:S(2)}) %copy-start.5) | copy-done | bytes 8216
  4.6 0.7 %copy-done.6 = f32[256]{0:T(256)S(1)} copy-done((f32[256]{0:T(256)S(1)}, f32[256]{0:T(256)}, u32[]{:S(2)}) %copy-start.6) | copy-done | bytes 1048
  5.3 10.9 %shard_map.86 = (f32[32,264,256]{2,1,0:T(8,128)S(1)}, f32[3,264,256]{2,1,0:T(8,128)S(1)}, f32[264,256]{1,0:T(8,128)S(1)}) custom-call(f32[32,64]{1,0:T(8,128)S(1)} %copy-done.4, f32[32,64]{1,0:T(8,128)S(1)} %copy-done.5, f32[32,256]{1,0:T(8,128)S(1)} %copy-done.3, f32[256,256]{1,0:T(8,128)S(1)} %copy-done, f32[64,256]{1,0:T(8,128)S(1)} %copy-done.2, ...), custom_call_target="tpu_custom_call" | custom-call | flops 4362076160 | bytes 1048576 | tf_op jit(solution)/shard_map/pallas_call | solution.py:280
  16.2 0.0 copy-start.1
  16.2 0.6 collective-permute-start
  16.7 1.2 %collective-permute-done.other_ref = f32[264,256]{1,0:T(8,128)S(1)} collective-permute-done((f32[264,256]{1,0:T(8,128)S(1)}, f32[264,256]{1,0:T(8,128)S(1)}, u32[]{:S(2)}, u32[]{:S(2)}) %collective-permute-start) | collective-permute-done | bytes 270368 | tf_op jit(solution)/shard_map/ppermute | solution.py:303
  17.9 0.3 shard_map.87
  18.2 2.9 %collective-permute-start.1 = (f32[264,128]{1,0:T(8,128)S(1)}, f32[264,128]{1,0:T(8,128)S(1)}, u32[]{:S(2)}, u32[]{:S(2)}) collective-permute-start(f32[264,128]{1,0:T(8,128)S(1)} %get-tuple-element.21._), channel_id=1, source_target_pairs={{0,2},{1,3},{2,0},{3,1},{4,6},{5,7},{6,4},{7,5},{8,10},{9,11},{10,... | collective-permute-start | bytes 405512 | tf_op jit(solution)/shard_map/ppermute | solution.py:309
  21.1 1.5 %collective-permute-start.2 = (f32[264,128]{1,0:T(8,128)S(1)}, f32[264,128]{1,0:T(8,128)S(1)}, u32[]{:S(2)}, u32[]{:S(2)}) collective-permute-start(f32[264,128]{1,0:T(8,128)S(1)} %get-tuple-element.21._), channel_id=1, source_target_pairs={{0,4},{1,5},{2,6},{3,7},{4,0},{5,1},{6,2},{7,3},{8,12},{9,13},{10,... | collective-permute-start | bytes 405512 | tf_op jit(solution)/shard_map/ppermute | solution.py:309
  22.6 0.0 collective-permute-start.3
  22.7 2.6 %collective-permute-done.1 = f32[264,128]{1,0:T(8,128)S(1)} collective-permute-done((f32[264,128]{1,0:T(8,128)S(1)}, f32[264,128]{1,0:T(8,128)S(1)}, u32[]{:S(2)}, u32[]{:S(2)}) %collective-permute-start.1) | collective-permute-done | bytes 135200 | tf_op jit(solution)/shard_map/ppermute | solution.py:309
  25.3 4.1 %collective-permute-done.2 = f32[264,128]{1,0:T(8,128)S(1)} collective-permute-done((f32[264,128]{1,0:T(8,128)S(1)}, f32[264,128]{1,0:T(8,128)S(1)}, u32[]{:S(2)}, u32[]{:S(2)}) %collective-permute-start.2) | collective-permute-done | bytes 135200 | tf_op jit(solution)/shard_map/ppermute | solution.py:309
  29.4 0.1 collective-permute-start.4
  29.5 5.0 %shard_map.88 = (bf16[768,256]{1,0:T(8,128)(2,1)S(1)}, bf16[10,256,256]{2,1,0:T(8,128)(2,1)S(1)}, bf16[10,256,256]{2,1,0:T(8,128)(2,1)S(1)}) custom-call(f32[256,256]{1,0:T(8,128)S(1)} %copy-done, f32[256,256]{1,0:T(8,128)S(1)} %copy-done.1, f32[264,128]{1,0:T(8,128)S(1)} %get-tuple-element.21._), custom_call_target="tpu_custom_call" | custom-call | flops 2013265920 | bytes 1048576 | tf_op jit(solution)/shard_map/pallas_call | solution.py:313
  34.5 0.0 collective-permute-done.4.other_ref
  34.5 0.9 %shard_map.89 = (f32[264,256]{1,0:T(8,128)S(1)}, f32[264,256]{1,0:T(8,128)S(1)}, f32[8,256]{1,0:T(8,128)S(1)}) custom-call(f32[264,256]{1,0:T(8,128)S(1)} %get-tuple-element.20.chip_ref, f32[3,264,128]{2,1,0:T(8,128)S(1)} %pad_maximum_fusion.mine_ref, f32[3,264,128]{2,1,0:T(8,128)S(1)} %collective-permute-done.4.other_ref, ...), custom_call_target="tpu_custom_call" | custom-call | flops 301989888 | bytes 1048576 | tf_op jit(solution)/shard_map/pallas_call | solution.py:328
  35.4 3.5 %collective-permute-start.5 = (f32[8,256]{1,0:T(8,128)S(1)}, f32[8,256]{1,0:T(8,128)S(1)}, u32[]{:S(2)}, u32[]{:S(2)}) collective-permute-start(f32[8,256]{1,0:T(8,128)S(1)} %get-tuple-element.24), channel_id=1, source_target_pairs={{0,8},{1,9},{2,10},{3,11},{4,12},{5,13},{6,14},{7,15},{8,0},{9,1},... | collective-permute-start | bytes 24584 | tf_op jit(solution)/shard_map/ppermute | solution.py:353
  38.9 2.1 %collective-permute-done.5.came_ref = f32[8,256]{1,0:T(8,128)S(1)} collective-permute-done((f32[8,256]{1,0:T(8,128)S(1)}, f32[8,256]{1,0:T(8,128)S(1)}, u32[]{:S(2)}, u32[]{:S(2)}) %collective-permute-start.5) | collective-permute-done | bytes 8224 | tf_op jit(solution)/shard_map/ppermute | solution.py:353
  41.0 0.3 shard_map.90
  41.2 0.7 collective-permute-start.6
  41.9 0.0 collective-permute-done.6.came_ref
  41.9 0.3 shard_map.91
  42.2 0.7 collective-permute-start.7
  42.9 0.9 %shard_map.92.entry_ref = f32[4,264,256]{2,1,0:T(8,128)S(1)} custom-call(f32[264,256]{1,0:T(8,128)S(1)} %get-tuple-element.29.before_ref, f32[264,256]{1,0:T(8,128)S(1)} %collective-permute-done.other_ref, f32[3,264,256]{2,1,0:T(8,128)S(1)} %get-tuple-element.30.chunk_ref), custom_call_target="tpu_custom_call" | custom-call | flops 402653184 | bytes 1048576 | tf_op jit(solution)/shard_map/pallas_call | solution.py:335
  43.7 0.0 collective-permute-done.7.came_ref
  43.8 2.8 %shard_map.93 = (f32[32,256]{1,0:T(8,128)}, f32[32,256]{1,0:T(8,128)S(1)}) custom-call(f32[8,256]{1,0:T(8,128)S(1)} %collective-permute-done.7.came_ref, f32[8,256]{1,0:T(8,128)S(1)} %get-tuple-element.28.enter_ref, f32[4,264,256]{2,1,0:T(8,128)S(1)} %shard_map.92.entry_ref, f32[32,264,256]{2,1,0:T(8,128)S(1)} %get-tuple-element.31.path_ref, ...), custom_call_target="tpu_custom_call" | custom-call | flops 671088640 | bytes 1048576 | tf_op jit(solution)/shard_map/pallas_call | solution.py:355
  46.6 18.2 %all_to_all.8 = f32[32,1,256]{2,1,0:T(1,128)S(1)} all-to-all(f32[32,1,256]{2,1,0:T(1,128)S(1)} %broadcast_in_dim.13), channel_id=1, replica_groups=mesh['tm'=32,'panel'=1] {'tm'}, dimensions={0} | all-to-all | bytes 65536 | tf_op jit(solution)/shard_map/all_to_all | solution.py:362
  64.8 2.7 %shard_map.94 = f32[32,256]{1,0:T(8,128)} custom-call(f32[32,256]{1,0:T(8,128)S(1)} %bitcast.8, f32[32,256]{1,0:T(8,128)S(1)} %get-tuple-element.35.local_ref, bf16[10,256,256]{2,1,0:T(8,128)(2,1)S(1)} %get-tuple-element.32.high_ref, bf16[10,256,256]{2,1,0:T(8,128)(2,1)S(1)} %get-tuple-element.33.low_ref), custom_call_target="tpu_custom_call" | custom-call | flops 671088640 | bytes 1048576 | tf_op jit(solution)/shard_map/pallas_call | solution.py:363
  (13 shorter events, 0.1 us)
Async XLA Ops:
  0.6 1.0 %copy-start = (f32[256,256]{1,0:T(8,128)S(1)}, f32[256,256]{1,0:T(8,128)}, u32[]{:S(2)}) copy-start(f32[256,256]{1,0:T(8,128)} %trans_hbm.3) | copy-start | bytes 786436
  1.6 0.8 %copy-start.2 = (f32[64,256]{1,0:T(8,128)S(1)}, f32[64,256]{1,0:T(8,128)}, u32[]{:S(2)}) copy-start(f32[64,256]{1,0:T(8,128)} %obsmat_hbm.1) | copy-start | bytes 196612
  2.4 0.8 %copy-start.3 = (f32[32,256]{1,0:T(8,128)S(1)}, f32[32,256]{1,0:T(8,128)}, u32[]{:S(2)}) copy-start(f32[32,256]{1,0:T(8,128)} %damp_hbm.1) | copy-start | bytes 98308
  3.2 0.7 %copy-start.4 = (f32[32,64]{1,0:T(8,128)S(1)}, f32[32,64]{1,0:T(8,128)}, u32[]{:S(2)}) copy-start(f32[32,64]{1,0:T(8,128)} %obs_hbm.1) | copy-start | bytes 24580
  3.9 0.7 %copy-start.5 = (f32[32,64]{1,0:T(8,128)S(1)}, f32[32,64]{1,0:T(8,128)}, u32[]{:S(2)}) copy-start(f32[32,64]{1,0:T(8,128)} %weight_hbm.1) | copy-start | bytes 24580
  4.6 0.7 %copy-start.6 = (f32[256]{0:T(256)S(1)}, f32[256]{0:T(256)}, u32[]{:S(2)}) copy-start(f32[256]{0:T(256)} %param.13) | copy-start | bytes 3076
  16.2 13.3 %copy-start.1 = (f32[256,256]{1,0:T(8,128)S(1)}, f32[256,256]{1,0:T(8,128)}, u32[]{:S(2)}) copy-start(f32[256,256]{1,0:T(8,128)} %gain_hbm.1) | copy-start | bytes 786436
  16.2 1.7 %collective-permute-start = (f32[264,256]{1,0:T(8,128)S(1)}, f32[264,256]{1,0:T(8,128)S(1)}, u32[]{:S(2)}, u32[]{:S(2)}) collective-permute-start(f32[264,256]{1,0:T(8,128)S(1)} %get-tuple-element.19.mine_ref), channel_id=1, source_target_pairs={{0,1},{1,0},{2,3},{3,2},{4,5},{5,4},{6,7},{7,6},{8,9},{9,8},{10,11... | collective-permute-start | bytes 811016 | tf_op jit(solution)/shard_map/ppermute | solution.py:303
  18.2 7.1 %collective-permute-start.1 = (f32[264,128]{1,0:T(8,128)S(1)}, f32[264,128]{1,0:T(8,128)S(1)}, u32[]{:S(2)}, u32[]{:S(2)}) collective-permute-start(f32[264,128]{1,0:T(8,128)S(1)} %get-tuple-element.21._), channel_id=1, source_target_pairs={{0,2},{1,3},{2,0},{3,1},{4,6},{5,7},{6,4},{7,5},{8,10},{9,11},{10,... | collective-permute-start | bytes 405512 | tf_op jit(solution)/shard_map/ppermute | solution.py:309
  21.1 8.2 %collective-permute-start.2 = (f32[264,128]{1,0:T(8,128)S(1)}, f32[264,128]{1,0:T(8,128)S(1)}, u32[]{:S(2)}, u32[]{:S(2)}) collective-permute-start(f32[264,128]{1,0:T(8,128)S(1)} %get-tuple-element.21._), channel_id=1, source_target_pairs={{0,4},{1,5},{2,6},{3,7},{4,0},{5,1},{6,2},{7,3},{8,12},{9,13},{10,... | collective-permute-start | bytes 405512 | tf_op jit(solution)/shard_map/ppermute | solution.py:309
  22.6 6.7 %collective-permute-start.3 = (f32[264,128]{1,0:T(8,128)S(1)}, f32[264,128]{1,0:T(8,128)S(1)}, u32[]{:S(2)}, u32[]{:S(2)}) collective-permute-start(f32[264,128]{1,0:T(8,128)S(1)} %get-tuple-element.21._), channel_id=1, source_target_pairs={{0,6},{1,7},{2,4},{3,5},{4,2},{5,3},{6,0},{7,1},{8,14},{9,15},{10,... | collective-permute-start | bytes 405512 | tf_op jit(solution)/shard_map/ppermute | solution.py:309
  29.4 5.1 %collective-permute-start.4 = (f32[3,264,128]{2,1,0:T(8,128)S(1)}, f32[3,264,128]{2,1,0:T(8,128)S(1)}, u32[]{:S(2)}, u32[]{:S(2)}) collective-permute-start(f32[3,264,128]{2,1,0:T(8,128)S(1)} %pad_maximum_fusion.mine_ref), channel_id=1, source_target_pairs={{0,1},{1,0},{2,3},{3,2},{4,5},{5,4},{6,7},{7,6},{8,9},{9,8},{10,11... | collective-permute-start | bytes 1216520 | tf_op jit(solution)/shard_map/ppermute | solution.py:311
  35.4 5.5 %collective-permute-start.5 = (f32[8,256]{1,0:T(8,128)S(1)}, f32[8,256]{1,0:T(8,128)S(1)}, u32[]{:S(2)}, u32[]{:S(2)}) collective-permute-start(f32[8,256]{1,0:T(8,128)S(1)} %get-tuple-element.24), channel_id=1, source_target_pairs={{0,8},{1,9},{2,10},{3,11},{4,12},{5,13},{6,14},{7,15},{8,0},{9,1},... | collective-permute-start | bytes 24584 | tf_op jit(solution)/shard_map/ppermute | solution.py:353
  41.2 0.7 collective-permute-start.6
  42.2 1.6 %collective-permute-start.7 = (f32[8,256]{1,0:T(8,128)S(1)}, f32[8,256]{1,0:T(8,128)S(1)}, u32[]{:S(2)}, u32[]{:S(2)}) collective-permute-start(f32[8,256]{1,0:T(8,128)S(1)} %get-tuple-element.27), channel_id=1, source_target_pairs={{16,24},{17,25},{18,26},{19,27},{20,28},{21,29},{22,30},{23,31},{2... | collective-permute-start | bytes 24584 | tf_op jit(solution)/shard_map/ppermute | solution.py:353

commit v3 on v2

--- a/solution.py
+++ b/solution.py
@@ -44,6 +44,10 @@
     rows = lax.broadcasted_iota(jnp.int32, (width + PAD, width), 0)
     cols = lax.broadcasted_iota(jnp.int32, (width + PAD, width), 1)
     return (rows == cols).astype(f32)
+
+
+def as_column(rows):
+    return rows.T[:, 0:1]
 
 
 def fetch(sources, targets, sems):
@@ -60,7 +64,7 @@
 def local_kernel(
     obs_hbm, weight_hbm, damp_hbm, trans_hbm, obsmat_hbm, prior_hbm,
     path_ref, chunk_ref, total_ref,
-    high_ref, low_ref, state_ref, offset_ref, wide_ref, base_ref,
+    high_even, low_even, high_odd, low_odd, state_ref, offset_ref, wide_ref, base_ref,
     obs_ref, weight_ref, damp_ref, trans_ref, obsmat_ref, prior_ref, sems,
 ):
     fetch(
@@ -92,42 +96,59 @@
     offsets = offsets + jnp.where(step_ids == 0, is_first, 0.0) * begun[0:1]
     offset_ref[...] = offsets
 
-    def make(step, carry):
-        scaled = base_ref[1] * wide_ref[pl.ds(step, 1), :]
+    half = width // 2
+
+    def make(time):
+        scaled = base_ref[1] * wide_ref[pl.ds(time, 1), :]
         high, low = split(scaled)
-        half = width // 2
         pieces = jnp.concatenate([high[:, :half], low[:, half:]], axis=1)
-        moved = base_ref[0] - jnp.dot(pieces, obs_stack, preferred_element_type=f32)
-        high, low = split(moved)
-        high_ref[step] = high
-        low_ref[step] = low
-        return carry
-
-    lax.fori_loop(0, steps, make, 0, unroll=2)
-
-    identity = eye_map(width)
+        return base_ref[0] - jnp.dot(pieces, obs_stack, preferred_element_type=f32)
+
     for chunk in range(CHUNKS):
-        state_ref[chunk] = identity * (1.0 - is_first) if chunk == 0 else identity
-
-    def advance(step, carry):
+        time = chunk * span
+        damp = as_column(jnp.broadcast_to(damp_ref[time : time + 1], (PAD, width)))
+        begin = make(time) * damp
+        if chunk == 0:
+            begin = begin * (1.0 - is_first)
+        moved = jnp.concatenate(
+            [begin, jnp.broadcast_to(offset_ref[time : time + 1], (PAD, width))], axis=0
+        )
+        state_ref[chunk] = moved
+        path_ref[time] = moved
+
+    def ready(step, chunk, slot):
+        slot[0][chunk], slot[1][chunk] = split(make(chunk * span + step))
+
+    def advance(step, slot, following):
         for chunk in range(CHUNKS):
             time = chunk * span + step
             damped = state_ref[chunk] * damp_ref[pl.ds(time, 1), :]
-            moved = dot_split(damped, stack_right(high_ref[time], low_ref[time]))
+            moved = dot_split(damped, stack_right(slot[0][chunk], slot[1][chunk]))
             moved = jnp.concatenate(
                 [moved[:width], moved[width:] + offset_ref[pl.ds(time, 1), :]], axis=0
             )
             state_ref[chunk] = moved
             path_ref[time] = moved
+            if following is not None:
+                ready(step + 1, chunk, following)
+
+    even, odd = (high_even, low_even), (high_odd, low_odd)
+    for chunk in range(CHUNKS):
+        ready(1, chunk, odd)
+
+    def two(index, carry):
+        advance(2 * index + 1, odd, even)
+        advance(2 * index + 2, even, odd)
         return carry
 
-    lax.fori_loop(0, span, advance, 0)
-
-    entering = state_ref[0]
-    for chunk in range(1, CHUNKS):
-        chunk_ref[chunk - 1] = entering
-        entering = compose(entering, state_ref[chunk])
-    total_ref[...] = entering
+    lax.fori_loop(0, span // 2 - 1, two, 0)
+    advance(span - 1, odd, None)
+
+    first = compose(state_ref[0], state_ref[1])
+    chunk_ref[0] = state_ref[0]
+    chunk_ref[1] = first
+    chunk_ref[2] = state_ref[2]
+    total_ref[...] = compose(first, compose(state_ref[2], state_ref[3]))
 
 
 def pair_kernel(mine_ref, other_ref, chip_ref, half_ref):
@@ -148,10 +169,14 @@
     place = (me // 2) % 4
     half = chip_ref.shape[1] // 2
     all_ref[place] = chip_ref[...]
-    for distance in range(1, 4):
-        mine, other = mine_ref[distance - 1], other_ref[distance - 1]
-        all_ref[place ^ distance, :, :half] = jnp.where(upper, other, mine)
-        all_ref[place ^ distance, :, half:] = jnp.where(upper, mine, other)
+    for part in range(2):
+        mine, other = mine_ref[part], other_ref[part]
+        columns = pl.ds(part * half, half)
+        all_ref[place ^ 1, :, columns] = jnp.where(upper, other, mine)
+        all_ref[place ^ 2, :, columns] = jnp.where(upper, mine, other)
+    mine, other = mine_ref[2], other_ref[2]
+    all_ref[place ^ 3, :, :half] = jnp.where(upper, other, mine)
+    all_ref[place ^ 3, :, half:] = jnp.where(upper, mine, other)
     running = all_ref[0]
     prefix_ref[0] = eye_map(chip_ref.shape[1])
     for position in range(1, 4):
@@ -162,10 +187,6 @@
     before_ref[...] = prefix_ref[place]
 
 
-def as_column(rows):
-    return rows.T[:, 0:1]
-
-
 def hop_kernel(plane_ref, came_ref, enter_ref, leave_ref, next_ref, *, hop):
     width = plane_ref.shape[1]
     here = lax.axis_index("tm") // PLANE == hop
@@ -181,8 +202,9 @@
     joined = compose(before, other_ref[...])
     start = jnp.where(upper, joined, before)
     entry_ref[0] = start
-    for chunk in range(1, CHUNKS):
-        entry_ref[chunk] = compose(start, chunk_ref[chunk - 1])
+    entry_ref[1] = compose(start, chunk_ref[0])
+    entry_ref[2] = compose(start, chunk_ref[1])
+    entry_ref[3] = compose(entry_ref[2], chunk_ref[2])
 
 
 def power_kernel(trans_hbm, gain_hbm, _, mix_ref, high_ref, low_ref, trans_ref, gain_ref, sems):
@@ -268,6 +290,13 @@
 def per_device(
     observations, obs_weights, damping, transition, obs_matrix, smoother_gain, prior_mean
 ):
+    observations, obs_weights, damping, transition, obs_matrix, smoother_gain, prior_row = (
+        pltpu.with_memory_space_constraint(value, pltpu.HBM)
+        for value in (
+            observations, obs_weights, damping, transition, obs_matrix, smoother_gain,
+            prior_mean[None, :],
+        )
+    )
     steps, width = damping.shape
     count = lax.axis_size("tm")
     rows = width + PAD
@@ -281,8 +310,10 @@
         local_kernel,
         (struct(steps, rows, width), struct(CHUNKS - 1, rows, width), struct(rows, width)),
         (
-            pltpu.VMEM((steps, width, width), bf16),
-            pltpu.VMEM((steps, width, width), bf16),
+            pltpu.VMEM((CHUNKS, width, width), bf16),
+            pltpu.VMEM((CHUNKS, width, width), bf16),
+            pltpu.VMEM((CHUNKS, width, width), bf16),
+            pltpu.VMEM((CHUNKS, width, width), bf16),
             pltpu.VMEM((CHUNKS, rows, width), f32),
             pltpu.VMEM((steps, width), f32),
             pltpu.VMEM((steps, width), f32),
@@ -298,17 +329,17 @@
         flops=130 * cube,
         limit=32,
         spaces=[pltpu.HBM] * 6,
-    )(observations, obs_weights, damping, transition, obs_matrix, prior_mean[None, :])
+    )(observations, obs_weights, damping, transition, obs_matrix, prior_row)
 
     partner = lax.ppermute(total, "tm", swap(count, 1))
     chip, half = call(
         pair_kernel, (struct(rows, width), struct(rows, width // 2)), flops=3 * cube
     )(total, partner)
 
-    halves = jnp.stack(
-        [lax.ppermute(half, "tm", swap(count, 2 * distance)) for distance in range(1, 4)]
-    )
-    other_halves = lax.ppermute(halves, "tm", swap(count, 1))
+    straight = [(index, index ^ (4 if index % 2 else 2)) for index in range(count)]
+    diagonal = lax.ppermute(half, "tm", swap(count, 6))
+    whole = lax.ppermute(chip, "tm", straight)
+    middle = width // 2
     power_count = levels + max((count - 1).bit_length(), 1)
     mix, power_high, power_low = call(
         power_kernel,
@@ -325,6 +356,9 @@
         flops=60 * cube,
         spaces=[pltpu.HBM, pltpu.HBM, pl.ANY],
     )(transition, smoother_gain, half)
+    whole, diagonal, mix = lax.optimization_barrier((whole, diagonal, mix))
+    halves = jnp.stack([whole[:, :middle], whole[:, middle:], diagonal])
+    other_halves = lax.ppermute(halves, "tm", swap(count, 1))
     plane, before, leave = call(
         plane_kernel,
         (struct(rows, width), struct(rows, width), struct(PAD, width)),

time: 67.9 us -> 57.4 us (0.85)
  local copies, waits for them, and re-layouts: 4.69 us -> 0.05 us
  waiting for transfers between devices: 9.94 us -> 6.33 us
  Pallas kernels: 23.9 us -> 22 us
    ppermute x3 -> x2, waiting for transfers between devices: 6.7 us -> 1.38 us  [the longest x1 1.37 us: per_device(): diagonal = lax.ppermute(half, 'tm', swap(count, 6))]
    unnamed x15 -> x1, local copies, waits for them, and re-layouts: 4.66 us -> 0.01 us
    pallas_call x1, Pallas kernels: 10.9 us -> 7.97 us  [per_device(): call(local_kernel, (struct(steps, rows, width), struct(CHUNKS - 1, rows,...]
    ppermute x1, waiting for transfers between devices: 0.01 us -> 1.73 us  [per_device(): other_halves = lax.ppermute(halves, 'tm', swap(count, 1))]
    pallas_call x1, Pallas kernels: 4.96 us -> 5.95 us  [per_device(): call(power_kernel, (struct(3 * width, width, dtype=bf16), struct(power_co...]
    ppermute x3 -> x2, starting transfers between devices: 4.46 us -> 4.4 us  [the longest x1 2.91 us: per_device(): whole = lax.ppermute(chip, 'tm', straight)]
  transfers between devices with their start and end apart: 8 -> 7, of which waited for: 4 -> 4; matrix products, arithmetic and copies ran while one was open for 0% -> 0% of each run, Pallas kernels for 9% -> 12%
where the time goes in v3:
time: 57.4 us; the launch traced here: 57.2 us
  Pallas kernels  22 us (38%)
  blocking collectives  18.1 us (32%)
  starting transfers between devices  9.83 us (17%)
  waiting for transfers between devices  6.33 us (11%)
  between operations  0.74 us (1%)
    all_to_all x1, blocking collectives, per_device(): offsets = lax.all_to_all(sent, 'tm', 0, 0, tiled=True)  18.1 us
    pallas_call x1, Pallas kernels, per_device(): call(local_kernel, (struct(steps, rows, width), struct(CHUNKS - 1, rows,...  7.97 us
    pallas_call x1, Pallas kernels, per_device(): call(power_kernel, (struct(3 * width, width, dtype=bf16), struct(power_co...  5.95 us
    ppermute x3, starting transfers between devices, per_device(): came = lax.ppermute(leave, 'tm', pairs)  4.81 us
    ppermute x1, starting transfers between devices, per_device(): whole = lax.ppermute(chip, 'tm', straight)  2.91 us
    pallas_call x1, Pallas kernels, per_device(): call(functools.partial(filter_kernel, levels=levels, hop=hops), (struct(s...  2.74 us
    pallas_call x1, Pallas kernels, per_device(): call(functools.partial(smooth_kernel, levels=levels), struct(steps, width...  2.67 us
    ppermute x3, waiting for transfers between devices, per_device(): came = lax.ppermute(leave, 'tm', pairs)  2.06 us
  transfers between devices with their start and end apart: 7, of which 4 were waited for; matrix products, arithmetic and copies ran while one was open for 0% of the time, Pallas kernels for 12%

profile of v3, /device:TPU:0, one launch (start us, length us, event | category | flops | bytes accessed | tf_op | source)
XLA Modules:
  0.0 57.2 jit_solution(5125674422975226837)
XLA Ops:
  0.6 8.0 %shard_map.86 = (f32[32,264,256]{2,1,0:T(8,128)S(1)}, f32[3,264,256]{2,1,0:T(8,128)S(1)}, f32[264,256]{1,0:T(8,128)S(1)}) custom-call(f32[32,64]{1,0:T(8,128)} %obs_hbm.1, f32[32,64]{1,0:T(8,128)} %weight_hbm.1, f32[32,256]{1,0:T(8,128)} %damp_hbm.1, f32[256,256]{1,0:T(8,128)} %trans_hbm.3, f32[64,256]{1,0:T(8,128)} %obsmat_hbm.1, f32[1,256]{1,0:T(1,128)} %bitcast.13), custom_call_target="tpu_custom_call" | custom-call | flops 4362076160 | bytes 1048576 | tf_op jit(solution)/shard_map/pallas_call | solution.py:309
  8.6 0.6 collective-permute-start
  9.2 1.2 %collective-permute-done.other_ref = f32[264,256]{1,0:T(8,128)S(1)} collective-permute-done((f32[264,256]{1,0:T(8,128)S(1)}, f32[264,256]{1,0:T(8,128)S(1)}, u32[]{:S(2)}, u32[]{:S(2)}) %collective-permute-start) | collective-permute-done | bytes 270368 | tf_op jit(solution)/shard_map/ppermute | solution.py:334
  10.3 0.3 shard_map.87
  10.6 2.9 %collective-permute-start.1 = (f32[264,256]{1,0:T(8,128)S(1)}, f32[264,256]{1,0:T(8,128)S(1)}, u32[]{:S(2)}, u32[]{:S(2)}) collective-permute-start(f32[264,256]{1,0:T(8,128)S(1)} %get-tuple-element.23.chip_ref), channel_id=1, source_target_pairs={{0,2},{1,5},{2,0},{3,7},{4,6},{5,1},{6,4},{7,3},{8,10},{9,13},{10,... | collective-permute-start | bytes 811016 | tf_op jit(solution)/shard_map/ppermute | solution.py:341
  13.6 1.5 %collective-permute-start.2 = (f32[264,128]{1,0:T(8,128)S(1)}, f32[264,128]{1,0:T(8,128)S(1)}, u32[]{:S(2)}, u32[]{:S(2)}) collective-permute-start(f32[264,128]{1,0:T(8,128)S(1)} %get-tuple-element.24._), channel_id=1, source_target_pairs={{0,6},{1,7},{2,4},{3,5},{4,2},{5,3},{6,0},{7,1},{8,14},{9,15},{10,... | collective-permute-start | bytes 405512 | tf_op jit(solution)/shard_map/ppermute | solution.py:340
  15.0 5.9 %shard_map.88 = (bf16[768,256]{1,0:T(8,128)(2,1)S(1)}, bf16[10,256,256]{2,1,0:T(8,128)(2,1)S(1)}, bf16[10,256,256]{2,1,0:T(8,128)(2,1)S(1)}) custom-call(f32[256,256]{1,0:T(8,128)} %trans_hbm.3, f32[256,256]{1,0:T(8,128)} %gain_hbm.1, f32[264,128]{1,0:T(8,128)S(1)} %get-tuple-element.24._), custom_call_target="tpu_custom_call" | custom-call | flops 2013265920 | bytes 1048576 | tf_op jit(solution)/shard_map/pallas_call | solution.py:344
  21.0 1.4 %collective-permute-done.2 = f32[264,128]{1,0:T(8,128)S(1)} collective-permute-done((f32[264,128]{1,0:T(8,128)S(1)}, f32[264,128]{1,0:T(8,128)S(1)}, u32[]{:S(2)}, u32[]{:S(2)}) %collective-permute-start.2) | collective-permute-done | bytes 135200 | tf_op jit(solution)/shard_map/ppermute | solution.py:340
  22.4 0.0 collective-permute-done.1
  22.4 0.1 collective-permute-start.3
  22.5 1.7 %collective-permute-done.3.other_ref = f32[3,264,128]{2,1,0:T(8,128)S(1)} collective-permute-done((f32[3,264,128]{2,1,0:T(8,128)S(1)}, f32[3,264,128]{2,1,0:T(8,128)S(1)}, u32[]{:S(2)}, u32[]{:S(2)}) %collective-permute-start.3) | collective-permute-done | bytes 405536 | tf_op jit(solution)/shard_map/ppermute | solution.py:361
  24.3 0.9 %shard_map.89 = (f32[264,256]{1,0:T(8,128)S(1)}, f32[264,256]{1,0:T(8,128)S(1)}, f32[8,256]{1,0:T(8,128)S(1)}) custom-call(f32[264,256]{1,0:T(8,128)S(1)} %get-tuple-element.23.chip_ref, f32[3,264,128]{2,1,0:T(8,128)S(1)} %pad_maximum_fusion.mine_ref, f32[3,264,128]{2,1,0:T(8,128)S(1)} %collective-permute-done.3.other_ref, ...), custom_call_target="tpu_custom_call" | custom-call | flops 301989888 | bytes 1048576 | tf_op jit(solution)/shard_map/pallas_call | solution.py:362
  25.2 3.5 %collective-permute-start.4 = (f32[8,256]{1,0:T(8,128)S(1)}, f32[8,256]{1,0:T(8,128)S(1)}, u32[]{:S(2)}, u32[]{:S(2)}) collective-permute-start(f32[8,256]{1,0:T(8,128)S(1)} %get-tuple-element.30), channel_id=1, source_target_pairs={{0,8},{1,9},{2,10},{3,11},{4,12},{5,13},{6,14},{7,15},{8,0},{9,1},... | collective-permute-start | bytes 24584 | tf_op jit(solution)/shard_map/ppermute | solution.py:387
  28.7 2.1 %collective-permute-done.4.came_ref = f32[8,256]{1,0:T(8,128)S(1)} collective-permute-done((f32[8,256]{1,0:T(8,128)S(1)}, f32[8,256]{1,0:T(8,128)S(1)}, u32[]{:S(2)}, u32[]{:S(2)}) %collective-permute-start.4) | collective-permute-done | bytes 8224 | tf_op jit(solution)/shard_map/ppermute | solution.py:387
  30.8 0.3 shard_map.90
  31.0 0.7 %collective-permute-start.5 = (f32[8,256]{1,0:T(8,128)S(1)}, f32[8,256]{1,0:T(8,128)S(1)}, u32[]{:S(2)}, u32[]{:S(2)}) collective-permute-start(f32[8,256]{1,0:T(8,128)S(1)} %get-tuple-element.31), channel_id=1, source_target_pairs={{8,16},{9,17},{10,18},{11,19},{12,20},{13,21},{14,22},{15,23},{16,... | collective-permute-start | bytes 24584 | tf_op jit(solution)/shard_map/ppermute | solution.py:387
  31.7 0.0 collective-permute-done.5.came_ref
  31.7 0.3 shard_map.91
  32.0 0.7 %collective-permute-start.6 = (f32[8,256]{1,0:T(8,128)S(1)}, f32[8,256]{1,0:T(8,128)S(1)}, u32[]{:S(2)}, u32[]{:S(2)}) collective-permute-start(f32[8,256]{1,0:T(8,128)S(1)} %get-tuple-element.33), channel_id=1, source_target_pairs={{16,24},{17,25},{18,26},{19,27},{20,28},{21,29},{22,30},{23,31},{2... | collective-permute-start | bytes 24584 | tf_op jit(solution)/shard_map/ppermute | solution.py:387
  32.6 0.9 %shard_map.92.entry_ref = f32[4,264,256]{2,1,0:T(8,128)S(1)} custom-call(f32[264,256]{1,0:T(8,128)S(1)} %get-tuple-element.35.before_ref, f32[264,256]{1,0:T(8,128)S(1)} %collective-permute-done.other_ref, f32[3,264,256]{2,1,0:T(8,128)S(1)} %get-tuple-element.36.chunk_ref), custom_call_target="tpu_custom_call" | custom-call | flops 402653184 | bytes 1048576 | tf_op jit(solution)/shard_map/pallas_call | solution.py:369
  33.6 0.0 collective-permute-done.6.came_ref
  33.6 2.7 %shard_map.93 = (f32[32,256]{1,0:T(8,128)}, f32[32,256]{1,0:T(8,128)S(1)}) custom-call(f32[8,256]{1,0:T(8,128)S(1)} %collective-permute-done.6.came_ref, f32[8,256]{1,0:T(8,128)S(1)} %get-tuple-element.34.enter_ref, f32[4,264,256]{2,1,0:T(8,128)S(1)} %shard_map.92.entry_ref, f32[32,264,256]{2,1,0:T(8,128)S(1)} %get-tuple-element.37.path_ref, ...), custom_call_target="tpu_custom_call" | custom-call | flops 671088640 | bytes 1048576 | tf_op jit(solution)/shard_map/pallas_call | solution.py:389
  36.4 18.1 %all_to_all.8 = f32[32,1,256]{2,1,0:T(1,128)S(1)} all-to-all(f32[32,1,256]{2,1,0:T(1,128)S(1)} %broadcast_in_dim.13), channel_id=1, replica_groups=mesh['tm'=32,'panel'=1] {'tm'}, dimensions={0} | all-to-all | bytes 65536 | tf_op jit(solution)/shard_map/all_to_all | solution.py:396
  54.5 2.7 %shard_map.94 = f32[32,256]{1,0:T(8,128)} custom-call(f32[32,256]{1,0:T(8,128)S(1)} %bitcast.10, f32[32,256]{1,0:T(8,128)S(1)} %get-tuple-element.41.local_ref, bf16[10,256,256]{2,1,0:T(8,128)(2,1)S(1)} %get-tuple-element.38.high_ref, bf16[10,256,256]{2,1,0:T(8,128)(2,1)S(1)} %get-tuple-element.39.low_ref), custom_call_target="tpu_custom_call" | custom-call | flops 671088640 | bytes 1048576 | tf_op jit(solution)/shard_map/pallas_call | solution.py:397
  (6 shorter events, 0.1 us)
Async XLA Ops:
  8.6 1.7 %collective-permute-start = (f32[264,256]{1,0:T(8,128)S(1)}, f32[264,256]{1,0:T(8,128)S(1)}, u32[]{:S(2)}, u32[]{:S(2)}) collective-permute-start(f32[264,256]{1,0:T(8,128)S(1)} %get-tuple-element.22.mine_ref), channel_id=1, source_target_pairs={{0,1},{1,0},{2,3},{3,2},{4,5},{5,4},{6,7},{7,6},{8,9},{9,8},{10,11... | collective-permute-start | bytes 811016 | tf_op jit(solution)/shard_map/ppermute | solution.py:334
  10.6 11.7 %collective-permute-start.1 = (f32[264,256]{1,0:T(8,128)S(1)}, f32[264,256]{1,0:T(8,128)S(1)}, u32[]{:S(2)}, u32[]{:S(2)}) collective-permute-start(f32[264,256]{1,0:T(8,128)S(1)} %get-tuple-element.23.chip_ref), channel_id=1, source_target_pairs={{0,2},{1,5},{2,0},{3,7},{4,6},{5,1},{6,4},{7,3},{8,10},{9,13},{10,... | collective-permute-start | bytes 811016 | tf_op jit(solution)/shard_map/ppermute | solution.py:341
  13.6 8.8 %collective-permute-start.2 = (f32[264,128]{1,0:T(8,128)S(1)}, f32[264,128]{1,0:T(8,128)S(1)}, u32[]{:S(2)}, u32[]{:S(2)}) collective-permute-start(f32[264,128]{1,0:T(8,128)S(1)} %get-tuple-element.24._), channel_id=1, source_target_pairs={{0,6},{1,7},{2,4},{3,5},{4,2},{5,3},{6,0},{7,1},{8,14},{9,15},{10,... | collective-permute-start | bytes 405512 | tf_op jit(solution)/shard_map/ppermute | solution.py:340
  22.4 1.8 %collective-permute-start.3 = (f32[3,264,128]{2,1,0:T(8,128)S(1)}, f32[3,264,128]{2,1,0:T(8,128)S(1)}, u32[]{:S(2)}, u32[]{:S(2)}) collective-permute-start(f32[3,264,128]{2,1,0:T(8,128)S(1)} %pad_maximum_fusion.mine_ref), channel_id=1, source_target_pairs={{0,1},{1,0},{2,3},{3,2},{4,5},{5,4},{6,7},{7,6},{8,9},{9,8},{10,11... | collective-permute-start | bytes 1216520 | tf_op jit(solution)/shard_map/ppermute | solution.py:361
  25.2 5.5 %collective-permute-start.4 = (f32[8,256]{1,0:T(8,128)S(1)}, f32[8,256]{1,0:T(8,128)S(1)}, u32[]{:S(2)}, u32[]{:S(2)}) collective-permute-start(f32[8,256]{1,0:T(8,128)S(1)} %get-tuple-element.30), channel_id=1, source_target_pairs={{0,8},{1,9},{2,10},{3,11},{4,12},{5,13},{6,14},{7,15},{8,0},{9,1},... | collective-permute-start | bytes 24584 | tf_op jit(solution)/shard_map/ppermute | solution.py:387
  31.0 0.7 %collective-permute-start.5 = (f32[8,256]{1,0:T(8,128)S(1)}, f32[8,256]{1,0:T(8,128)S(1)}, u32[]{:S(2)}, u32[]{:S(2)}) collective-permute-start(f32[8,256]{1,0:T(8,128)S(1)} %get-tuple-element.31), channel_id=1, source_target_pairs={{8,16},{9,17},{10,18},{11,19},{12,20},{13,21},{14,22},{15,23},{16,... | collective-permute-start | bytes 24584 | tf_op jit(solution)/shard_map/ppermute | solution.py:387
  32.0 1.6 %collective-permute-start.6 = (f32[8,256]{1,0:T(8,128)S(1)}, f32[8,256]{1,0:T(8,128)S(1)}, u32[]{:S(2)}, u32[]{:S(2)}) collective-permute-start(f32[8,256]{1,0:T(8,128)S(1)} %get-tuple-element.33), channel_id=1, source_target_pairs={{16,24},{17,25},{18,26},{19,27},{20,28},{21,29},{22,30},{23,31},{2... | collective-permute-start | bytes 24584 | tf_op jit(solution)/shard_map/ppermute | solution.py:387

commit v4 on v3

--- a/solution.py
+++ b/solution.py
@@ -32,6 +32,21 @@
     return jnp.dot(
         jnp.concatenate([high, high, low], axis=1), right_stack, preferred_element_type=f32
     )
+
+
+def dot_few(left, right_high, right_low):
+    count = left.shape[0]
+    high, low = split(left)
+    stacked = jnp.concatenate(
+        [
+            jnp.concatenate([high, high], axis=1),
+            jnp.concatenate([low, jnp.zeros_like(low)], axis=1),
+        ],
+        axis=0,
+    )
+    right = jnp.concatenate([right_high, right_low], axis=0)
+    both = jnp.dot(stacked, right, preferred_element_type=f32)
+    return both[:count] + both[count:]
 
 
 def compose(first, second):
@@ -86,15 +101,6 @@
     wide_ref[...] = jnp.concatenate([weights] * 4, axis=1)
     obs_high, obs_low = split(obs_mat)
     obs_stack = jnp.concatenate([obs_high, obs_low, obs_high, obs_low], axis=0)
-    offsets = exact(weights * obs_ref[...], obs_mat)
-    prior = jnp.broadcast_to(prior_ref[...], (PAD, width))
-    seen = lax.dot_general(
-        prior, obs_mat, (((1,), (1,)), ((), ())), precision=highest, preferred_element_type=f32
-    )
-    begun = prior - exact(seen * weights[0:1], obs_mat)
-    step_ids = lax.broadcasted_iota(jnp.int32, (steps, 1), 0)
-    offsets = offsets + jnp.where(step_ids == 0, is_first, 0.0) * begun[0:1]
-    offset_ref[...] = offsets
 
     half = width // 2
 
@@ -110,11 +116,8 @@
         begin = make(time) * damp
         if chunk == 0:
             begin = begin * (1.0 - is_first)
-        moved = jnp.concatenate(
-            [begin, jnp.broadcast_to(offset_ref[time : time + 1], (PAD, width))], axis=0
-        )
-        state_ref[chunk] = moved
-        path_ref[time] = moved
+        state_ref[chunk, :width] = begin
+        path_ref[time, :width] = begin
 
     def ready(step, chunk, slot):
         slot[0][chunk], slot[1][chunk] = split(make(chunk * span + step))
@@ -135,6 +138,21 @@
     even, odd = (high_even, low_even), (high_odd, low_odd)
     for chunk in range(CHUNKS):
         ready(1, chunk, odd)
+
+    offsets = exact(weights * obs_ref[...], obs_mat)
+    prior = jnp.broadcast_to(prior_ref[...], (PAD, width))
+    seen = lax.dot_general(
+        prior, obs_mat, (((1,), (1,)), ((), ())), precision=highest, preferred_element_type=f32
+    )
+    begun = prior - exact(seen * weights[0:1], obs_mat)
+    step_ids = lax.broadcasted_iota(jnp.int32, (steps, 1), 0)
+    offsets = offsets + jnp.where(step_ids == 0, is_first, 0.0) * begun[0:1]
+    offset_ref[...] = offsets
+    for chunk in range(CHUNKS):
+        time = chunk * span
+        begin = jnp.broadcast_to(offsets[time : time + 1], (PAD, width))
+        state_ref[chunk, width:] = begin
+        path_ref[time, width:] = begin
 
     def two(index, carry):
         advance(2 * index + 1, odd, even)
@@ -177,13 +195,16 @@
     mine, other = mine_ref[2], other_ref[2]
     all_ref[place ^ 3, :, :half] = jnp.where(upper, other, mine)
     all_ref[place ^ 3, :, half:] = jnp.where(upper, mine, other)
-    running = all_ref[0]
-    prefix_ref[0] = eye_map(chip_ref.shape[1])
-    for position in range(1, 4):
-        prefix_ref[position] = running
-        running = compose(running, all_ref[position])
-    plane_ref[...] = running
-    leave_ref[...] = running[chip_ref.shape[1] :]
+    width = chip_ref.shape[1]
+    left = compose(all_ref[0], all_ref[1])
+    right = compose(all_ref[2], all_ref[3])
+    whole = compose(left, right)
+    plane_ref[...] = whole
+    leave_ref[...] = whole[width:]
+    prefix_ref[0] = eye_map(width)
+    prefix_ref[1] = all_ref[0]
+    prefix_ref[2] = left
+    prefix_ref[3] = compose(left, all_ref[2])
     before_ref[...] = prefix_ref[place]
 
 
@@ -226,8 +247,7 @@
         later = jnp.concatenate(
             [rows[distance:], jnp.zeros((distance, width), f32)], axis=0
         )
-        right = stack_right(high_ref[first_level + level], low_ref[first_level + level])
-        rows = rows + dot_split(later, right)
+        rows = rows + dot_few(later, high_ref[first_level + level], low_ref[first_level + level])
     return rows
 
 
@@ -265,7 +285,7 @@
         all_ref[...], high_ref, low_ref, levels, (count - 1).bit_length()
     )
     incoming = jnp.broadcast_to(sum_ref[pl.ds(me + 1, 1), :], (PAD, width))
-    lifted = dot_split(incoming, stack_right(high_ref[0], low_ref[0]))[0:1]
+    lifted = dot_few(incoming, high_ref[0], low_ref[0])[0:1]
     step_ids = lax.broadcasted_iota(jnp.int32, (steps, 1), 0)
     rows = jnp.where(step_ids == steps - 1, lifted, 0.0)
     out_ref[...] = local_ref[...] + suffix_scan(rows, high_ref, low_ref, 0, levels)

time: 57.4 us -> 57 us (level)
  no operation moved by 1% of the time
where the time goes in v4:
time: 57 us; the launch traced here: 56.8 us
  Pallas kernels  21.6 us (38%)
  blocking collectives  18.1 us (32%)
  starting transfers between devices  9.83 us (17%)
  waiting for transfers between devices  6.35 us (11%)
  between operations  0.73 us (1%)
    all_to_all x1, blocking collectives, per_device(): offsets = lax.all_to_all(sent, 'tm', 0, 0, tiled=True)  18.1 us
    pallas_call x1, Pallas kernels, per_device(): call(local_kernel, (struct(steps, rows, width), struct(CHUNKS - 1, rows,...  8.08 us
    pallas_call x1, Pallas kernels, per_device(): call(power_kernel, (struct(3 * width, width, dtype=bf16), struct(power_co...  5.95 us
    ppermute x3, starting transfers between devices, per_device(): came = lax.ppermute(leave, 'tm', pairs)  4.79 us
    ppermute x1, starting transfers between devices, per_device(): whole = lax.ppermute(chip, 'tm', straight)  2.91 us
    pallas_call x1, Pallas kernels, per_device(): call(functools.partial(filter_kernel, levels=levels, hop=hops), (struct(s...  2.51 us
    pallas_call x1, Pallas kernels, per_device(): call(functools.partial(smooth_kernel, levels=levels), struct(steps, width...  2.44 us
    ppermute x3, waiting for transfers between devices, per_device(): came = lax.ppermute(leave, 'tm', pairs)  2.07 us
  transfers between devices with their start and end apart: 7, of which 4 were waited for; matrix products, arithmetic and copies ran while one was open for 0% of the time, Pallas kernels for 12%

profile of v4, /device:TPU:0, one launch (start us, length us, event | category | flops | bytes accessed | tf_op | source)
XLA Modules:
  0.0 56.8 jit_solution(17752180459346547069)
XLA Ops:
  0.6 8.1 %shard_map.86 = (f32[32,264,256]{2,1,0:T(8,128)S(1)}, f32[3,264,256]{2,1,0:T(8,128)S(1)}, f32[264,256]{1,0:T(8,128)S(1)}) custom-call(f32[32,64]{1,0:T(8,128)} %obs_hbm.1, f32[32,64]{1,0:T(8,128)} %weight_hbm.1, f32[32,256]{1,0:T(8,128)} %damp_hbm.1, f32[256,256]{1,0:T(8,128)} %trans_hbm.3, f32[64,256]{1,0:T(8,128)} %obsmat_hbm.1, f32[1,256]{1,0:T(1,128)} %bitcast.13), custom_call_target="tpu_custom_call" | custom-call | flops 4362076160 | bytes 1048576 | tf_op jit(solution)/shard_map/pallas_call | solution.py:329
  8.7 0.6 collective-permute-start
  9.3 1.2 %collective-permute-done.other_ref = f32[264,256]{1,0:T(8,128)S(1)} collective-permute-done((f32[264,256]{1,0:T(8,128)S(1)}, f32[264,256]{1,0:T(8,128)S(1)}, u32[]{:S(2)}, u32[]{:S(2)}) %collective-permute-start) | collective-permute-done | bytes 270368 | tf_op jit(solution)/shard_map/ppermute | solution.py:354
  10.5 0.3 shard_map.87
  10.8 2.9 %collective-permute-start.1 = (f32[264,256]{1,0:T(8,128)S(1)}, f32[264,256]{1,0:T(8,128)S(1)}, u32[]{:S(2)}, u32[]{:S(2)}) collective-permute-start(f32[264,256]{1,0:T(8,128)S(1)} %get-tuple-element.23.chip_ref), channel_id=1, source_target_pairs={{0,2},{1,5},{2,0},{3,7},{4,6},{5,1},{6,4},{7,3},{8,10},{9,13},{10,... | collective-permute-start | bytes 811016 | tf_op jit(solution)/shard_map/ppermute | solution.py:361
  13.7 1.5 %collective-permute-start.2 = (f32[264,128]{1,0:T(8,128)S(1)}, f32[264,128]{1,0:T(8,128)S(1)}, u32[]{:S(2)}, u32[]{:S(2)}) collective-permute-start(f32[264,128]{1,0:T(8,128)S(1)} %get-tuple-element.24._), channel_id=1, source_target_pairs={{0,6},{1,7},{2,4},{3,5},{4,2},{5,3},{6,0},{7,1},{8,14},{9,15},{10,... | collective-permute-start | bytes 405512 | tf_op jit(solution)/shard_map/ppermute | solution.py:360
  15.2 6.0 %shard_map.88 = (bf16[768,256]{1,0:T(8,128)(2,1)S(1)}, bf16[10,256,256]{2,1,0:T(8,128)(2,1)S(1)}, bf16[10,256,256]{2,1,0:T(8,128)(2,1)S(1)}) custom-call(f32[256,256]{1,0:T(8,128)} %trans_hbm.3, f32[256,256]{1,0:T(8,128)} %gain_hbm.1, f32[264,128]{1,0:T(8,128)S(1)} %get-tuple-element.24._), custom_call_target="tpu_custom_call" | custom-call | flops 2013265920 | bytes 1048576 | tf_op jit(solution)/shard_map/pallas_call | solution.py:364
  21.1 1.4 %collective-permute-done.2 = f32[264,128]{1,0:T(8,128)S(1)} collective-permute-done((f32[264,128]{1,0:T(8,128)S(1)}, f32[264,128]{1,0:T(8,128)S(1)}, u32[]{:S(2)}, u32[]{:S(2)}) %collective-permute-start.2) | collective-permute-done | bytes 135200 | tf_op jit(solution)/shard_map/ppermute | solution.py:360
  22.5 0.0 collective-permute-done.1
  22.6 0.1 collective-permute-start.3
  22.7 1.7 %collective-permute-done.3.other_ref = f32[3,264,128]{2,1,0:T(8,128)S(1)} collective-permute-done((f32[3,264,128]{2,1,0:T(8,128)S(1)}, f32[3,264,128]{2,1,0:T(8,128)S(1)}, u32[]{:S(2)}, u32[]{:S(2)}) %collective-permute-start.3) | collective-permute-done | bytes 405536 | tf_op jit(solution)/shard_map/ppermute | solution.py:381
  24.4 0.9 %shard_map.89 = (f32[264,256]{1,0:T(8,128)S(1)}, f32[264,256]{1,0:T(8,128)S(1)}, f32[8,256]{1,0:T(8,128)S(1)}) custom-call(f32[264,256]{1,0:T(8,128)S(1)} %get-tuple-element.23.chip_ref, f32[3,264,128]{2,1,0:T(8,128)S(1)} %pad_maximum_fusion.mine_ref, f32[3,264,128]{2,1,0:T(8,128)S(1)} %collective-permute-done.3.other_ref, ...), custom_call_target="tpu_custom_call" | custom-call | flops 301989888 | bytes 1048576 | tf_op jit(solution)/shard_map/pallas_call | solution.py:382
  25.2 3.5 %collective-permute-start.4 = (f32[8,256]{1,0:T(8,128)S(1)}, f32[8,256]{1,0:T(8,128)S(1)}, u32[]{:S(2)}, u32[]{:S(2)}) collective-permute-start(f32[8,256]{1,0:T(8,128)S(1)} %get-tuple-element.30), channel_id=1, source_target_pairs={{0,8},{1,9},{2,10},{3,11},{4,12},{5,13},{6,14},{7,15},{8,0},{9,1},... | collective-permute-start | bytes 24584 | tf_op jit(solution)/shard_map/ppermute | solution.py:407
  28.7 2.1 %collective-permute-done.4.came_ref = f32[8,256]{1,0:T(8,128)S(1)} collective-permute-done((f32[8,256]{1,0:T(8,128)S(1)}, f32[8,256]{1,0:T(8,128)S(1)}, u32[]{:S(2)}, u32[]{:S(2)}) %collective-permute-start.4) | collective-permute-done | bytes 8224 | tf_op jit(solution)/shard_map/ppermute | solution.py:407
  30.8 0.3 shard_map.90
  31.1 0.7 %collective-permute-start.5 = (f32[8,256]{1,0:T(8,128)S(1)}, f32[8,256]{1,0:T(8,128)S(1)}, u32[]{:S(2)}, u32[]{:S(2)}) collective-permute-start(f32[8,256]{1,0:T(8,128)S(1)} %get-tuple-element.31), channel_id=1, source_target_pairs={{8,16},{9,17},{10,18},{11,19},{12,20},{13,21},{14,22},{15,23},{16,... | collective-permute-start | bytes 24584 | tf_op jit(solution)/shard_map/ppermute | solution.py:407
  31.7 0.0 collective-permute-done.5.came_ref
  31.7 0.3 shard_map.91
  32.0 0.7 %collective-permute-start.6 = (f32[8,256]{1,0:T(8,128)S(1)}, f32[8,256]{1,0:T(8,128)S(1)}, u32[]{:S(2)}, u32[]{:S(2)}) collective-permute-start(f32[8,256]{1,0:T(8,128)S(1)} %get-tuple-element.33), channel_id=1, source_target_pairs={{16,24},{17,25},{18,26},{19,27},{20,28},{21,29},{22,30},{23,31},{2... | collective-permute-start | bytes 24584 | tf_op jit(solution)/shard_map/ppermute | solution.py:407
  32.7 0.9 %shard_map.92.entry_ref = f32[4,264,256]{2,1,0:T(8,128)S(1)} custom-call(f32[264,256]{1,0:T(8,128)S(1)} %get-tuple-element.35.before_ref, f32[264,256]{1,0:T(8,128)S(1)} %collective-permute-done.other_ref, f32[3,264,256]{2,1,0:T(8,128)S(1)} %get-tuple-element.36.chunk_ref), custom_call_target="tpu_custom_call" | custom-call | flops 402653184 | bytes 1048576 | tf_op jit(solution)/shard_map/pallas_call | solution.py:389
  33.6 0.0 collective-permute-done.6.came_ref
  33.6 2.5 %shard_map.93 = (f32[32,256]{1,0:T(8,128)}, f32[32,256]{1,0:T(8,128)S(1)}) custom-call(f32[8,256]{1,0:T(8,128)S(1)} %collective-permute-done.6.came_ref, f32[8,256]{1,0:T(8,128)S(1)} %get-tuple-element.34.enter_ref, f32[4,264,256]{2,1,0:T(8,128)S(1)} %shard_map.92.entry_ref, f32[32,264,256]{2,1,0:T(8,128)S(1)} %get-tuple-element.37.path_ref, ...), custom_call_target="tpu_custom_call" | custom-call | flops 671088640 | bytes 1048576 | tf_op jit(solution)/shard_map/pallas_call | solution.py:409
  36.2 18.1 %all_to_all.8 = f32[32,1,256]{2,1,0:T(1,128)S(1)} all-to-all(f32[32,1,256]{2,1,0:T(1,128)S(1)} %broadcast_in_dim.13), channel_id=1, replica_groups=mesh['tm'=32,'panel'=1] {'tm'}, dimensions={0} | all-to-all | bytes 65536 | tf_op jit(solution)/shard_map/all_to_all | solution.py:416
  54.3 2.4 %shard_map.94 = f32[32,256]{1,0:T(8,128)} custom-call(f32[32,256]{1,0:T(8,128)S(1)} %bitcast.10, f32[32,256]{1,0:T(8,128)S(1)} %get-tuple-element.41.local_ref, bf16[10,256,256]{2,1,0:T(8,128)(2,1)S(1)} %get-tuple-element.38.high_ref, bf16[10,256,256]{2,1,0:T(8,128)(2,1)S(1)} %get-tuple-element.39.low_ref), custom_call_target="tpu_custom_call" | custom-call | flops 671088640 | bytes 1048576 | tf_op jit(solution)/shard_map/pallas_call | solution.py:417
  (6 shorter events, 0.1 us)
Async XLA Ops:
  8.7 1.7 %collective-permute-start = (f32[264,256]{1,0:T(8,128)S(1)}, f32[264,256]{1,0:T(8,128)S(1)}, u32[]{:S(2)}, u32[]{:S(2)}) collective-permute-start(f32[264,256]{1,0:T(8,128)S(1)} %get-tuple-element.22.mine_ref), channel_id=1, source_target_pairs={{0,1},{1,0},{2,3},{3,2},{4,5},{5,4},{6,7},{7,6},{8,9},{9,8},{10,11... | collective-permute-start | bytes 811016 | tf_op jit(solution)/shard_map/ppermute | solution.py:354
  10.8 11.7 %collective-permute-start.1 = (f32[264,256]{1,0:T(8,128)S(1)}, f32[264,256]{1,0:T(8,128)S(1)}, u32[]{:S(2)}, u32[]{:S(2)}) collective-permute-start(f32[264,256]{1,0:T(8,128)S(1)} %get-tuple-element.23.chip_ref), channel_id=1, source_target_pairs={{0,2},{1,5},{2,0},{3,7},{4,6},{5,1},{6,4},{7,3},{8,10},{9,13},{10,... | collective-permute-start | bytes 811016 | tf_op jit(solution)/shard_map/ppermute | solution.py:361
  13.7 8.8 %collective-permute-start.2 = (f32[264,128]{1,0:T(8,128)S(1)}, f32[264,128]{1,0:T(8,128)S(1)}, u32[]{:S(2)}, u32[]{:S(2)}) collective-permute-start(f32[264,128]{1,0:T(8,128)S(1)} %get-tuple-element.24._), channel_id=1, source_target_pairs={{0,6},{1,7},{2,4},{3,5},{4,2},{5,3},{6,0},{7,1},{8,14},{9,15},{10,... | collective-permute-start | bytes 405512 | tf_op jit(solution)/shard_map/ppermute | solution.py:360
  22.6 1.8 %collective-permute-start.3 = (f32[3,264,128]{2,1,0:T(8,128)S(1)}, f32[3,264,128]{2,1,0:T(8,128)S(1)}, u32[]{:S(2)}, u32[]{:S(2)}) collective-permute-start(f32[3,264,128]{2,1,0:T(8,128)S(1)} %pad_maximum_fusion.mine_ref), channel_id=1, source_target_pairs={{0,1},{1,0},{2,3},{3,2},{4,5},{5,4},{6,7},{7,6},{8,9},{9,8},{10,11... | collective-permute-start | bytes 1216520 | tf_op jit(solution)/shard_map/ppermute | solution.py:381
  25.2 5.5 %collective-permute-start.4 = (f32[8,256]{1,0:T(8,128)S(1)}, f32[8,256]{1,0:T(8,128)S(1)}, u32[]{:S(2)}, u32[]{:S(2)}) collective-permute-start(f32[8,256]{1,0:T(8,128)S(1)} %get-tuple-element.30), channel_id=1, source_target_pairs={{0,8},{1,9},{2,10},{3,11},{4,12},{5,13},{6,14},{7,15},{8,0},{9,1},... | collective-permute-start | bytes 24584 | tf_op jit(solution)/shard_map/ppermute | solution.py:407
  31.1 0.7 %collective-permute-start.5 = (f32[8,256]{1,0:T(8,128)S(1)}, f32[8,256]{1,0:T(8,128)S(1)}, u32[]{:S(2)}, u32[]{:S(2)}) collective-permute-start(f32[8,256]{1,0:T(8,128)S(1)} %get-tuple-element.31), channel_id=1, source_target_pairs={{8,16},{9,17},{10,18},{11,19},{12,20},{13,21},{14,22},{15,23},{16,... | collective-permute-start | bytes 24584 | tf_op jit(solution)/shard_map/ppermute | solution.py:407
  32.0 1.6 %collective-permute-start.6 = (f32[8,256]{1,0:T(8,128)S(1)}, f32[8,256]{1,0:T(8,128)S(1)}, u32[]{:S(2)}, u32[]{:S(2)}) collective-permute-start(f32[8,256]{1,0:T(8,128)S(1)} %get-tuple-element.33), channel_id=1, source_target_pairs={{16,24},{17,25},{18,26},{19,27},{20,28},{21,29},{22,30},{23,31},{2... | collective-permute-start | bytes 24584 | tf_op jit(solution)/shard_map/ppermute | solution.py:407

commit v5 on v4

--- a/solution.py
+++ b/solution.py
@@ -403,7 +403,6 @@
             )(plane, came, enter)
         low, high = hop * PLANE, (hop + 1) * PLANE
         pairs = [(low + i, high + i) for i in range(PLANE)]
-        pairs = pairs + [(b, a) for a, b in pairs]
         came = lax.ppermute(leave, "tm", pairs)
 
     filtered, local = call(

time: 57 us -> 55.2 us (0.968)
  blocking collectives: 18.1 us -> 17 us
  waiting for transfers between devices: 6.35 us -> 5.63 us
    all_to_all x1, blocking collectives: 18.1 us -> 17 us  [per_device(): offsets = lax.all_to_all(sent, 'tm', 0, 0, tiled=True)]
    ppermute x3, waiting for transfers between devices: 2.07 us -> 1.35 us  [per_device(): came = lax.ppermute(leave, 'tm', pairs)]
  transfers between devices with their start and end apart: 7 -> 7, of which waited for: 4 -> 4; matrix products, arithmetic and copies ran while one was open for 0% -> 0% of each run, Pallas kernels for 12% -> 13%
where the time goes in v5:
time: 55.2 us; the launch traced here: 54.9 us
  Pallas kernels  21.6 us (39%)
  blocking collectives  17 us (31%)
  starting transfers between devices  9.83 us (18%)
  waiting for transfers between devices  5.63 us (10%)
  between operations  0.73 us (1%)
    all_to_all x1, blocking collectives, per_device(): offsets = lax.all_to_all(sent, 'tm', 0, 0, tiled=True)  17 us
    pallas_call x1, Pallas kernels, per_device(): call(local_kernel, (struct(steps, rows, width), struct(CHUNKS - 1, rows,...  8.08 us
    pallas_call x1, Pallas kernels, per_device(): call(power_kernel, (struct(3 * width, width, dtype=bf16), struct(power_co...  5.95 us
    ppermute x3, starting transfers between devices, per_device(): came = lax.ppermute(leave, 'tm', pairs)  4.79 us
    ppermute x1, starting transfers between devices, per_device(): whole = lax.ppermute(chip, 'tm', straight)  2.91 us
    pallas_call x1, Pallas kernels, per_device(): call(functools.partial(filter_kernel, levels=levels, hop=hops), (struct(s...  2.51 us
    pallas_call x1, Pallas kernels, per_device(): call(functools.partial(smooth_kernel, levels=levels), struct(steps, width...  2.45 us
    ppermute x1, waiting for transfers between devices, per_device(): other_halves = lax.ppermute(halves, 'tm', swap(count, 1))  1.73 us
  transfers between devices with their start and end apart: 7, of which 4 were waited for; matrix products, arithmetic and copies ran while one was open for 0% of the time, Pallas kernels for 13%

profile of v5, /device:TPU:0, one launch (start us, length us, event | category | flops | bytes accessed | tf_op | source)
XLA Modules:
  0.0 54.9 jit_solution(3402276634770512082)
XLA Ops:
  0.6 8.1 %shard_map.86 = (f32[32,264,256]{2,1,0:T(8,128)S(1)}, f32[3,264,256]{2,1,0:T(8,128)S(1)}, f32[264,256]{1,0:T(8,128)S(1)}) custom-call(f32[32,64]{1,0:T(8,128)} %obs_hbm.1, f32[32,64]{1,0:T(8,128)} %weight_hbm.1, f32[32,256]{1,0:T(8,128)} %damp_hbm.1, f32[256,256]{1,0:T(8,128)} %trans_hbm.3, f32[64,256]{1,0:T(8,128)} %obsmat_hbm.1, f32[1,256]{1,0:T(1,128)} %bitcast.13), custom_call_target="tpu_custom_call" | custom-call | flops 4362076160 | bytes 1048576 | tf_op jit(solution)/shard_map/pallas_call | solution.py:329
  8.7 0.6 %collective-permute-start = (f32[264,256]{1,0:T(8,128)S(1)}, f32[264,256]{1,0:T(8,128)S(1)}, u32[]{:S(2)}, u32[]{:S(2)}) collective-permute-start(f32[264,256]{1,0:T(8,128)S(1)} %get-tuple-element.22.mine_ref), channel_id=1, source_target_pairs={{0,1},{1,0},{2,3},{3,2},{4,5},{5,4},{6,7},{7,6},{8,9},{9,8},{10,11... | collective-permute-start | bytes 811016 | tf_op jit(solution)/shard_map/ppermute | solution.py:354
  9.3 1.2 %collective-permute-done.other_ref = f32[264,256]{1,0:T(8,128)S(1)} collective-permute-done((f32[264,256]{1,0:T(8,128)S(1)}, f32[264,256]{1,0:T(8,128)S(1)}, u32[]{:S(2)}, u32[]{:S(2)}) %collective-permute-start) | collective-permute-done | bytes 270368 | tf_op jit(solution)/shard_map/ppermute | solution.py:354
  10.5 0.3 shard_map.87
  10.8 2.9 %collective-permute-start.1 = (f32[264,256]{1,0:T(8,128)S(1)}, f32[264,256]{1,0:T(8,128)S(1)}, u32[]{:S(2)}, u32[]{:S(2)}) collective-permute-start(f32[264,256]{1,0:T(8,128)S(1)} %get-tuple-element.23.chip_ref), channel_id=1, source_target_pairs={{0,2},{1,5},{2,0},{3,7},{4,6},{5,1},{6,4},{7,3},{8,10},{9,13},{10,... | collective-permute-start | bytes 811016 | tf_op jit(solution)/shard_map/ppermute | solution.py:361
  13.7 1.5 %collective-permute-start.2 = (f32[264,128]{1,0:T(8,128)S(1)}, f32[264,128]{1,0:T(8,128)S(1)}, u32[]{:S(2)}, u32[]{:S(2)}) collective-permute-start(f32[264,128]{1,0:T(8,128)S(1)} %get-tuple-element.24._), channel_id=1, source_target_pairs={{0,6},{1,7},{2,4},{3,5},{4,2},{5,3},{6,0},{7,1},{8,14},{9,15},{10,... | collective-permute-start | bytes 405512 | tf_op jit(solution)/shard_map/ppermute | solution.py:360
  15.2 6.0 %shard_map.88 = (bf16[768,256]{1,0:T(8,128)(2,1)S(1)}, bf16[10,256,256]{2,1,0:T(8,128)(2,1)S(1)}, bf16[10,256,256]{2,1,0:T(8,128)(2,1)S(1)}) custom-call(f32[256,256]{1,0:T(8,128)} %trans_hbm.3, f32[256,256]{1,0:T(8,128)} %gain_hbm.1, f32[264,128]{1,0:T(8,128)S(1)} %get-tuple-element.24._), custom_call_target="tpu_custom_call" | custom-call | flops 2013265920 | bytes 1048576 | tf_op jit(solution)/shard_map/pallas_call | solution.py:364
  21.1 1.4 %collective-permute-done.2 = f32[264,128]{1,0:T(8,128)S(1)} collective-permute-done((f32[264,128]{1,0:T(8,128)S(1)}, f32[264,128]{1,0:T(8,128)S(1)}, u32[]{:S(2)}, u32[]{:S(2)}) %collective-permute-start.2) | collective-permute-done | bytes 135200 | tf_op jit(solution)/shard_map/ppermute | solution.py:360
  22.5 0.0 collective-permute-done.1
  22.6 0.1 collective-permute-start.3
  22.7 1.7 %collective-permute-done.3.other_ref = f32[3,264,128]{2,1,0:T(8,128)S(1)} collective-permute-done((f32[3,264,128]{2,1,0:T(8,128)S(1)}, f32[3,264,128]{2,1,0:T(8,128)S(1)}, u32[]{:S(2)}, u32[]{:S(2)}) %collective-permute-start.3) | collective-permute-done | bytes 405536 | tf_op jit(solution)/shard_map/ppermute | solution.py:381
  24.4 0.9 %shard_map.89 = (f32[264,256]{1,0:T(8,128)S(1)}, f32[264,256]{1,0:T(8,128)S(1)}, f32[8,256]{1,0:T(8,128)S(1)}) custom-call(f32[264,256]{1,0:T(8,128)S(1)} %get-tuple-element.23.chip_ref, f32[3,264,128]{2,1,0:T(8,128)S(1)} %pad_maximum_fusion.mine_ref, f32[3,264,128]{2,1,0:T(8,128)S(1)} %collective-permute-done.3.other_ref, ...), custom_call_target="tpu_custom_call" | custom-call | flops 301989888 | bytes 1048576 | tf_op jit(solution)/shard_map/pallas_call | solution.py:382
  25.2 3.5 %collective-permute-start.4 = (f32[8,256]{1,0:T(8,128)S(1)}, f32[8,256]{1,0:T(8,128)S(1)}, u32[]{:S(2)}, u32[]{:S(2)}) collective-permute-start(f32[8,256]{1,0:T(8,128)S(1)} %get-tuple-element.30), channel_id=1, source_target_pairs={{0,8},{1,9},{2,10},{3,11},{4,12},{5,13},{6,14},{7,15}} | collective-permute-start | bytes 24584 | tf_op jit(solution)/shard_map/ppermute | solution.py:406
  28.7 1.3 %collective-permute-done.4.came_ref = f32[8,256]{1,0:T(8,128)S(1)} collective-permute-done((f32[8,256]{1,0:T(8,128)S(1)}, f32[8,256]{1,0:T(8,128)S(1)}, u32[]{:S(2)}, u32[]{:S(2)}) %collective-permute-start.4) | collective-permute-done | bytes 8224 | tf_op jit(solution)/shard_map/ppermute | solution.py:406
  30.1 0.3 shard_map.90
  30.3 0.7 %collective-permute-start.5 = (f32[8,256]{1,0:T(8,128)S(1)}, f32[8,256]{1,0:T(8,128)S(1)}, u32[]{:S(2)}, u32[]{:S(2)}) collective-permute-start(f32[8,256]{1,0:T(8,128)S(1)} %get-tuple-element.31), channel_id=1, source_target_pairs={{8,16},{9,17},{10,18},{11,19},{12,20},{13,21},{14,22},{15,23}} | collective-permute-start | bytes 24584 | tf_op jit(solution)/shard_map/ppermute | solution.py:406
  31.0 0.0 collective-permute-done.5.came_ref
  31.0 0.3 shard_map.91
  31.3 0.7 %collective-permute-start.6 = (f32[8,256]{1,0:T(8,128)S(1)}, f32[8,256]{1,0:T(8,128)S(1)}, u32[]{:S(2)}, u32[]{:S(2)}) collective-permute-start(f32[8,256]{1,0:T(8,128)S(1)} %get-tuple-element.33), channel_id=1, source_target_pairs={{16,24},{17,25},{18,26},{19,27},{20,28},{21,29},{22,30},{23,31}} | collective-permute-start | bytes 24584 | tf_op jit(solution)/shard_map/ppermute | solution.py:406
  32.0 0.9 %shard_map.92.entry_ref = f32[4,264,256]{2,1,0:T(8,128)S(1)} custom-call(f32[264,256]{1,0:T(8,128)S(1)} %get-tuple-element.35.before_ref, f32[264,256]{1,0:T(8,128)S(1)} %collective-permute-done.other_ref, f32[3,264,256]{2,1,0:T(8,128)S(1)} %get-tuple-element.36.chunk_ref), custom_call_target="tpu_custom_call" | custom-call | flops 402653184 | bytes 1048576 | tf_op jit(solution)/shard_map/pallas_call | solution.py:389
  32.9 0.0 collective-permute-done.6.came_ref
  32.9 2.5 %shard_map.93 = (f32[32,256]{1,0:T(8,128)}, f32[32,256]{1,0:T(8,128)S(1)}) custom-call(f32[8,256]{1,0:T(8,128)S(1)} %collective-permute-done.6.came_ref, f32[8,256]{1,0:T(8,128)S(1)} %get-tuple-element.34.enter_ref, f32[4,264,256]{2,1,0:T(8,128)S(1)} %shard_map.92.entry_ref, f32[32,264,256]{2,1,0:T(8,128)S(1)} %get-tuple-element.37.path_ref, ...), custom_call_target="tpu_custom_call" | custom-call | flops 671088640 | bytes 1048576 | tf_op jit(solution)/shard_map/pallas_call | solution.py:408
  35.5 17.0 %all_to_all.8 = f32[32,1,256]{2,1,0:T(1,128)S(1)} all-to-all(f32[32,1,256]{2,1,0:T(1,128)S(1)} %broadcast_in_dim.13), channel_id=1, replica_groups=mesh['tm'=32,'panel'=1] {'tm'}, dimensions={0} | all-to-all | bytes 65536 | tf_op jit(solution)/shard_map/all_to_all | solution.py:415
  52.5 2.4 %shard_map.94 = f32[32,256]{1,0:T(8,128)} custom-call(f32[32,256]{1,0:T(8,128)S(1)} %bitcast.10, f32[32,256]{1,0:T(8,128)S(1)} %get-tuple-element.41.local_ref, bf16[10,256,256]{2,1,0:T(8,128)(2,1)S(1)} %get-tuple-element.38.high_ref, bf16[10,256,256]{2,1,0:T(8,128)(2,1)S(1)} %get-tuple-element.39.low_ref), custom_call_target="tpu_custom_call" | custom-call | flops 671088640 | bytes 1048576 | tf_op jit(solution)/shard_map/pallas_call | solution.py:416
  (6 shorter events, 0.1 us)
Async XLA Ops:
  8.7 1.7 %collective-permute-start = (f32[264,256]{1,0:T(8,128)S(1)}, f32[264,256]{1,0:T(8,128)S(1)}, u32[]{:S(2)}, u32[]{:S(2)}) collective-permute-start(f32[264,256]{1,0:T(8,128)S(1)} %get-tuple-element.22.mine_ref), channel_id=1, source_target_pairs={{0,1},{1,0},{2,3},{3,2},{4,5},{5,4},{6,7},{7,6},{8,9},{9,8},{10,11... | collective-permute-start | bytes 811016 | tf_op jit(solution)/shard_map/ppermute | solution.py:354
  10.8 11.7 %collective-permute-start.1 = (f32[264,256]{1,0:T(8,128)S(1)}, f32[264,256]{1,0:T(8,128)S(1)}, u32[]{:S(2)}, u32[]{:S(2)}) collective-permute-start(f32[264,256]{1,0:T(8,128)S(1)} %get-tuple-element.23.chip_ref), channel_id=1, source_target_pairs={{0,2},{1,5},{2,0},{3,7},{4,6},{5,1},{6,4},{7,3},{8,10},{9,13},{10,... | collective-permute-start | bytes 811016 | tf_op jit(solution)/shard_map/ppermute | solution.py:361
  13.7 8.8 %collective-permute-start.2 = (f32[264,128]{1,0:T(8,128)S(1)}, f32[264,128]{1,0:T(8,128)S(1)}, u32[]{:S(2)}, u32[]{:S(2)}) collective-permute-start(f32[264,128]{1,0:T(8,128)S(1)} %get-tuple-element.24._), channel_id=1, source_target_pairs={{0,6},{1,7},{2,4},{3,5},{4,2},{5,3},{6,0},{7,1},{8,14},{9,15},{10,... | collective-permute-start | bytes 405512 | tf_op jit(solution)/shard_map/ppermute | solution.py:360
  22.6 1.8 %collective-permute-start.3 = (f32[3,264,128]{2,1,0:T(8,128)S(1)}, f32[3,264,128]{2,1,0:T(8,128)S(1)}, u32[]{:S(2)}, u32[]{:S(2)}) collective-permute-start(f32[3,264,128]{2,1,0:T(8,128)S(1)} %pad_maximum_fusion.mine_ref), channel_id=1, source_target_pairs={{0,1},{1,0},{2,3},{3,2},{4,5},{5,4},{6,7},{7,6},{8,9},{9,8},{10,11... | collective-permute-start | bytes 1216520 | tf_op jit(solution)/shard_map/ppermute | solution.py:381
  25.2 4.8 %collective-permute-start.4 = (f32[8,256]{1,0:T(8,128)S(1)}, f32[8,256]{1,0:T(8,128)S(1)}, u32[]{:S(2)}, u32[]{:S(2)}) collective-permute-start(f32[8,256]{1,0:T(8,128)S(1)} %get-tuple-element.30), channel_id=1, source_target_pairs={{0,8},{1,9},{2,10},{3,11},{4,12},{5,13},{6,14},{7,15}} | collective-permute-start | bytes 24584 | tf_op jit(solution)/shard_map/ppermute | solution.py:406
  30.3 0.7 %collective-permute-start.5 = (f32[8,256]{1,0:T(8,128)S(1)}, f32[8,256]{1,0:T(8,128)S(1)}, u32[]{:S(2)}, u32[]{:S(2)}) collective-permute-start(f32[8,256]{1,0:T(8,128)S(1)} %get-tuple-element.31), channel_id=1, source_target_pairs={{8,16},{9,17},{10,18},{11,19},{12,20},{13,21},{14,22},{15,23}} | collective-permute-start | bytes 24584 | tf_op jit(solution)/shard_map/ppermute | solution.py:406
  31.3 1.6 %collective-permute-start.6 = (f32[8,256]{1,0:T(8,128)S(1)}, f32[8,256]{1,0:T(8,128)S(1)}, u32[]{:S(2)}, u32[]{:S(2)}) collective-permute-start(f32[8,256]{1,0:T(8,128)S(1)} %get-tuple-element.33), channel_id=1, source_target_pairs={{16,24},{17,25},{18,26},{19,27},{20,28},{21,29},{22,30},{23,31}} | collective-permute-start | bytes 24584 | tf_op jit(solution)/shard_map/ppermute | solution.py:406

commit v6 on v5

--- a/solution.py
+++ b/solution.py
@@ -231,8 +231,7 @@
 def power_kernel(trans_hbm, gain_hbm, _, mix_ref, high_ref, low_ref, trans_ref, gain_ref, sems):
     fetch((trans_hbm, gain_hbm), (trans_ref, gain_ref), sems)
     gain_t = gain_ref[...].T
-    mix_high, mix_low = split(exact(trans_ref[...].T, gain_t))
-    mix_ref[...] = stack_right(mix_high, mix_low)
+    mix_ref[0], mix_ref[1] = split(exact(trans_ref[...].T, gain_t))
     power = gain_t
     for level in range(high_ref.shape[0]):
         high_ref[level], low_ref[level] = split(power)
@@ -252,14 +251,17 @@
 
 
 def filter_kernel(
-    came_ref, enter_ref, entry_ref, path_ref, mix_ref, high_ref, low_ref,
+    came_ref, enter_ref, came_zero_ref, enter_zero_ref, entry_ref, path_ref, mix_ref, high_ref, low_ref,
     filtered_ref, local_ref, *, levels, hop
 ):
     steps, _, width = path_ref.shape
     span = steps // CHUNKS
     is_final = lax.axis_index("tm") == lax.axis_size("tm") - 1
-    here = lax.axis_index("tm") // PLANE == hop
-    column = as_column(jnp.where(here, came_ref[...], enter_ref[...]))
+    me = lax.axis_index("tm")
+    here, upper = me // PLANE == hop, me % 2 == 1
+    came = jnp.where(upper, came_ref[...], came_zero_ref[...])
+    enter = jnp.where(upper, enter_ref[...], enter_zero_ref[...])
+    column = as_column(jnp.where(here, came, enter))
     for chunk in range(CHUNKS):
         entry = entry_ref[chunk]
         start = jnp.sum(entry[:width] * column, axis=0, keepdims=True) + entry[width : width + 1]
@@ -272,7 +274,7 @@
     filtered = filtered_ref[...]
     step_ids = lax.broadcasted_iota(jnp.int32, (steps, 1), 0)
     keep = jnp.where(jnp.logical_and(step_ids == steps - 1, is_final), 0.0, 1.0)
-    change = filtered - keep * dot_split(filtered, mix_ref[...])
+    change = filtered - keep * dot_few(filtered, mix_ref[0], mix_ref[1])
     local_ref[...] = suffix_scan(change, high_ref, low_ref, 0, levels)
 
 
@@ -364,7 +366,7 @@
     mix, power_high, power_low = call(
         power_kernel,
         (
-            struct(3 * width, width, dtype=bf16),
+            struct(2, width, width, dtype=bf16),
             struct(power_count, width, width, dtype=bf16),
             struct(power_count, width, width, dtype=bf16),
         ),
@@ -391,7 +393,7 @@
     )
 
     enter = jnp.zeros((PAD, width), f32)
-    came = leave
+    came = enter
     hops = count // PLANE - 1
     for hop in range(hops):
         if hop > 0:
@@ -402,14 +404,18 @@
                 limit=2,
             )(plane, came, enter)
         low, high = hop * PLANE, (hop + 1) * PLANE
-        pairs = [(low + i, high + i) for i in range(PLANE)]
+        pairs = [(low + i, high + i) for i in range(1, PLANE, 2)]
         came = lax.ppermute(leave, "tm", pairs)
 
+    to_zero = [(index, index - 1) for index in range(1, count, 2)]
+    enter_zero = lax.ppermute(enter, "tm", to_zero)
+    came, entry = lax.optimization_barrier((came, entry))
+    came_zero = lax.ppermute(came, "tm", to_zero)
     filtered, local = call(
         functools.partial(filter_kernel, levels=levels, hop=hops),
         (struct(steps, width), struct(steps, width)),
         flops=20 * cube,
-    )(came, enter, entry, path, mix, power_high, power_low)
+    )(came, enter, came_zero, enter_zero, entry, path, mix, power_high, power_low)
 
     sent = jnp.broadcast_to(local[0:1], (count, width))
     offsets = lax.all_to_all(sent, "tm", 0, 0, tiled=True)

time: 55.2 us -> 54.6 us (0.989)
  blocking collectives: 17 us -> 13.8 us
  waiting for transfers between devices: 5.63 us -> 8.33 us
    ppermute x0 -> x2, waiting for transfers between devices: none -> 4.04 us  [the longest x1 2.73 us: per_device(): enter_zero = lax.ppermute(enter, 'tm', to_zero)]
    all_to_all x1, blocking collectives: 17 us -> 13.8 us  [per_device(): offsets = lax.all_to_all(sent, 'tm', 0, 0, tiled=True)]
    ppermute x3, starting transfers between devices: 4.79 us -> 1.98 us  [per_device(): came = lax.ppermute(leave, 'tm', pairs)]
    ppermute x0 -> x2, starting transfers between devices: none -> 2.58 us  [the longest x1 1.29 us: per_device(): enter_zero = lax.ppermute(enter, 'tm', to_zero)]
    ppermute x3, waiting for transfers between devices: 1.35 us -> 0.01 us  [per_device(): came = lax.ppermute(leave, 'tm', pairs)]
  transfers between devices with their start and end apart: 7 -> 9, of which waited for: 4 -> 5; matrix products, arithmetic and copies ran while one was open for 0% -> 0% of each run, Pallas kernels for 13% -> 13%
where the time goes in v6:
time: 54.6 us; the launch traced here: 54.3 us
  Pallas kernels  21.7 us (40%)
  blocking collectives  13.8 us (25%)
  starting transfers between devices  9.61 us (18%)
  waiting for transfers between devices  8.33 us (15%)
  between operations  0.77 us (1%)
    all_to_all x1, blocking collectives, per_device(): offsets = lax.all_to_all(sent, 'tm', 0, 0, tiled=True)  13.8 us
    pallas_call x1, Pallas kernels, per_device(): call(local_kernel, (struct(steps, rows, width), struct(CHUNKS - 1, rows,...  8.08 us
    pallas_call x1, Pallas kernels, per_device(): call(power_kernel, (struct(2, width, width, dtype=bf16), struct(power_cou...  5.95 us
    ppermute x1, starting transfers between devices, per_device(): whole = lax.ppermute(chip, 'tm', straight)  2.91 us
    ppermute x1, waiting for transfers between devices, per_device(): enter_zero = lax.ppermute(enter, 'tm', to_zero)  2.73 us
    pallas_call x1, Pallas kernels, per_device(): call(functools.partial(filter_kernel, levels=levels, hop=hops), (struct(s...  2.63 us
    pallas_call x1, Pallas kernels, per_device(): call(functools.partial(smooth_kernel, levels=levels), struct(steps, width...  2.44 us
    ppermute x3, starting transfers between devices, per_device(): came = lax.ppermute(leave, 'tm', pairs)  1.98 us
  transfers between devices with their start and end apart: 9, of which 5 were waited for; matrix products, arithmetic and copies ran while one was open for 0% of the time, Pallas kernels for 13%

profile of v6, /device:TPU:0, one launch (start us, length us, event | category | flops | bytes accessed | tf_op | source)
XLA Modules:
  0.0 54.3 jit_solution(13349149343296191162)
XLA Ops:
  0.6 8.1 %shard_map.86 = (f32[32,264,256]{2,1,0:T(8,128)S(1)}, f32[3,264,256]{2,1,0:T(8,128)S(1)}, f32[264,256]{1,0:T(8,128)S(1)}) custom-call(f32[32,64]{1,0:T(8,128)} %obs_hbm.1, f32[32,64]{1,0:T(8,128)} %weight_hbm.1, f32[32,256]{1,0:T(8,128)} %damp_hbm.1, f32[256,256]{1,0:T(8,128)} %trans_hbm.3, f32[64,256]{1,0:T(8,128)} %obsmat_hbm.1, f32[1,256]{1,0:T(1,128)} %bitcast.13), custom_call_target="tpu_custom_call" | custom-call | flops 4362076160 | bytes 1048576 | tf_op jit(solution)/shard_map/pallas_call | solution.py:331
  8.7 0.6 %collective-permute-start = (f32[264,256]{1,0:T(8,128)S(1)}, f32[264,256]{1,0:T(8,128)S(1)}, u32[]{:S(2)}, u32[]{:S(2)}) collective-permute-start(f32[264,256]{1,0:T(8,128)S(1)} %get-tuple-element.24.mine_ref), channel_id=1, source_target_pairs={{0,1},{1,0},{2,3},{3,2},{4,5},{5,4},{6,7},{7,6},{8,9},{9,8},{10,11... | collective-permute-start | bytes 811016 | tf_op jit(solution)/shard_map/ppermute | solution.py:356
  9.3 1.2 %collective-permute-done.other_ref = f32[264,256]{1,0:T(8,128)S(1)} collective-permute-done((f32[264,256]{1,0:T(8,128)S(1)}, f32[264,256]{1,0:T(8,128)S(1)}, u32[]{:S(2)}, u32[]{:S(2)}) %collective-permute-start) | collective-permute-done | bytes 270368 | tf_op jit(solution)/shard_map/ppermute | solution.py:356
  10.5 0.3 shard_map.87
  10.8 2.9 %collective-permute-start.1 = (f32[264,256]{1,0:T(8,128)S(1)}, f32[264,256]{1,0:T(8,128)S(1)}, u32[]{:S(2)}, u32[]{:S(2)}) collective-permute-start(f32[264,256]{1,0:T(8,128)S(1)} %get-tuple-element.25.chip_ref), channel_id=1, source_target_pairs={{0,2},{1,5},{2,0},{3,7},{4,6},{5,1},{6,4},{7,3},{8,10},{9,13},{10,... | collective-permute-start | bytes 811016 | tf_op jit(solution)/shard_map/ppermute | solution.py:363
  13.7 1.5 %collective-permute-start.2 = (f32[264,128]{1,0:T(8,128)S(1)}, f32[264,128]{1,0:T(8,128)S(1)}, u32[]{:S(2)}, u32[]{:S(2)}) collective-permute-start(f32[264,128]{1,0:T(8,128)S(1)} %get-tuple-element.26._), channel_id=1, source_target_pairs={{0,6},{1,7},{2,4},{3,5},{4,2},{5,3},{6,0},{7,1},{8,14},{9,15},{10,... | collective-permute-start | bytes 405512 | tf_op jit(solution)/shard_map/ppermute | solution.py:362
  15.2 5.9 %shard_map.88 = (bf16[2,256,256]{2,1,0:T(8,128)(2,1)S(1)}, bf16[10,256,256]{2,1,0:T(8,128)(2,1)S(1)}, bf16[10,256,256]{2,1,0:T(8,128)(2,1)S(1)}) custom-call(f32[256,256]{1,0:T(8,128)} %trans_hbm.3, f32[256,256]{1,0:T(8,128)} %gain_hbm.1, f32[264,128]{1,0:T(8,128)S(1)} %get-tuple-element.26._), custom_call_target="tpu_custom_call" | custom-call | flops 2013265920 | bytes 1048576 | tf_op jit(solution)/shard_map/pallas_call | solution.py:366
  21.1 1.4 %collective-permute-done.2 = f32[264,128]{1,0:T(8,128)S(1)} collective-permute-done((f32[264,128]{1,0:T(8,128)S(1)}, f32[264,128]{1,0:T(8,128)S(1)}, u32[]{:S(2)}, u32[]{:S(2)}) %collective-permute-start.2) | collective-permute-done | bytes 135200 | tf_op jit(solution)/shard_map/ppermute | solution.py:362
  22.5 0.0 collective-permute-done.1
  22.6 0.1 collective-permute-start.3
  22.7 1.7 %collective-permute-done.3.other_ref = f32[3,264,128]{2,1,0:T(8,128)S(1)} collective-permute-done((f32[3,264,128]{2,1,0:T(8,128)S(1)}, f32[3,264,128]{2,1,0:T(8,128)S(1)}, u32[]{:S(2)}, u32[]{:S(2)}) %collective-permute-start.3) | collective-permute-done | bytes 405536 | tf_op jit(solution)/shard_map/ppermute | solution.py:383
  24.4 0.9 %shard_map.89 = (f32[264,256]{1,0:T(8,128)S(1)}, f32[264,256]{1,0:T(8,128)S(1)}, f32[8,256]{1,0:T(8,128)S(1)}) custom-call(f32[264,256]{1,0:T(8,128)S(1)} %get-tuple-element.25.chip_ref, f32[3,264,128]{2,1,0:T(8,128)S(1)} %pad_maximum_fusion.mine_ref, f32[3,264,128]{2,1,0:T(8,128)S(1)} %collective-permute-done.3.other_ref, ...), custom_call_target="tpu_custom_call" | custom-call | flops 301989888 | bytes 1048576 | tf_op jit(solution)/shard_map/pallas_call | solution.py:384
  25.2 0.7 %collective-permute-start.4 = (f32[8,256]{1,0:T(8,128)S(1)}, f32[8,256]{1,0:T(8,128)S(1)}, u32[]{:S(2)}, u32[]{:S(2)}) collective-permute-start(f32[8,256]{1,0:T(8,128)S(1)} %get-tuple-element.32), channel_id=1, source_target_pairs={{1,9},{3,11},{5,13},{7,15}} | collective-permute-start | bytes 24584 | tf_op jit(solution)/shard_map/ppermute | solution.py:408
  25.9 0.0 collective-permute-done.4.came_ref
  25.9 0.3 shard_map.90
  26.2 0.7 %collective-permute-start.5 = (f32[8,256]{1,0:T(8,128)S(1)}, f32[8,256]{1,0:T(8,128)S(1)}, u32[]{:S(2)}, u32[]{:S(2)}) collective-permute-start(f32[8,256]{1,0:T(8,128)S(1)} %get-tuple-element.33), channel_id=1, source_target_pairs={{9,17},{11,19},{13,21},{15,23}} | collective-permute-start | bytes 24584 | tf_op jit(solution)/shard_map/ppermute | solution.py:408
  26.9 0.0 collective-permute-done.5.came_ref
  26.9 0.3 shard_map.91
  27.2 0.7 %collective-permute-start.6 = (f32[8,256]{1,0:T(8,128)S(1)}, f32[8,256]{1,0:T(8,128)S(1)}, u32[]{:S(2)}, u32[]{:S(2)}) collective-permute-start(f32[8,256]{1,0:T(8,128)S(1)} %get-tuple-element.35), channel_id=1, source_target_pairs={{17,25},{19,27},{21,29},{23,31}} | collective-permute-start | bytes 24584 | tf_op jit(solution)/shard_map/ppermute | solution.py:408
  27.8 0.9 %shard_map.92.entry_ref = f32[4,264,256]{2,1,0:T(8,128)S(1)} custom-call(f32[264,256]{1,0:T(8,128)S(1)} %get-tuple-element.36.before_ref, f32[264,256]{1,0:T(8,128)S(1)} %collective-permute-done.other_ref, f32[3,264,256]{2,1,0:T(8,128)S(1)} %get-tuple-element.37.chunk_ref), custom_call_target="tpu_custom_call" | custom-call | flops 402653184 | bytes 1048576 | tf_op jit(solution)/shard_map/pallas_call | solution.py:391
  28.8 1.3 %collective-permute-start.8 = (f32[8,256]{1,0:T(8,128)S(1)}, f32[8,256]{1,0:T(8,128)S(1)}, u32[]{:S(2)}, u32[]{:S(2)}) collective-permute-start(f32[8,256]{1,0:T(8,128)S(1)} %get-tuple-element.39.enter_ref), channel_id=1, source_target_pairs={{1,0},{3,2},{5,4},{7,6},{9,8},{11,10},{13,12},{15,14},{17,16},{19,... | collective-permute-start | bytes 24584 | tf_op jit(solution)/shard_map/ppermute | solution.py:411
  30.1 0.0 collective-permute-done.6.came_ref
  30.1 1.3 %collective-permute-start.7 = (f32[8,256]{1,0:T(8,128)S(1)}, f32[8,256]{1,0:T(8,128)S(1)}, u32[]{:S(2)}, u32[]{:S(2)}) collective-permute-start(f32[8,256]{1,0:T(8,128)S(1)} %collective-permute-done.6.came_ref), channel_id=1, source_target_pairs={{1,0},{3,2},{5,4},{7,6},{9,8},{11,10},{13,12},{15,14},{17,16},{19,... | collective-permute-start | bytes 24584 | tf_op jit(solution)/shard_map/ppermute | solution.py:413
  31.4 2.7 %collective-permute-done.8.enter_zero_ref = f32[8,256]{1,0:T(8,128)S(1)} collective-permute-done((f32[8,256]{1,0:T(8,128)S(1)}, f32[8,256]{1,0:T(8,128)S(1)}, u32[]{:S(2)}, u32[]{:S(2)}) %collective-permute-start.8) | collective-permute-done | bytes 8224 | tf_op jit(solution)/shard_map/ppermute | solution.py:411
  34.1 1.3 %collective-permute-done.7.came_zero_ref = f32[8,256]{1,0:T(8,128)S(1)} collective-permute-done((f32[8,256]{1,0:T(8,128)S(1)}, f32[8,256]{1,0:T(8,128)S(1)}, u32[]{:S(2)}, u32[]{:S(2)}) %collective-permute-start.7) | collective-permute-done | bytes 8224 | tf_op jit(solution)/shard_map/ppermute | solution.py:413
  35.4 2.6 %shard_map.93 = (f32[32,256]{1,0:T(8,128)}, f32[32,256]{1,0:T(8,128)S(1)}) custom-call(f32[8,256]{1,0:T(8,128)S(1)} %collective-permute-done.6.came_ref, f32[8,256]{1,0:T(8,128)S(1)} %get-tuple-element.39.enter_ref, f32[8,256]{1,0:T(8,128)S(1)} %collective-permute-done.7.came_zero_ref, f32[8,256]{1,0:T(8,128)S(1)} %collective-permute-done.8.enter_zero_ref, ...), custom_call_target="tpu_custom_call" | custom-call | flops 671088640 | bytes 1048576 | tf_op jit(solution)/shard_map/pallas_call | solution.py:414
  38.1 13.8 %all_to_all.8 = f32[32,1,256]{2,1,0:T(1,128)S(1)} all-to-all(f32[32,1,256]{2,1,0:T(1,128)S(1)} %broadcast_in_dim.13), channel_id=1, replica_groups=mesh['tm'=32,'panel'=1] {'tm'}, dimensions={0} | all-to-all | bytes 65536 | tf_op jit(solution)/shard_map/all_to_all | solution.py:421
  51.9 2.4 %shard_map.94 = f32[32,256]{1,0:T(8,128)} custom-call(f32[32,256]{1,0:T(8,128)S(1)} %bitcast.10, f32[32,256]{1,0:T(8,128)S(1)} %get-tuple-element.45.local_ref, bf16[10,256,256]{2,1,0:T(8,128)(2,1)S(1)} %get-tuple-element.42.high_ref, bf16[10,256,256]{2,1,0:T(8,128)(2,1)S(1)} %get-tuple-element.43.low_ref), custom_call_target="tpu_custom_call" | custom-call | flops 671088640 | bytes 1048576 | tf_op jit(solution)/shard_map/pallas_call | solution.py:422
  (6 shorter events, 0.1 us)
Async XLA Ops:
  8.7 1.7 %collective-permute-start = (f32[264,256]{1,0:T(8,128)S(1)}, f32[264,256]{1,0:T(8,128)S(1)}, u32[]{:S(2)}, u32[]{:S(2)}) collective-permute-start(f32[264,256]{1,0:T(8,128)S(1)} %get-tuple-element.24.mine_ref), channel_id=1, source_target_pairs={{0,1},{1,0},{2,3},{3,2},{4,5},{5,4},{6,7},{7,6},{8,9},{9,8},{10,11... | collective-permute-start | bytes 811016 | tf_op jit(solution)/shard_map/ppermute | solution.py:356
  10.8 11.7 %collective-permute-start.1 = (f32[264,256]{1,0:T(8,128)S(1)}, f32[264,256]{1,0:T(8,128)S(1)}, u32[]{:S(2)}, u32[]{:S(2)}) collective-permute-start(f32[264,256]{1,0:T(8,128)S(1)} %get-tuple-element.25.chip_ref), channel_id=1, source_target_pairs={{0,2},{1,5},{2,0},{3,7},{4,6},{5,1},{6,4},{7,3},{8,10},{9,13},{10,... | collective-permute-start | bytes 811016 | tf_op jit(solution)/shard_map/ppermute | solution.py:363
  13.7 8.8 %collective-permute-start.2 = (f32[264,128]{1,0:T(8,128)S(1)}, f32[264,128]{1,0:T(8,128)S(1)}, u32[]{:S(2)}, u32[]{:S(2)}) collective-permute-start(f32[264,128]{1,0:T(8,128)S(1)} %get-tuple-element.26._), channel_id=1, source_target_pairs={{0,6},{1,7},{2,4},{3,5},{4,2},{5,3},{6,0},{7,1},{8,14},{9,15},{10,... | collective-permute-start | bytes 405512 | tf_op jit(solution)/shard_map/ppermute | solution.py:362
  22.6 1.8 %collective-permute-start.3 = (f32[3,264,128]{2,1,0:T(8,128)S(1)}, f32[3,264,128]{2,1,0:T(8,128)S(1)}, u32[]{:S(2)}, u32[]{:S(2)}) collective-permute-start(f32[3,264,128]{2,1,0:T(8,128)S(1)} %pad_maximum_fusion.mine_ref), channel_id=1, source_target_pairs={{0,1},{1,0},{2,3},{3,2},{4,5},{5,4},{6,7},{7,6},{8,9},{9,8},{10,11... | collective-permute-start | bytes 1216520 | tf_op jit(solution)/shard_map/ppermute | solution.py:383
  25.2 0.7 %collective-permute-start.4 = (f32[8,256]{1,0:T(8,128)S(1)}, f32[8,256]{1,0:T(8,128)S(1)}, u32[]{:S(2)}, u32[]{:S(2)}) collective-permute-start(f32[8,256]{1,0:T(8,128)S(1)} %get-tuple-element.32), channel_id=1, source_target_pairs={{1,9},{3,11},{5,13},{7,15}} | collective-permute-start | bytes 24584 | tf_op jit(solution)/shard_map/ppermute | solution.py:408
  26.2 0.7 %collective-permute-start.5 = (f32[8,256]{1,0:T(8,128)S(1)}, f32[8,256]{1,0:T(8,128)S(1)}, u32[]{:S(2)}, u32[]{:S(2)}) collective-permute-start(f32[8,256]{1,0:T(8,128)S(1)} %get-tuple-element.33), channel_id=1, source_target_pairs={{9,17},{11,19},{13,21},{15,23}} | collective-permute-start | bytes 24584 | tf_op jit(solution)/shard_map/ppermute | solution.py:408
  27.2 2.9 %collective-permute-start.6 = (f32[8,256]{1,0:T(8,128)S(1)}, f32[8,256]{1,0:T(8,128)S(1)}, u32[]{:S(2)}, u32[]{:S(2)}) collective-permute-start(f32[8,256]{1,0:T(8,128)S(1)} %get-tuple-element.35), channel_id=1, source_target_pairs={{17,25},{19,27},{21,29},{23,31}} | collective-permute-start | bytes 24584 | tf_op jit(solution)/shard_map/ppermute | solution.py:408
  28.8 5.3 %collective-permute-start.8 = (f32[8,256]{1,0:T(8,128)S(1)}, f32[8,256]{1,0:T(8,128)S(1)}, u32[]{:S(2)}, u32[]{:S(2)}) collective-permute-start(f32[8,256]{1,0:T(8,128)S(1)} %get-tuple-element.39.enter_ref), channel_id=1, source_target_pairs={{1,0},{3,2},{5,4},{7,6},{9,8},{11,10},{13,12},{15,14},{17,16},{19,... | collective-permute-start | bytes 24584 | tf_op jit(solution)/shard_map/ppermute | solution.py:411
  30.1 5.3 %collective-permute-start.7 = (f32[8,256]{1,0:T(8,128)S(1)}, f32[8,256]{1,0:T(8,128)S(1)}, u32[]{:S(2)}, u32[]{:S(2)}) collective-permute-start(f32[8,256]{1,0:T(8,128)S(1)} %collective-permute-done.6.came_ref), channel_id=1, source_target_pairs={{1,0},{3,2},{5,4},{7,6},{9,8},{11,10},{13,12},{15,14},{17,16},{19,... | collective-permute-start | bytes 24584 | tf_op jit(solution)/shard_map/ppermute | solution.py:413

commit v7 on v6

--- a/solution.py
+++ b/solution.py
@@ -393,7 +393,7 @@
     )
 
     enter = jnp.zeros((PAD, width), f32)
-    came = enter
+    came = came_zero = enter
     hops = count // PLANE - 1
     for hop in range(hops):
         if hop > 0:
@@ -405,12 +405,13 @@
             )(plane, came, enter)
         low, high = hop * PLANE, (hop + 1) * PLANE
         pairs = [(low + i, high + i) for i in range(1, PLANE, 2)]
+        if hop == hops - 1:
+            across = [(source, target - 1) for source, target in pairs]
+            came_zero = lax.ppermute(leave, "tm", across)
         came = lax.ppermute(leave, "tm", pairs)
 
     to_zero = [(index, index - 1) for index in range(1, count, 2)]
     enter_zero = lax.ppermute(enter, "tm", to_zero)
-    came, entry = lax.optimization_barrier((came, entry))
-    came_zero = lax.ppermute(came, "tm", to_zero)
     filtered, local = call(
         functools.partial(filter_kernel, levels=levels, hop=hops),
         (struct(steps, width), struct(steps, width)),

time: 54.6 us -> 54 us (0.989)
  blocking collectives: 13.8 us -> 14.9 us
  waiting for transfers between devices: 8.33 us -> 7.36 us
  starting transfers between devices: 9.61 us -> 8.98 us
    ppermute x1, waiting for transfers between devices: 1.31 us -> 0.01 us  [per_device(): came_zero = lax.ppermute(leave, 'tm', across)]
    all_to_all x1, blocking collectives: 13.8 us -> 14.9 us  [per_device(): offsets = lax.all_to_all(sent, 'tm', 0, 0, tiled=True)]
    ppermute x1, starting transfers between devices: 1.29 us -> 0.66 us  [per_device(): came_zero = lax.ppermute(leave, 'tm', across)]
  transfers between devices with their start and end apart: 9 -> 9, of which waited for: 5 -> 4; matrix products, arithmetic and copies ran while one was open for 0% -> 0% of each run, Pallas kernels for 13% -> 13%
where the time goes in v7:
time: 54 us; the launch traced here: 53.8 us
  Pallas kernels  21.7 us (40%)
  blocking collectives  14.9 us (28%)
  starting transfers between devices  8.98 us (17%)
  waiting for transfers between devices  7.36 us (14%)
  between operations  0.77 us (1%)
    all_to_all x1, blocking collectives, per_device(): offsets = lax.all_to_all(sent, 'tm', 0, 0, tiled=True)  14.9 us
    pallas_call x1, Pallas kernels, per_device(): call(local_kernel, (struct(steps, rows, width), struct(CHUNKS - 1, rows,...  8.08 us
    pallas_call x1, Pallas kernels, per_device(): call(power_kernel, (struct(2, width, width, dtype=bf16), struct(power_cou...  5.95 us
    ppermute x1, waiting for transfers between devices, per_device(): enter_zero = lax.ppermute(enter, 'tm', to_zero)  3.08 us
    ppermute x1, starting transfers between devices, per_device(): whole = lax.ppermute(chip, 'tm', straight)  2.91 us
    pallas_call x1, Pallas kernels, per_device(): call(functools.partial(filter_kernel, levels=levels, hop=hops), (struct(s...  2.63 us
    pallas_call x1, Pallas kernels, per_device(): call(functools.partial(smooth_kernel, levels=levels), struct(steps, width...  2.45 us
    ppermute x3, starting transfers between devices, per_device(): came = lax.ppermute(leave, 'tm', pairs)  1.98 us
  transfers between devices with their start and end apart: 9, of which 4 were waited for; matrix products, arithmetic and copies ran while one was open for 0% of the time, Pallas kernels for 13%

profile of v7, /device:TPU:0, one launch (start us, length us, event | category | flops | bytes accessed | tf_op | source)
XLA Modules:
  0.0 53.8 jit_solution(12282882586338282123)
XLA Ops:
  0.6 8.1 %shard_map.86 = (f32[32,264,256]{2,1,0:T(8,128)S(1)}, f32[3,264,256]{2,1,0:T(8,128)S(1)}, f32[264,256]{1,0:T(8,128)S(1)}) custom-call(f32[32,64]{1,0:T(8,128)} %obs_hbm.1, f32[32,64]{1,0:T(8,128)} %weight_hbm.1, f32[32,256]{1,0:T(8,128)} %damp_hbm.1, f32[256,256]{1,0:T(8,128)} %trans_hbm.3, f32[64,256]{1,0:T(8,128)} %obsmat_hbm.1, f32[1,256]{1,0:T(1,128)} %bitcast.13), custom_call_target="tpu_custom_call" | custom-call | flops 4362076160 | bytes 1048576 | tf_op jit(solution)/shard_map/pallas_call | solution.py:331
  8.7 0.6 %collective-permute-start = (f32[264,256]{1,0:T(8,128)S(1)}, f32[264,256]{1,0:T(8,128)S(1)}, u32[]{:S(2)}, u32[]{:S(2)}) collective-permute-start(f32[264,256]{1,0:T(8,128)S(1)} %get-tuple-element.22.mine_ref), channel_id=1, source_target_pairs={{0,1},{1,0},{2,3},{3,2},{4,5},{5,4},{6,7},{7,6},{8,9},{9,8},{10,11... | collective-permute-start | bytes 811016 | tf_op jit(solution)/shard_map/ppermute | solution.py:356
  9.3 1.2 %collective-permute-done.other_ref = f32[264,256]{1,0:T(8,128)S(1)} collective-permute-done((f32[264,256]{1,0:T(8,128)S(1)}, f32[264,256]{1,0:T(8,128)S(1)}, u32[]{:S(2)}, u32[]{:S(2)}) %collective-permute-start) | collective-permute-done | bytes 270368 | tf_op jit(solution)/shard_map/ppermute | solution.py:356
  10.5 0.3 shard_map.87
  10.8 2.9 %collective-permute-start.1 = (f32[264,256]{1,0:T(8,128)S(1)}, f32[264,256]{1,0:T(8,128)S(1)}, u32[]{:S(2)}, u32[]{:S(2)}) collective-permute-start(f32[264,256]{1,0:T(8,128)S(1)} %get-tuple-element.23.chip_ref), channel_id=1, source_target_pairs={{0,2},{1,5},{2,0},{3,7},{4,6},{5,1},{6,4},{7,3},{8,10},{9,13},{10,... | collective-permute-start | bytes 811016 | tf_op jit(solution)/shard_map/ppermute | solution.py:363
  13.7 1.5 %collective-permute-start.2 = (f32[264,128]{1,0:T(8,128)S(1)}, f32[264,128]{1,0:T(8,128)S(1)}, u32[]{:S(2)}, u32[]{:S(2)}) collective-permute-start(f32[264,128]{1,0:T(8,128)S(1)} %get-tuple-element.24._), channel_id=1, source_target_pairs={{0,6},{1,7},{2,4},{3,5},{4,2},{5,3},{6,0},{7,1},{8,14},{9,15},{10,... | collective-permute-start | bytes 405512 | tf_op jit(solution)/shard_map/ppermute | solution.py:362
  15.2 5.9 %shard_map.88 = (bf16[2,256,256]{2,1,0:T(8,128)(2,1)S(1)}, bf16[10,256,256]{2,1,0:T(8,128)(2,1)S(1)}, bf16[10,256,256]{2,1,0:T(8,128)(2,1)S(1)}) custom-call(f32[256,256]{1,0:T(8,128)} %trans_hbm.3, f32[256,256]{1,0:T(8,128)} %gain_hbm.1, f32[264,128]{1,0:T(8,128)S(1)} %get-tuple-element.24._), custom_call_target="tpu_custom_call" | custom-call | flops 2013265920 | bytes 1048576 | tf_op jit(solution)/shard_map/pallas_call | solution.py:366
  21.1 1.4 %collective-permute-done.2 = f32[264,128]{1,0:T(8,128)S(1)} collective-permute-done((f32[264,128]{1,0:T(8,128)S(1)}, f32[264,128]{1,0:T(8,128)S(1)}, u32[]{:S(2)}, u32[]{:S(2)}) %collective-permute-start.2) | collective-permute-done | bytes 135200 | tf_op jit(solution)/shard_map/ppermute | solution.py:362
  22.5 0.0 collective-permute-done.1
  22.6 0.1 collective-permute-start.3
  22.7 1.7 %collective-permute-done.3.other_ref = f32[3,264,128]{2,1,0:T(8,128)S(1)} collective-permute-done((f32[3,264,128]{2,1,0:T(8,128)S(1)}, f32[3,264,128]{2,1,0:T(8,128)S(1)}, u32[]{:S(2)}, u32[]{:S(2)}) %collective-permute-start.3) | collective-permute-done | bytes 405536 | tf_op jit(solution)/shard_map/ppermute | solution.py:383
  24.4 0.9 %shard_map.89 = (f32[264,256]{1,0:T(8,128)S(1)}, f32[264,256]{1,0:T(8,128)S(1)}, f32[8,256]{1,0:T(8,128)S(1)}) custom-call(f32[264,256]{1,0:T(8,128)S(1)} %get-tuple-element.23.chip_ref, f32[3,264,128]{2,1,0:T(8,128)S(1)} %pad_maximum_fusion.mine_ref, f32[3,264,128]{2,1,0:T(8,128)S(1)} %collective-permute-done.3.other_ref, ...), custom_call_target="tpu_custom_call" | custom-call | flops 301989888 | bytes 1048576 | tf_op jit(solution)/shard_map/pallas_call | solution.py:384
  25.2 0.7 %collective-permute-start.4 = (f32[8,256]{1,0:T(8,128)S(1)}, f32[8,256]{1,0:T(8,128)S(1)}, u32[]{:S(2)}, u32[]{:S(2)}) collective-permute-start(f32[8,256]{1,0:T(8,128)S(1)} %get-tuple-element.30), channel_id=1, source_target_pairs={{1,9},{3,11},{5,13},{7,15}} | collective-permute-start | bytes 24584 | tf_op jit(solution)/shard_map/ppermute | solution.py:411
  25.9 0.0 collective-permute-done.4.came_ref
  25.9 0.3 shard_map.90
  26.2 0.7 %collective-permute-start.5 = (f32[8,256]{1,0:T(8,128)S(1)}, f32[8,256]{1,0:T(8,128)S(1)}, u32[]{:S(2)}, u32[]{:S(2)}) collective-permute-start(f32[8,256]{1,0:T(8,128)S(1)} %get-tuple-element.31), channel_id=1, source_target_pairs={{9,17},{11,19},{13,21},{15,23}} | collective-permute-start | bytes 24584 | tf_op jit(solution)/shard_map/ppermute | solution.py:411
  26.9 0.0 collective-permute-done.5.came_ref
  26.9 0.3 shard_map.91
  27.2 0.7 %collective-permute-start.6 = (f32[8,256]{1,0:T(8,128)S(1)}, f32[8,256]{1,0:T(8,128)S(1)}, u32[]{:S(2)}, u32[]{:S(2)}) collective-permute-start(f32[8,256]{1,0:T(8,128)S(1)} %get-tuple-element.33), channel_id=1, source_target_pairs={{17,25},{19,27},{21,29},{23,31}} | collective-permute-start | bytes 24584 | tf_op jit(solution)/shard_map/ppermute | solution.py:411
  27.8 0.7 %collective-permute-start.7 = (f32[8,256]{1,0:T(8,128)S(1)}, f32[8,256]{1,0:T(8,128)S(1)}, u32[]{:S(2)}, u32[]{:S(2)}) collective-permute-start(f32[8,256]{1,0:T(8,128)S(1)} %get-tuple-element.33), channel_id=1, source_target_pairs={{17,24},{19,26},{21,28},{23,30}} | collective-permute-start | bytes 24584 | tf_op jit(solution)/shard_map/ppermute | solution.py:410
  28.5 1.3 %collective-permute-start.8 = (f32[8,256]{1,0:T(8,128)S(1)}, f32[8,256]{1,0:T(8,128)S(1)}, u32[]{:S(2)}, u32[]{:S(2)}) collective-permute-start(f32[8,256]{1,0:T(8,128)S(1)} %get-tuple-element.34.enter_ref), channel_id=1, source_target_pairs={{1,0},{3,2},{5,4},{7,6},{9,8},{11,10},{13,12},{15,14},{17,16},{19,... | collective-permute-start | bytes 24584 | tf_op jit(solution)/shard_map/ppermute | solution.py:414
  29.8 0.9 %shard_map.92.entry_ref = f32[4,264,256]{2,1,0:T(8,128)S(1)} custom-call(f32[264,256]{1,0:T(8,128)S(1)} %get-tuple-element.35.before_ref, f32[264,256]{1,0:T(8,128)S(1)} %collective-permute-done.other_ref, f32[3,264,256]{2,1,0:T(8,128)S(1)} %get-tuple-element.36.chunk_ref), custom_call_target="tpu_custom_call" | custom-call | flops 402653184 | bytes 1048576 | tf_op jit(solution)/shard_map/pallas_call | solution.py:391
  30.7 0.0 collective-permute-done.6.came_ref
  30.8 0.0 collective-permute-done.7.came_zero_ref
  30.8 3.1 %collective-permute-done.8.enter_zero_ref = f32[8,256]{1,0:T(8,128)S(1)} collective-permute-done((f32[8,256]{1,0:T(8,128)S(1)}, f32[8,256]{1,0:T(8,128)S(1)}, u32[]{:S(2)}, u32[]{:S(2)}) %collective-permute-start.8) | collective-permute-done | bytes 8224 | tf_op jit(solution)/shard_map/ppermute | solution.py:414
  33.8 2.6 %shard_map.93 = (f32[32,256]{1,0:T(8,128)}, f32[32,256]{1,0:T(8,128)S(1)}) custom-call(f32[8,256]{1,0:T(8,128)S(1)} %collective-permute-done.6.came_ref, f32[8,256]{1,0:T(8,128)S(1)} %get-tuple-element.34.enter_ref, f32[8,256]{1,0:T(8,128)S(1)} %collective-permute-done.7.came_zero_ref, f32[8,256]{1,0:T(8,128)S(1)} %collective-permute-done.8.enter_zero_ref, ...), custom_call_target="tpu_custom_call" | custom-call | flops 671088640 | bytes 1048576 | tf_op jit(solution)/shard_map/pallas_call | solution.py:415
  36.5 14.9 %all_to_all.8 = f32[32,1,256]{2,1,0:T(1,128)S(1)} all-to-all(f32[32,1,256]{2,1,0:T(1,128)S(1)} %broadcast_in_dim.13), channel_id=1, replica_groups=mesh['tm'=32,'panel'=1] {'tm'}, dimensions={0} | all-to-all | bytes 65536 | tf_op jit(solution)/shard_map/all_to_all | solution.py:422
  51.4 2.4 %shard_map.94 = f32[32,256]{1,0:T(8,128)} custom-call(f32[32,256]{1,0:T(8,128)S(1)} %bitcast.10, f32[32,256]{1,0:T(8,128)S(1)} %get-tuple-element.41.local_ref, bf16[10,256,256]{2,1,0:T(8,128)(2,1)S(1)} %get-tuple-element.38.high_ref, bf16[10,256,256]{2,1,0:T(8,128)(2,1)S(1)} %get-tuple-element.39.low_ref), custom_call_target="tpu_custom_call" | custom-call | flops 671088640 | bytes 1048576 | tf_op jit(solution)/shard_map/pallas_call | solution.py:423
  (6 shorter events, 0.1 us)
Async XLA Ops:
  8.7 1.7 %collective-permute-start = (f32[264,256]{1,0:T(8,128)S(1)}, f32[264,256]{1,0:T(8,128)S(1)}, u32[]{:S(2)}, u32[]{:S(2)}) collective-permute-start(f32[264,256]{1,0:T(8,128)S(1)} %get-tuple-element.22.mine_ref), channel_id=1, source_target_pairs={{0,1},{1,0},{2,3},{3,2},{4,5},{5,4},{6,7},{7,6},{8,9},{9,8},{10,11... | collective-permute-start | bytes 811016 | tf_op jit(solution)/shard_map/ppermute | solution.py:356
  10.8 11.7 %collective-permute-start.1 = (f32[264,256]{1,0:T(8,128)S(1)}, f32[264,256]{1,0:T(8,128)S(1)}, u32[]{:S(2)}, u32[]{:S(2)}) collective-permute-start(f32[264,256]{1,0:T(8,128)S(1)} %get-tuple-element.23.chip_ref), channel_id=1, source_target_pairs={{0,2},{1,5},{2,0},{3,7},{4,6},{5,1},{6,4},{7,3},{8,10},{9,13},{10,... | collective-permute-start | bytes 811016 | tf_op jit(solution)/shard_map/ppermute | solution.py:363
  13.7 8.8 %collective-permute-start.2 = (f32[264,128]{1,0:T(8,128)S(1)}, f32[264,128]{1,0:T(8,128)S(1)}, u32[]{:S(2)}, u32[]{:S(2)}) collective-permute-start(f32[264,128]{1,0:T(8,128)S(1)} %get-tuple-element.24._), channel_id=1, source_target_pairs={{0,6},{1,7},{2,4},{3,5},{4,2},{5,3},{6,0},{7,1},{8,14},{9,15},{10,... | collective-permute-start | bytes 405512 | tf_op jit(solution)/shard_map/ppermute | solution.py:362
  22.6 1.8 %collective-permute-start.3 = (f32[3,264,128]{2,1,0:T(8,128)S(1)}, f32[3,264,128]{2,1,0:T(8,128)S(1)}, u32[]{:S(2)}, u32[]{:S(2)}) collective-permute-start(f32[3,264,128]{2,1,0:T(8,128)S(1)} %pad_maximum_fusion.mine_ref), channel_id=1, source_target_pairs={{0,1},{1,0},{2,3},{3,2},{4,5},{5,4},{6,7},{7,6},{8,9},{9,8},{10,11... | collective-permute-start | bytes 1216520 | tf_op jit(solution)/shard_map/ppermute | solution.py:383
  25.2 0.7 %collective-permute-start.4 = (f32[8,256]{1,0:T(8,128)S(1)}, f32[8,256]{1,0:T(8,128)S(1)}, u32[]{:S(2)}, u32[]{:S(2)}) collective-permute-start(f32[8,256]{1,0:T(8,128)S(1)} %get-tuple-element.30), channel_id=1, source_target_pairs={{1,9},{3,11},{5,13},{7,15}} | collective-permute-start | bytes 24584 | tf_op jit(solution)/shard_map/ppermute | solution.py:411
  26.2 0.7 %collective-permute-start.5 = (f32[8,256]{1,0:T(8,128)S(1)}, f32[8,256]{1,0:T(8,128)S(1)}, u32[]{:S(2)}, u32[]{:S(2)}) collective-permute-start(f32[8,256]{1,0:T(8,128)S(1)} %get-tuple-element.31), channel_id=1, source_target_pairs={{9,17},{11,19},{13,21},{15,23}} | collective-permute-start | bytes 24584 | tf_op jit(solution)/shard_map/ppermute | solution.py:411
  27.2 3.6 %collective-permute-start.6 = (f32[8,256]{1,0:T(8,128)S(1)}, f32[8,256]{1,0:T(8,128)S(1)}, u32[]{:S(2)}, u32[]{:S(2)}) collective-permute-start(f32[8,256]{1,0:T(8,128)S(1)} %get-tuple-element.33), channel_id=1, source_target_pairs={{17,25},{19,27},{21,29},{23,31}} | collective-permute-start | bytes 24584 | tf_op jit(solution)/shard_map/ppermute | solution.py:411
  27.8 2.9 %collective-permute-start.7 = (f32[8,256]{1,0:T(8,128)S(1)}, f32[8,256]{1,0:T(8,128)S(1)}, u32[]{:S(2)}, u32[]{:S(2)}) collective-permute-start(f32[8,256]{1,0:T(8,128)S(1)} %get-tuple-element.33), channel_id=1, source_target_pairs={{17,24},{19,26},{21,28},{23,30}} | collective-permute-start | bytes 24584 | tf_op jit(solution)/shard_map/ppermute | solution.py:410
  28.5 5.3 %collective-permute-start.8 = (f32[8,256]{1,0:T(8,128)S(1)}, f32[8,256]{1,0:T(8,128)S(1)}, u32[]{:S(2)}, u32[]{:S(2)}) collective-permute-start(f32[8,256]{1,0:T(8,128)S(1)} %get-tuple-element.34.enter_ref), channel_id=1, source_target_pairs={{1,0},{3,2},{5,4},{7,6},{9,8},{11,10},{13,12},{15,14},{17,16},{19,... | collective-permute-start | bytes 24584 | tf_op jit(solution)/shard_map/ppermute | solution.py:414

commit v8 on v7

--- a/solution.py
+++ b/solution.py
@@ -287,10 +287,12 @@
         all_ref[...], high_ref, low_ref, levels, (count - 1).bit_length()
     )
     incoming = jnp.broadcast_to(sum_ref[pl.ds(me + 1, 1), :], (PAD, width))
-    lifted = dot_few(incoming, high_ref[0], low_ref[0])[0:1]
     step_ids = lax.broadcasted_iota(jnp.int32, (steps, 1), 0)
-    rows = jnp.where(step_ids == steps - 1, lifted, 0.0)
-    out_ref[...] = local_ref[...] + suffix_scan(rows, high_ref, low_ref, 0, levels)
+    after = jnp.where(step_ids[:PAD] == 0, incoming, 0.0)
+    rows = jnp.concatenate([jnp.zeros((steps, width), f32), after], axis=0)
+    lifted = suffix_scan(rows, high_ref, low_ref, 0, levels)[:steps]
+    start = sum_ref[pl.ds(me, 1), :]
+    out_ref[...] = jnp.where(step_ids == 0, start, local_ref[...] + lifted)
 
 
 def call(kernel, outs, scratch=(), flops=0, limit=8, spaces=None):

time: 54 us -> 53.9 us (level)
  no operation moved by 1% of the time
where the time goes in v8:
time: 53.9 us; the launch traced here: 53.7 us
  Pallas kernels  21.6 us (40%)
  blocking collectives  14.9 us (28%)
  starting transfers between devices  8.98 us (17%)
  waiting for transfers between devices  7.36 us (14%)
  between operations  0.77 us (1%)
    all_to_all x1, blocking collectives, per_device(): offsets = lax.all_to_all(sent, 'tm', 0, 0, tiled=True)  14.9 us
    pallas_call x1, Pallas kernels, per_device(): call(local_kernel, (struct(steps, rows, width), struct(CHUNKS - 1, rows,...  8.08 us
    pallas_call x1, Pallas kernels, per_device(): call(power_kernel, (struct(2, width, width, dtype=bf16), struct(power_cou...  5.95 us
    ppermute x1, waiting for transfers between devices, per_device(): enter_zero = lax.ppermute(enter, 'tm', to_zero)  3.08 us
    ppermute x1, starting transfers between devices, per_device(): whole = lax.ppermute(chip, 'tm', straight)  2.91 us
    pallas_call x1, Pallas kernels, per_device(): call(functools.partial(filter_kernel, levels=levels, hop=hops), (struct(s...  2.63 us
    pallas_call x1, Pallas kernels, per_device(): call(functools.partial(smooth_kernel, levels=levels), struct(steps, width...  2.33 us
    ppermute x3, starting transfers between devices, per_device(): came = lax.ppermute(leave, 'tm', pairs)  1.98 us
  transfers between devices with their start and end apart: 9, of which 4 were waited for; matrix products, arithmetic and copies ran while one was open for 0% of the time, Pallas kernels for 13%

profile of v8, /device:TPU:0, one launch (start us, length us, event | category | flops | bytes accessed | tf_op | source)
XLA Modules:
  0.0 53.7 jit_solution(10016977395944022562)
XLA Ops:
  0.6 8.1 %shard_map.86 = (f32[32,264,256]{2,1,0:T(8,128)S(1)}, f32[3,264,256]{2,1,0:T(8,128)S(1)}, f32[264,256]{1,0:T(8,128)S(1)}) custom-call(f32[32,64]{1,0:T(8,128)} %obs_hbm.1, f32[32,64]{1,0:T(8,128)} %weight_hbm.1, f32[32,256]{1,0:T(8,128)} %damp_hbm.1, f32[256,256]{1,0:T(8,128)} %trans_hbm.3, f32[64,256]{1,0:T(8,128)} %obsmat_hbm.1, f32[1,256]{1,0:T(1,128)} %bitcast.13), custom_call_target="tpu_custom_call" | custom-call | flops 4362076160 | bytes 1048576 | tf_op jit(solution)/shard_map/pallas_call | solution.py:333
  8.7 0.6 %collective-permute-start = (f32[264,256]{1,0:T(8,128)S(1)}, f32[264,256]{1,0:T(8,128)S(1)}, u32[]{:S(2)}, u32[]{:S(2)}) collective-permute-start(f32[264,256]{1,0:T(8,128)S(1)} %get-tuple-element.22.mine_ref), channel_id=1, source_target_pairs={{0,1},{1,0},{2,3},{3,2},{4,5},{5,4},{6,7},{7,6},{8,9},{9,8},{10,11... | collective-permute-start | bytes 811016 | tf_op jit(solution)/shard_map/ppermute | solution.py:358
  9.3 1.2 %collective-permute-done.other_ref = f32[264,256]{1,0:T(8,128)S(1)} collective-permute-done((f32[264,256]{1,0:T(8,128)S(1)}, f32[264,256]{1,0:T(8,128)S(1)}, u32[]{:S(2)}, u32[]{:S(2)}) %collective-permute-start) | collective-permute-done | bytes 270368 | tf_op jit(solution)/shard_map/ppermute | solution.py:358
  10.5 0.3 shard_map.87
  10.8 2.9 %collective-permute-start.1 = (f32[264,256]{1,0:T(8,128)S(1)}, f32[264,256]{1,0:T(8,128)S(1)}, u32[]{:S(2)}, u32[]{:S(2)}) collective-permute-start(f32[264,256]{1,0:T(8,128)S(1)} %get-tuple-element.23.chip_ref), channel_id=1, source_target_pairs={{0,2},{1,5},{2,0},{3,7},{4,6},{5,1},{6,4},{7,3},{8,10},{9,13},{10,... | collective-permute-start | bytes 811016 | tf_op jit(solution)/shard_map/ppermute | solution.py:365
  13.7 1.5 %collective-permute-start.2 = (f32[264,128]{1,0:T(8,128)S(1)}, f32[264,128]{1,0:T(8,128)S(1)}, u32[]{:S(2)}, u32[]{:S(2)}) collective-permute-start(f32[264,128]{1,0:T(8,128)S(1)} %get-tuple-element.24._), channel_id=1, source_target_pairs={{0,6},{1,7},{2,4},{3,5},{4,2},{5,3},{6,0},{7,1},{8,14},{9,15},{10,... | collective-permute-start | bytes 405512 | tf_op jit(solution)/shard_map/ppermute | solution.py:364
  15.2 5.9 %shard_map.88 = (bf16[2,256,256]{2,1,0:T(8,128)(2,1)S(1)}, bf16[10,256,256]{2,1,0:T(8,128)(2,1)S(1)}, bf16[10,256,256]{2,1,0:T(8,128)(2,1)S(1)}) custom-call(f32[256,256]{1,0:T(8,128)} %trans_hbm.3, f32[256,256]{1,0:T(8,128)} %gain_hbm.1, f32[264,128]{1,0:T(8,128)S(1)} %get-tuple-element.24._), custom_call_target="tpu_custom_call" | custom-call | flops 2013265920 | bytes 1048576 | tf_op jit(solution)/shard_map/pallas_call | solution.py:368
  21.1 1.4 %collective-permute-done.2 = f32[264,128]{1,0:T(8,128)S(1)} collective-permute-done((f32[264,128]{1,0:T(8,128)S(1)}, f32[264,128]{1,0:T(8,128)S(1)}, u32[]{:S(2)}, u32[]{:S(2)}) %collective-permute-start.2) | collective-permute-done | bytes 135200 | tf_op jit(solution)/shard_map/ppermute | solution.py:364
  22.5 0.0 collective-permute-done.1
  22.6 0.1 collective-permute-start.3
  22.7 1.7 %collective-permute-done.3.other_ref = f32[3,264,128]{2,1,0:T(8,128)S(1)} collective-permute-done((f32[3,264,128]{2,1,0:T(8,128)S(1)}, f32[3,264,128]{2,1,0:T(8,128)S(1)}, u32[]{:S(2)}, u32[]{:S(2)}) %collective-permute-start.3) | collective-permute-done | bytes 405536 | tf_op jit(solution)/shard_map/ppermute | solution.py:385
  24.4 0.9 %shard_map.89 = (f32[264,256]{1,0:T(8,128)S(1)}, f32[264,256]{1,0:T(8,128)S(1)}, f32[8,256]{1,0:T(8,128)S(1)}) custom-call(f32[264,256]{1,0:T(8,128)S(1)} %get-tuple-element.23.chip_ref, f32[3,264,128]{2,1,0:T(8,128)S(1)} %pad_maximum_fusion.mine_ref, f32[3,264,128]{2,1,0:T(8,128)S(1)} %collective-permute-done.3.other_ref, ...), custom_call_target="tpu_custom_call" | custom-call | flops 301989888 | bytes 1048576 | tf_op jit(solution)/shard_map/pallas_call | solution.py:386
  25.2 0.7 %collective-permute-start.4 = (f32[8,256]{1,0:T(8,128)S(1)}, f32[8,256]{1,0:T(8,128)S(1)}, u32[]{:S(2)}, u32[]{:S(2)}) collective-permute-start(f32[8,256]{1,0:T(8,128)S(1)} %get-tuple-element.30), channel_id=1, source_target_pairs={{1,9},{3,11},{5,13},{7,15}} | collective-permute-start | bytes 24584 | tf_op jit(solution)/shard_map/ppermute | solution.py:413
  25.9 0.0 collective-permute-done.4.came_ref
  25.9 0.3 shard_map.90
  26.2 0.7 %collective-permute-start.5 = (f32[8,256]{1,0:T(8,128)S(1)}, f32[8,256]{1,0:T(8,128)S(1)}, u32[]{:S(2)}, u32[]{:S(2)}) collective-permute-start(f32[8,256]{1,0:T(8,128)S(1)} %get-tuple-element.31), channel_id=1, source_target_pairs={{9,17},{11,19},{13,21},{15,23}} | collective-permute-start | bytes 24584 | tf_op jit(solution)/shard_map/ppermute | solution.py:413
  26.9 0.0 collective-permute-done.5.came_ref
  26.9 0.3 shard_map.91
  27.2 0.7 %collective-permute-start.6 = (f32[8,256]{1,0:T(8,128)S(1)}, f32[8,256]{1,0:T(8,128)S(1)}, u32[]{:S(2)}, u32[]{:S(2)}) collective-permute-start(f32[8,256]{1,0:T(8,128)S(1)} %get-tuple-element.33), channel_id=1, source_target_pairs={{17,25},{19,27},{21,29},{23,31}} | collective-permute-start | bytes 24584 | tf_op jit(solution)/shard_map/ppermute | solution.py:413
  27.8 0.7 %collective-permute-start.7 = (f32[8,256]{1,0:T(8,128)S(1)}, f32[8,256]{1,0:T(8,128)S(1)}, u32[]{:S(2)}, u32[]{:S(2)}) collective-permute-start(f32[8,256]{1,0:T(8,128)S(1)} %get-tuple-element.33), channel_id=1, source_target_pairs={{17,24},{19,26},{21,28},{23,30}} | collective-permute-start | bytes 24584 | tf_op jit(solution)/shard_map/ppermute | solution.py:412
  28.5 1.3 %collective-permute-start.8 = (f32[8,256]{1,0:T(8,128)S(1)}, f32[8,256]{1,0:T(8,128)S(1)}, u32[]{:S(2)}, u32[]{:S(2)}) collective-permute-start(f32[8,256]{1,0:T(8,128)S(1)} %get-tuple-element.34.enter_ref), channel_id=1, source_target_pairs={{1,0},{3,2},{5,4},{7,6},{9,8},{11,10},{13,12},{15,14},{17,16},{19,... | collective-permute-start | bytes 24584 | tf_op jit(solution)/shard_map/ppermute | solution.py:416
  29.8 0.9 %shard_map.92.entry_ref = f32[4,264,256]{2,1,0:T(8,128)S(1)} custom-call(f32[264,256]{1,0:T(8,128)S(1)} %get-tuple-element.35.before_ref, f32[264,256]{1,0:T(8,128)S(1)} %collective-permute-done.other_ref, f32[3,264,256]{2,1,0:T(8,128)S(1)} %get-tuple-element.36.chunk_ref), custom_call_target="tpu_custom_call" | custom-call | flops 402653184 | bytes 1048576 | tf_op jit(solution)/shard_map/pallas_call | solution.py:393
  30.7 0.0 collective-permute-done.6.came_ref
  30.8 0.0 collective-permute-done.7.came_zero_ref
  30.8 3.1 %collective-permute-done.8.enter_zero_ref = f32[8,256]{1,0:T(8,128)S(1)} collective-permute-done((f32[8,256]{1,0:T(8,128)S(1)}, f32[8,256]{1,0:T(8,128)S(1)}, u32[]{:S(2)}, u32[]{:S(2)}) %collective-permute-start.8) | collective-permute-done | bytes 8224 | tf_op jit(solution)/shard_map/ppermute | solution.py:416
  33.8 2.6 %shard_map.93 = (f32[32,256]{1,0:T(8,128)}, f32[32,256]{1,0:T(8,128)S(1)}) custom-call(f32[8,256]{1,0:T(8,128)S(1)} %collective-permute-done.6.came_ref, f32[8,256]{1,0:T(8,128)S(1)} %get-tuple-element.34.enter_ref, f32[8,256]{1,0:T(8,128)S(1)} %collective-permute-done.7.came_zero_ref, f32[8,256]{1,0:T(8,128)S(1)} %collective-permute-done.8.enter_zero_ref, ...), custom_call_target="tpu_custom_call" | custom-call | flops 671088640 | bytes 1048576 | tf_op jit(solution)/shard_map/pallas_call | solution.py:417
  36.5 14.9 %all_to_all.8 = f32[32,1,256]{2,1,0:T(1,128)S(1)} all-to-all(f32[32,1,256]{2,1,0:T(1,128)S(1)} %broadcast_in_dim.13), channel_id=1, replica_groups=mesh['tm'=32,'panel'=1] {'tm'}, dimensions={0} | all-to-all | bytes 65536 | tf_op jit(solution)/shard_map/all_to_all | solution.py:424
  51.4 2.3 %shard_map.94 = f32[32,256]{1,0:T(8,128)} custom-call(f32[32,256]{1,0:T(8,128)S(1)} %bitcast.10, f32[32,256]{1,0:T(8,128)S(1)} %get-tuple-element.41.local_ref, bf16[10,256,256]{2,1,0:T(8,128)(2,1)S(1)} %get-tuple-element.38.high_ref, bf16[10,256,256]{2,1,0:T(8,128)(2,1)S(1)} %get-tuple-element.39.low_ref), custom_call_target="tpu_custom_call" | custom-call | flops 671088640 | bytes 1048576 | tf_op jit(solution)/shard_map/pallas_call | solution.py:425
  (6 shorter events, 0.1 us)
Async XLA Ops:
  8.7 1.7 %collective-permute-start = (f32[264,256]{1,0:T(8,128)S(1)}, f32[264,256]{1,0:T(8,128)S(1)}, u32[]{:S(2)}, u32[]{:S(2)}) collective-permute-start(f32[264,256]{1,0:T(8,128)S(1)} %get-tuple-element.22.mine_ref), channel_id=1, source_target_pairs={{0,1},{1,0},{2,3},{3,2},{4,5},{5,4},{6,7},{7,6},{8,9},{9,8},{10,11... | collective-permute-start | bytes 811016 | tf_op jit(solution)/shard_map/ppermute | solution.py:358
  10.8 11.7 %collective-permute-start.1 = (f32[264,256]{1,0:T(8,128)S(1)}, f32[264,256]{1,0:T(8,128)S(1)}, u32[]{:S(2)}, u32[]{:S(2)}) collective-permute-start(f32[264,256]{1,0:T(8,128)S(1)} %get-tuple-element.23.chip_ref), channel_id=1, source_target_pairs={{0,2},{1,5},{2,0},{3,7},{4,6},{5,1},{6,4},{7,3},{8,10},{9,13},{10,... | collective-permute-start | bytes 811016 | tf_op jit(solution)/shard_map/ppermute | solution.py:365
  13.7 8.8 %collective-permute-start.2 = (f32[264,128]{1,0:T(8,128)S(1)}, f32[264,128]{1,0:T(8,128)S(1)}, u32[]{:S(2)}, u32[]{:S(2)}) collective-permute-start(f32[264,128]{1,0:T(8,128)S(1)} %get-tuple-element.24._), channel_id=1, source_target_pairs={{0,6},{1,7},{2,4},{3,5},{4,2},{5,3},{6,0},{7,1},{8,14},{9,15},{10,... | collective-permute-start | bytes 405512 | tf_op jit(solution)/shard_map/ppermute | solution.py:364
  22.6 1.8 %collective-permute-start.3 = (f32[3,264,128]{2,1,0:T(8,128)S(1)}, f32[3,264,128]{2,1,0:T(8,128)S(1)}, u32[]{:S(2)}, u32[]{:S(2)}) collective-permute-start(f32[3,264,128]{2,1,0:T(8,128)S(1)} %pad_maximum_fusion.mine_ref), channel_id=1, source_target_pairs={{0,1},{1,0},{2,3},{3,2},{4,5},{5,4},{6,7},{7,6},{8,9},{9,8},{10,11... | collective-permute-start | bytes 1216520 | tf_op jit(solution)/shard_map/ppermute | solution.py:385
  25.2 0.7 %collective-permute-start.4 = (f32[8,256]{1,0:T(8,128)S(1)}, f32[8,256]{1,0:T(8,128)S(1)}, u32[]{:S(2)}, u32[]{:S(2)}) collective-permute-start(f32[8,256]{1,0:T(8,128)S(1)} %get-tuple-element.30), channel_id=1, source_target_pairs={{1,9},{3,11},{5,13},{7,15}} | collective-permute-start | bytes 24584 | tf_op jit(solution)/shard_map/ppermute | solution.py:413
  26.2 0.7 %collective-permute-start.5 = (f32[8,256]{1,0:T(8,128)S(1)}, f32[8,256]{1,0:T(8,128)S(1)}, u32[]{:S(2)}, u32[]{:S(2)}) collective-permute-start(f32[8,256]{1,0:T(8,128)S(1)} %get-tuple-element.31), channel_id=1, source_target_pairs={{9,17},{11,19},{13,21},{15,23}} | collective-permute-start | bytes 24584 | tf_op jit(solution)/shard_map/ppermute | solution.py:413
  27.2 3.6 %collective-permute-start.6 = (f32[8,256]{1,0:T(8,128)S(1)}, f32[8,256]{1,0:T(8,128)S(1)}, u32[]{:S(2)}, u32[]{:S(2)}) collective-permute-start(f32[8,256]{1,0:T(8,128)S(1)} %get-tuple-element.33), channel_id=1, source_target_pairs={{17,25},{19,27},{21,29},{23,31}} | collective-permute-start | bytes 24584 | tf_op jit(solution)/shard_map/ppermute | solution.py:413
  27.8 2.9 %collective-permute-start.7 = (f32[8,256]{1,0:T(8,128)S(1)}, f32[8,256]{1,0:T(8,128)S(1)}, u32[]{:S(2)}, u32[]{:S(2)}) collective-permute-start(f32[8,256]{1,0:T(8,128)S(1)} %get-tuple-element.33), channel_id=1, source_target_pairs={{17,24},{19,26},{21,28},{23,30}} | collective-permute-start | bytes 24584 | tf_op jit(solution)/shard_map/ppermute | solution.py:412
  28.5 5.3 %collective-permute-start.8 = (f32[8,256]{1,0:T(8,128)S(1)}, f32[8,256]{1,0:T(8,128)S(1)}, u32[]{:S(2)}, u32[]{:S(2)}) collective-permute-start(f32[8,256]{1,0:T(8,128)S(1)} %get-tuple-element.34.enter_ref), channel_id=1, source_target_pairs={{1,0},{3,2},{5,4},{7,6},{9,8},{11,10},{13,12},{15,14},{17,16},{19,... | collective-permute-start | bytes 24584 | tf_op jit(solution)/shard_map/ppermute | solution.py:416
